TPU v7x, 32 devices: a whole 2x2x4 slice. The times are simulated.
32 devices in a mesh: dp: 8 (over z, y), tensor: 4 (over x, core).
Axes of the slice: x: 2, y: 2, z: 4, core: 2. Of those that a mesh axis runs over, the one named last changes fastest.
Arguments:
- tokens: bfloat16 [16, 1024, 1280], P('dp', 'tensor'), may hold values from -6 to 6
- pic_ids: int32 [16, 1024], P('dp'), may hold values from 0 to 9, as said below
- pos_rows: int32 [16, 1024], P('dp'), may hold values from 0 to 31, as said below
- pos_cols: int32 [16, 1024], P('dp'), may hold values from 0 to 31, as said below
- lengths: int32 [16, 10], P('dp'), may hold values from 0 to 1024, as said below
- ln1_gain: bfloat16 [1280], P(('dp', 'tensor')), may hold values from 0.5 to 1.5
- ln1_bias: bfloat16 [1280], P(('dp', 'tensor')), may hold values from -4 to 4
- qkv_weight: bfloat16 [1280, 3, 1280], P('dp', None, 'tensor'), may hold values from -0.25 to 0.25
- qkv_bias: bfloat16 [3840], P(('dp', 'tensor')), may hold values from -4 to 4
- proj_weight: bfloat16 [1280, 1280], P('tensor', 'dp'), may hold values from -0.3125 to 0.3125
- proj_bias: bfloat16 [1280], P(('dp', 'tensor')), may hold values from -4 to 4
- ln2_gain: bfloat16 [1280], P(('dp', 'tensor')), may hold values from 0.5 to 1.5
- ln2_bias: bfloat16 [1280], P(('dp', 'tensor')), may hold values from -4 to 4
- fc1_weight: bfloat16 [1280, 5120], P('dp', 'tensor'), may hold values from -0.15625 to 0.15625
- fc1_bias: bfloat16 [5120], P(('dp', 'tensor')), may hold values from -6 to 6
- fc2_weight: bfloat16 [5120, 1280], P('tensor', 'dp'), may hold values from -0.078125 to 0.078125
- fc2_bias: bfloat16 [1280], P(('dp', 'tensor')), may hold values from -4 to 4
- cotangent: bfloat16 [16, 1024, 1280], P('dp', 'tensor'), may hold values from -6 to 6
Outputs:
- output: bfloat16 [16, 1024, 1280], P('dp', 'tensor')
- tokens_grad: bfloat16 [16, 1024, 1280], P('dp', 'tensor')
- ln1_gain_grad: float32 [1280], P(('dp', 'tensor'))
- ln1_bias_grad: float32 [1280], P(('dp', 'tensor'))
- qkv_weight_grad: float32 [1280, 3, 1280], P('dp', None, 'tensor')
- qkv_bias_grad: float32 [3840], P(('dp', 'tensor'))
- proj_weight_grad: float32 [1280, 1280], P('tensor', 'dp')
- proj_bias_grad: float32 [1280], P(('dp', 'tensor'))
- ln2_gain_grad: float32 [1280], P(('dp', 'tensor'))
- ln2_bias_grad: float32 [1280], P(('dp', 'tensor'))
- fc1_weight_grad: float32 [1280, 5120], P('dp', 'tensor')
- fc1_bias_grad: float32 [5120], P(('dp', 'tensor'))
- fc2_weight_grad: float32 [5120, 1280], P('tensor', 'dp')
- fc2_bias_grad: float32 [1280], P(('dp', 'tensor'))
Inputs may be any that keep to these rules, and one draw needn't show every extreme that they name: `pic_ids`: in each row the used picture slots come first and their patches stand in slot order from position 0; padding slots follow at the row's end and carry the number of the row's last picture. `pos_rows`: each picture's patches are listed by 2 x 2 blocks of its grid, blocks in row order. `pos_cols`: as for pos_rows. A used slot holds the product of two even sides from 10 to 32; unused slots hold 0 and follow the used ones; a row's lengths sum to more than 824 and at most 1024.
All inputs are finite; a program needn't handle non-finite values.
Results may differ from a plain program's by a relative error of at most 0.019.
Values may be sent and summed in bfloat16 or wider, within the bound.
A program may use at most 256 MiB of HBM per device.

v0:
```python
import math

import jax
import jax.numpy as jnp
from jax import lax
from jax.sharding import PartitionSpec as P

HEAD_DIM = 80


norm_eps = 1e-06
masked_score = -1e30


def layer_norm(values, gain_row, shift_row):
    center = values - jnp.mean(values, axis=-1, keepdims=True)
    spread = jnp.mean(center * center, axis=-1, keepdims=True)
    scaled = lax.rsqrt(spread + norm_eps)
    normed = center * scaled
    return (normed * gain_row + shift_row, normed, scaled)


def norm_back(grad_rows, normed, scaled, gain_row):
    grad_hat = grad_rows * gain_row
    mean_one = jnp.mean(grad_hat, axis=-1, keepdims=True)
    mean_two = jnp.mean(grad_hat * normed, axis=-1, keepdims=True)
    return scaled * (grad_hat - mean_one - normed * mean_two)


def rotate_half(values):
    middle = values.shape[-1] // 2
    return jnp.concatenate([-values[..., middle:], values[..., :middle]], axis=-1)


def rotary_tables(row_places, col_places, head_size):
    quarter = head_size // 4
    freqs_base = 10000.0 ** (-(4.0 * jnp.arange(quarter, dtype=jnp.float32)) / head_size)
    angles = jnp.concatenate(
        [
            row_places.astype(jnp.float32)[:, None] * freqs_base[None, :],
            col_places.astype(jnp.float32)[:, None] * freqs_base[None, :],
        ],
        axis=-1,
    )
    angles = jnp.concatenate([angles, angles], axis=-1)[:, None, :]
    return (jnp.cos(angles), jnp.sin(angles))


def rotary_apply(values, cos_table, sin_table):
    return values * cos_table + rotate_half(values) * sin_table


def rotary_back(grad_rows, cos_table, sin_table):
    return grad_rows * cos_table - rotate_half(grad_rows * sin_table)


def key_window(row_ids, row_lengths):
    slot_ids = jnp.arange(row_lengths.shape[0], dtype=jnp.int32)
    offsets = jnp.cumsum(row_lengths) - row_lengths
    picked = (row_ids[:, None] == slot_ids[None, :]).astype(jnp.int32)
    window_start = jnp.sum(picked * offsets[None, :], axis=1)
    return (window_start, window_start + jnp.sum(picked * row_lengths[None, :], axis=1))


def block_scores(query_block, keys_bf, start_block, stop_block, score_scale):
    scores = (
        jnp.einsum("qhd,khd->hqk", query_block, keys_bf, preferred_element_type=jnp.float32)
        * score_scale
    )
    places = jnp.arange(keys_bf.shape[0], dtype=jnp.int32)
    inside = (places[None, :] >= start_block[:, None]) & (places[None, :] < stop_block[:, None])
    return jnp.where(inside[None], scores, masked_score)


def gather_weights(qkv_weight, proj_weight, fc1_weight, fc2_weight):
    return (
        lax.all_gather(qkv_weight, "dp", axis=0, tiled=True),
        lax.all_gather(proj_weight, "dp", axis=1, tiled=True),
        lax.all_gather(fc1_weight, "dp", axis=0, tiled=True),
        lax.all_gather(fc2_weight, "dp", axis=1, tiled=True),
    )


def reduce_grads(grad_qkv, grad_proj, grad_fc1, grad_fc2):
    return (
        lax.psum_scatter(
            grad_qkv.astype(jnp.bfloat16), "dp", scatter_dimension=0, tiled=True
        ).astype(jnp.float32),
        lax.psum_scatter(
            grad_proj.astype(jnp.bfloat16), "dp", scatter_dimension=1, tiled=True
        ).astype(jnp.float32),
        lax.psum_scatter(
            grad_fc1.astype(jnp.bfloat16), "dp", scatter_dimension=0, tiled=True
        ).astype(jnp.float32),
        lax.psum_scatter(
            grad_fc2.astype(jnp.bfloat16), "dp", scatter_dimension=1, tiled=True
        ).astype(jnp.float32),
    )


def on_device(
    tokens,
    pic_ids,
    pos_rows,
    pos_cols,
    lengths,
    ln1_gain,
    ln1_bias,
    qkv_weight,
    qkv_bias,
    proj_weight,
    proj_bias,
    ln2_gain,
    ln2_bias,
    fc1_weight,
    fc1_bias,
    fc2_weight,
    fc2_bias,
    cotangent,
):
    micro_count = tokens.shape[0]
    local_rows = tokens.shape[1]
    model_width = tokens.shape[2]
    row_length = pic_ids.shape[1]
    head_width = qkv_weight.shape[2]
    hidden_width = fc1_weight.shape[1]
    head_count = head_width // HEAD_DIM
    score_scale = 1.0 / math.sqrt(HEAD_DIM)
    block_rows = min(512, row_length)
    block_total = row_length // block_rows
    tensor_place = lax.axis_index("tensor")
    first_row = tensor_place * local_rows
    local_places = first_row + jnp.arange(local_rows, dtype=jnp.int32)
    f32 = jnp.float32
    bf16 = jnp.bfloat16
    vectors = (
        lax.all_gather(ln1_gain, ("dp", "tensor"), axis=0, tiled=True),
        lax.all_gather(ln1_bias, ("dp", "tensor"), axis=0, tiled=True),
        lax.all_gather(qkv_bias, ("dp", "tensor"), axis=0, tiled=True),
        lax.all_gather(proj_bias, ("dp", "tensor"), axis=0, tiled=True),
        lax.all_gather(ln2_gain, ("dp", "tensor"), axis=0, tiled=True),
        lax.all_gather(ln2_bias, ("dp", "tensor"), axis=0, tiled=True),
        lax.all_gather(fc1_bias, ("dp", "tensor"), axis=0, tiled=True),
        lax.all_gather(fc2_bias, ("dp", "tensor"), axis=0, tiled=True),
    )
    gain_one, shift_one, qkv_shift, proj_shift, gain_two, shift_two, fc1_shift, fc2_shift = [
        vector_part.astype(f32) for vector_part in vectors
    ]
    qkv_local_shift = lax.dynamic_slice_in_dim(
        qkv_shift.reshape(3, model_width), tensor_place * head_width, head_width, 1
    ).reshape(3 * head_width)
    fc1_local_shift = lax.dynamic_slice_in_dim(
        fc1_shift, tensor_place * hidden_width, hidden_width, 0
    )
    grad_gain_one = jnp.zeros((model_width,), f32)
    grad_shift_one = jnp.zeros((model_width,), f32)
    grad_proj_shift = jnp.zeros((model_width,), f32)
    grad_gain_two = jnp.zeros((model_width,), f32)
    grad_shift_two = jnp.zeros((model_width,), f32)
    grad_fc2_shift = jnp.zeros((model_width,), f32)
    grad_qkv_shift = jnp.zeros((3 * head_width,), f32)
    grad_fc1_shift = jnp.zeros((hidden_width,), f32)
    shard_grads = [
        jnp.zeros(qkv_weight.shape, f32),
        jnp.zeros(proj_weight.shape, f32),
        jnp.zeros(fc1_weight.shape, f32),
        jnp.zeros(fc2_weight.shape, f32),
    ]
    outputs = []
    token_grads = []
    for micro_index in range(micro_count):
        w_qkv, w_proj, w_fc1, w_fc2 = gather_weights(
            qkv_weight, proj_weight, fc1_weight, fc2_weight
        )
        tokens_row = tokens[micro_index].astype(f32)
        start_all, stop_all = key_window(pic_ids[micro_index], lengths[micro_index])
        cos_table, sin_table = rotary_tables(pos_rows[micro_index], pos_cols[micro_index], HEAD_DIM)
        pad_rows = (local_places < jnp.sum(lengths[micro_index])).astype(f32)[:, None]
        normed_one, hat_one, scale_one = layer_norm(tokens_row, gain_one, shift_one)
        lowered_one = lax.all_gather(normed_one.astype(bf16), "tensor", axis=0, tiled=True)
        w_qkv_flat = w_qkv.reshape(model_width, 3 * head_width)
        linear = jnp.dot(lowered_one, w_qkv_flat, preferred_element_type=f32) + qkv_local_shift
        linear = linear.reshape(row_length, 3, head_count, HEAD_DIM)
        queries_bf = rotary_apply(linear[:, 0], cos_table, sin_table).astype(bf16)
        keys_bf = rotary_apply(linear[:, 1], cos_table, sin_table).astype(bf16)
        values_bf = linear[:, 2].astype(bf16)
        context_blocks = []
        logsum_blocks = []
        for block_index in range(block_total):
            row_lower = block_index * block_rows
            row_upper = row_lower + block_rows
            scores = block_scores(
                queries_bf[row_lower:row_upper],
                keys_bf,
                start_all[row_lower:row_upper],
                stop_all[row_lower:row_upper],
                score_scale,
            )
            highest = jnp.max(scores, axis=-1, keepdims=True)
            shifted = jnp.exp(scores - highest)
            totals = jnp.sum(shifted, axis=-1, keepdims=True)
            attend = shifted / totals
            logsum_blocks.append(highest + jnp.log(totals))
            context_blocks.append(
                jnp.einsum(
                    "hqk,khd->qhd", attend.astype(bf16), values_bf, preferred_element_type=f32
                )
            )
        context_bf = (
            jnp.concatenate(context_blocks, axis=0).reshape(row_length, head_width).astype(bf16)
        )
        attn_branch = lax.psum_scatter(
            jnp.dot(context_bf, w_proj, preferred_element_type=f32).astype(jnp.bfloat16),
            "tensor",
            scatter_dimension=0,
            tiled=True,
        ).astype(jnp.float32)
        hidden_row = tokens_row + attn_branch + proj_shift
        normed_two, hat_two, scale_two = layer_norm(hidden_row, gain_two, shift_two)
        lowered_two = lax.all_gather(normed_two.astype(bf16), "tensor", axis=0, tiled=True)
        upward = jnp.dot(lowered_two, w_fc1, preferred_element_type=f32) + fc1_local_shift
        sigmoid_up = jax.nn.sigmoid(1.702 * upward)
        activated = (upward * sigmoid_up).astype(bf16)
        branch = (
            lax.psum_scatter(
                jnp.dot(activated, w_fc2, preferred_element_type=f32).astype(jnp.bfloat16),
                "tensor",
                scatter_dimension=0,
                tiled=True,
            ).astype(jnp.float32)
            + fc2_shift
        )
        outputs.append((pad_rows * (hidden_row + branch)).astype(bf16))
        w_qkv, w_proj, w_fc1, w_fc2 = gather_weights(
            qkv_weight, proj_weight, fc1_weight, fc2_weight
        )
        w_qkv_flat = w_qkv.reshape(model_width, 3 * head_width)
        grad_out = pad_rows * cotangent[micro_index].astype(f32)
        grad_fc2_shift = grad_fc2_shift + jnp.sum(grad_out, axis=0)
        grad_branch = lax.all_gather(grad_out.astype(bf16), "tensor", axis=0, tiled=True)
        micro_fc2 = jnp.einsum("sf,sd->fd", activated, grad_branch, preferred_element_type=f32)
        grad_act = jnp.einsum("sd,fd->sf", grad_branch, w_fc2, preferred_element_type=f32)
        grad_up = (
            grad_act * (sigmoid_up + 1.702 * upward * sigmoid_up * (1.0 - sigmoid_up))
        ).astype(bf16)
        grad_fc1_shift = grad_fc1_shift + jnp.sum(grad_up.astype(f32), axis=0)
        micro_fc1 = jnp.einsum("sd,sf->df", lowered_two, grad_up, preferred_element_type=f32)
        grad_normed_two = lax.psum_scatter(
            jnp.einsum("sf,df->sd", grad_up, w_fc1, preferred_element_type=f32).astype(
                jnp.bfloat16
            ),
            "tensor",
            scatter_dimension=0,
            tiled=True,
        ).astype(jnp.float32)
        grad_gain_two = grad_gain_two + jnp.sum(grad_normed_two * hat_two, axis=0)
        grad_shift_two = grad_shift_two + jnp.sum(grad_normed_two, axis=0)
        grad_hidden = grad_out + norm_back(grad_normed_two, hat_two, scale_two, gain_two)
        grad_proj_shift = grad_proj_shift + jnp.sum(grad_hidden, axis=0)
        grad_attn = lax.all_gather(grad_hidden.astype(bf16), "tensor", axis=0, tiled=True)
        micro_proj = jnp.einsum("sc,sd->cd", context_bf, grad_attn, preferred_element_type=f32)
        grad_context = (
            jnp.einsum("sd,cd->sc", grad_attn, w_proj, preferred_element_type=f32)
            .astype(bf16)
            .reshape(row_length, head_count, HEAD_DIM)
        )
        grad_keys = jnp.zeros((row_length, head_count, HEAD_DIM), f32)
        grad_values = jnp.zeros((row_length, head_count, HEAD_DIM), f32)
        query_grad_blocks = []
        for block_index in range(block_total):
            row_lower = block_index * block_rows
            row_upper = row_lower + block_rows
            scores = block_scores(
                queries_bf[row_lower:row_upper],
                keys_bf,
                start_all[row_lower:row_upper],
                stop_all[row_lower:row_upper],
                score_scale,
            )
            attend = jnp.exp(scores - logsum_blocks[block_index])
            context_grad = grad_context[row_lower:row_upper]
            grad_values = grad_values + jnp.einsum(
                "hqk,qhd->khd", attend.astype(bf16), context_grad, preferred_element_type=f32
            )
            attend_grad = jnp.einsum(
                "qhd,khd->hqk", context_grad, values_bf, preferred_element_type=f32
            )
            row_inner = jnp.sum(attend * attend_grad, axis=-1, keepdims=True)
            score_grad = (attend * (attend_grad - row_inner) * score_scale).astype(bf16)
            query_grad_blocks.append(
                jnp.einsum("hqk,khd->qhd", score_grad, keys_bf, preferred_element_type=f32)
            )
            grad_keys = grad_keys + jnp.einsum(
                "hqk,qhd->khd",
                score_grad,
                queries_bf[row_lower:row_upper],
                preferred_element_type=f32,
            )
        grad_queries = jnp.concatenate(query_grad_blocks, axis=0)
        grad_linear = jnp.stack(
            [
                rotary_back(grad_queries, cos_table, sin_table),
                rotary_back(grad_keys, cos_table, sin_table),
                grad_values,
            ],
            axis=1,
        )
        grad_linear = grad_linear.reshape(row_length, 3 * head_width).astype(bf16)
        grad_qkv_shift = grad_qkv_shift + jnp.sum(grad_linear.astype(f32), axis=0)
        micro_qkv = jnp.einsum(
            "sd,se->de", lowered_one, grad_linear, preferred_element_type=f32
        ).reshape(model_width, 3, head_width)
        grad_normed_one = lax.psum_scatter(
            jnp.einsum("se,de->sd", grad_linear, w_qkv_flat, preferred_element_type=f32).astype(
                jnp.bfloat16
            ),
            "tensor",
            scatter_dimension=0,
            tiled=True,
        ).astype(jnp.float32)
        grad_gain_one = grad_gain_one + jnp.sum(grad_normed_one * hat_one, axis=0)
        grad_shift_one = grad_shift_one + jnp.sum(grad_normed_one, axis=0)
        token_grads.append(
            (grad_hidden + norm_back(grad_normed_one, hat_one, scale_one, gain_one)).astype(bf16)
        )
        reduced = reduce_grads(micro_qkv, micro_proj, micro_fc1, micro_fc2)
        shard_grads = [former + latter for former, latter in zip(shard_grads, reduced)]
    qkv_full_grad = lax.dynamic_update_slice_in_dim(
        jnp.zeros((3, model_width), f32),
        grad_qkv_shift.reshape(3, head_width),
        tensor_place * head_width,
        1,
    ).reshape(3 * model_width)
    fc1_full_grad = lax.dynamic_update_slice_in_dim(
        jnp.zeros((hidden_width * (fc1_shift.shape[0] // hidden_width),), f32),
        grad_fc1_shift,
        tensor_place * hidden_width,
        0,
    )
    small_out = (
        lax.psum_scatter(grad_gain_one, ("dp", "tensor"), scatter_dimension=0, tiled=True),
        lax.psum_scatter(grad_shift_one, ("dp", "tensor"), scatter_dimension=0, tiled=True),
        lax.psum_scatter(qkv_full_grad, ("dp", "tensor"), scatter_dimension=0, tiled=True),
        lax.psum_scatter(grad_proj_shift, ("dp", "tensor"), scatter_dimension=0, tiled=True),
        lax.psum_scatter(grad_gain_two, ("dp", "tensor"), scatter_dimension=0, tiled=True),
        lax.psum_scatter(grad_shift_two, ("dp", "tensor"), scatter_dimension=0, tiled=True),
        lax.psum_scatter(fc1_full_grad, ("dp", "tensor"), scatter_dimension=0, tiled=True),
        lax.psum_scatter(grad_fc2_shift, ("dp", "tensor"), scatter_dimension=0, tiled=True),
    )
    return (
        jnp.stack(outputs, axis=0),
        jnp.stack(token_grads, axis=0),
        small_out[0],
        small_out[1],
        shard_grads[0],
        small_out[2],
        shard_grads[1],
        small_out[3],
        small_out[4],
        small_out[5],
        shard_grads[2],
        small_out[6],
        shard_grads[3],
        small_out[7],
    )


def solution(mesh):
    placed = (
        P("dp", "tensor", None),
        P("dp", None),
        P("dp", None),
        P("dp", None),
        P("dp", None),
        P(("dp", "tensor")),
        P(("dp", "tensor")),
        P("dp", None, "tensor"),
        P(("dp", "tensor")),
        P("tensor", "dp"),
        P(("dp", "tensor")),
        P(("dp", "tensor")),
        P(("dp", "tensor")),
        P("dp", "tensor"),
        P(("dp", "tensor")),
        P("tensor", "dp"),
        P(("dp", "tensor")),
        P("dp", "tensor", None),
    )
    return jax.shard_map(
        on_device,
        mesh=mesh,
        in_specs=placed,
        out_specs=(
            P("dp", "tensor", None),
            P("dp", "tensor", None),
            P(("dp", "tensor")),
            P(("dp", "tensor")),
            P("dp", None, "tensor"),
            P(("dp", "tensor")),
            P("tensor", "dp"),
            P(("dp", "tensor")),
            P(("dp", "tensor")),
            P(("dp", "tensor")),
            P("dp", "tensor"),
            P(("dp", "tensor")),
            P("tensor", "dp"),
            P(("dp", "tensor")),
        ),
        check_vma=False,
    )
```

profile of v0, /device:TPU:0, one launch (start us, length us, event | category | flops | bytes accessed | tf_op | source)
XLA Modules:
  0.0 1485.8 jit_solution(5448876101250859231)
XLA Ops:
  14.8 45.2 %all-reduce.17 = (bf16[1280]{0:T(1024)(128)(2,1)S(1)}, bf16[3840]{0:T(1024)(128)(2,1)S(1)}, bf16[1280]{0:T(1024)(128)(2,1)S(1)}, bf16[1280]{0:T(1024)(128)(2,1)S...) all-reduce(bf16[1280]{0:T(1024)(128)(2,1)S(1)} %dynamic-update-slic, ...), channel_id=1, replica_groups=mesh['dp'=8,'tensor'=4] {'dp','tensor'}, use_global_device_ids=true, to_apply=%add.3 | all-reduce | flops 16640 | bytes 66560
  74.5 35.1 %all_gather.77 = bf16[320,1280]{0,1:T(8,128)(2,1)} all-gather(bf16[320,160]{0,1:T(8,128)(2,1)} %param.27), channel_id=1, replica_groups=mesh['dp'=8,'tensor'=4] {'dp'}, dimensions={1}, use_global_device_ids=true | all-gather | bytes 921600 | tf_op jit(solution)/shard_map/all_gather | solution.py:78
  109.6 5.3 copy.40
  114.9 5.2 broadcast_add_fusion.1
  125.8 5.2 broadcast_add_fusion
  135.4 2.9 fusion.11
  151.0 3.0 convolution_convert_fusion.11
  154.1 3.2 fusion.217
  174.4 3.1 convolution_convert_fusion.13
  178.2 10.5 reduce-scatter.21.cloned.1.call-done
  188.7 36.9 %reduce-scatter.17.cloned.1.call-done = bf16[256,1280]{1,0:T(8,128)(2,1)} async-done(((bf16[1024,1280]{1,0:T(8,128)(2,1)}), bf16[256,1280]{1,0:T(8,128)(2,1)}) %reduce-scatter.17.cloned.1.call-update) | async-done | bytes 655376 | tf_op jit(solution)/shard_map/reduce_scatter | solution.py:212
  237.2 52.0 %all-gather.18.cloned.1.call-done = bf16[1280,1280]{1,0:T(8,128)(2,1)} async-done(((bf16[160,1280]{1,0:T(8,128)(2,1)}), bf16[1280,1280]{1,0:T(8,128)(2,1)}) %all-gather.18.cloned.1.call-update) | async-done | bytes 3276816 | tf_op jit(solution)/shard_map/all_gather | solution.py:79
  289.2 26.4 %all-gather.24.cloned.1.call-done = bf16[1024,1280]{1,0:T(8,128)(2,1)} async-done(((bf16[256,1280]{1,0:T(8,128)(2,1)}), bf16[1024,1280]{1,0:T(8,128)(2,1)}) %all-gather.24.cloned.1.call-update) | async-done | bytes 2621456 | tf_op jit(solution)/shard_map/all_gather | solution.py:220
  315.5 8.6 fusion.351
  324.2 19.1 %all-gather.30.cloned.1.call-done = bf16[1024,1280]{1,0:T(8,128)(2,1)} async-done(((bf16[256,1280]{1,0:T(8,128)(2,1)}), bf16[1024,1280]{1,0:T(8,128)(2,1)}) %all-gather.30.cloned.1.call-update) | async-done | bytes 2621456 | tf_op jit(solution)/shard_map/all_gather | solution.py:240
  343.2 63.7 %all-gather.20.cloned.1.call-done = bf16[1280,1280]{0,1:T(8,128)(2,1)} async-done(((bf16[1280,160]{0,1:T(8,128)(2,1)}), bf16[1280,1280]{0,1:T(8,128)(2,1)}) %all-gather.20.cloned.1.call-update) | async-done | bytes 3276816 | tf_op jit(solution)/shard_map/all_gather | solution.py:80
  406.9 9.6 convert_reduce_fusion
  418.0 4.9 convolution_convert_fusion.7
  423.4 9.8 all-gather.16.cloned.1.call-done
  433.2 8.6 fusion.350
  441.7 19.1 %all-gather.26.cloned.1.call-done = bf16[1024,1280]{1,0:T(8,128)(2,1)} async-done(((bf16[256,1280]{1,0:T(8,128)(2,1)}), bf16[1024,1280]{1,0:T(8,128)(2,1)}) %all-gather.26.cloned.1.call-update) | async-done | bytes 2621456 | tf_op jit(solution)/shard_map/all_gather | solution.py:240
  460.9 9.6 convert_reduce_fusion.1
  472.2 4.9 convolution_convert_fusion.9
  477.1 9.4 convolution_convert_fusion.10
  486.7 9.3 convolution_convert_fusion.12
  497.8 37.1 %reduce-scatter.25.cloned.1.call-done = bf16[256,1280]{1,0:T(8,128)(2,1)} async-done(((bf16[1024,1280]{1,0:T(8,128)(2,1)}), bf16[256,1280]{1,0:T(8,128)(2,1)}) %reduce-scatter.25.cloned.1.call-update) | async-done | bytes 655376 | tf_op jit(solution)/shard_map/reduce_scatter | solution.py:248
  534.8 3.3 fusion.212
  538.2 33.6 %reduce-scatter.23.cloned.1.call-done = bf16[256,1280]{1,0:T(8,128)(2,1)} async-done(((bf16[1024,1280]{1,0:T(8,128)(2,1)}), bf16[256,1280]{1,0:T(8,128)(2,1)}) %reduce-scatter.23.cloned.1.call-update) | async-done | bytes 655376 | tf_op jit(solution)/shard_map/reduce_scatter | solution.py:225
  571.8 3.8 fusion.322
  577.6 31.0 %reduce-scatter.19.cloned.1.call-done = bf16[256,1280]{1,0:T(8,128)(2,1)} async-done(((bf16[1024,1280]{1,0:T(8,128)(2,1)}), bf16[256,1280]{1,0:T(8,128)(2,1)}) %reduce-scatter.19.cloned.1.call-update) | async-done | bytes 655376 | tf_op jit(solution)/shard_map/reduce_scatter | solution.py:225
  608.7 4.1 fusion.228
  614.8 9.2 convolution_convert_fusion
  624.3 8.8 convolution_convert_fusion.1
  633.1 7.9 convolution_convert_fusion.2
  641.1 7.9 convolution_convert_fusion.3
  653.2 6.0 fusion.340
  659.2 18.0 %fusion.43 = f32[4,80,512]{2,1,0:T(8,128)} fusion(bf16[1024,4,80]{0,2,1:T(8,128)(2,1)S(1)} %copy-done.17, f32[4,512,1024]{2,1,0:T(8,128)} %fusion.340, f32[4,512,1024]{2,1,0:T(8,128)} %copy-done.5, f32[4,512]{1,0:T(4,128)S(1)} %log_add_fusion.1, pred[512,1024]{1,0:T(8,128)(4,1)S(1)} %copy-done.27), kind=kOutput, calls=%fused_computation.60 | convolution fusion | flops 358616064 | bytes 18620416 | tf_op jit(solution)/shard_map/hqk,khd->qhd/dot_general | solution.py:291
  677.2 23.5 %fusion.40 = f32[4,80,1024]{2,1,0:T(8,128)} fusion(f32[4,512,1024]{2,1,0:T(8,128)} %fusion.340, f32[4,512,1024]{2,1,0:T(8,128)} %copy-done.5, f32[4,512]{1,0:T(4,128)S(1)} %log_add_fusion.1, pred[512,1024]{1,0:T(8,128)(4,1)S(1)} %copy-done.27, bf16[1024,4,80]{0,2,1:T(8,128)(2,1)S(1)} %copy-done.33), kind=kOutput, calls=%fused_computation.59 | convolution fusion | flops 358616064 | bytes 36257792 | tf_op jit(solution)/shard_map/hqk,qhd->khd/dot_general | solution.py:293
  700.7 4.5 convolution_convert_fusion.14
  705.2 5.9 fusion.338
  711.4 18.0 %fusion.50 = f32[4,80,512]{2,1,0:T(8,128)} fusion(bf16[1024,4,80]{0,2,1:T(8,128)(2,1)S(1)} %copy-done.17, f32[4,512,1024]{2,1,0:T(8,128)} %fusion.338, f32[4,512,1024]{2,1,0:T(8,128)} %copy-done.4, f32[4,512]{1,0:T(4,128)S(1)} %log_add_fusion, pred[512,1024]{1,0:T(8,128)(4,1)S(1)} %copy-done.29), kind=kOutput, calls=%fused_computation.63 | convolution fusion | flops 358616064 | bytes 18620416 | tf_op jit(solution)/shard_map/hqk,khd->qhd/dot_general | solution.py:291
  729.4 24.1 %maximum_multiply_fusion.7 = (f32[1024,4,80]{0,2,1:T(8,128)}, f32[1024,4,80]{0,2,1:T(8,128)}, f32[1024,4,80]{0,2,1:T(8,128)}) fusion(f32[512,4,80]{0,2,1:T(8,128)} %bitcast.331, f32[512,4,80]{0,2,1:T(8,128)} %bitcast.329, f32[1024,80]{0,1:T(8,128)S(1)} %copy-done.44, f32[4,80,1024]{2,1,0:T(8,128)} %fusion.40, f32[4,512,1024]{2,1,0:T(8,128)} %fusion.338, ...), kind=kOutput, calls=%fused_computation.246 | convolution fusion | flops 359926784 | bytes 41828352 | tf_op jit(solution)/shard_map/hqk,qhd->khd/dot_general | solution.py:293
  753.5 4.3 convolution_convert_fusion.15
  761.7 4.9 fusion.100
  766.6 6.0 fusion.171
  779.6 6.6 fusion.346
  786.2 5.0 convolution_convert_fusion.4
  792.4 17.9 %fusion.29 = f32[4,80,512]{2,1,0:T(8,128)} fusion(bf16[1024,4,80]{0,2,1:T(8,128)(2,1)S(1)} %copy-done.15, f32[4,512,1024]{2,1,0:T(8,128)} %fusion.346, f32[4,512,1024]{2,1,0:T(8,128)} %copy-done.2, f32[4,512]{1,0:T(4,128)S(1)} %log_add_fusion.3, pred[512,1024]{1,0:T(8,128)(4,1)S(1)} %copy-done.23), kind=kOutput, calls=%fused_computation.54 | convolution fusion | flops 358616064 | bytes 18620416 | tf_op jit(solution)/shard_map/hqk,khd->qhd/dot_general | solution.py:291
  810.3 5.9 fusion.344
  816.2 18.0 %fusion.36 = f32[4,80,512]{2,1,0:T(8,128)} fusion(bf16[1024,4,80]{0,2,1:T(8,128)(2,1)S(1)} %copy-done.15, f32[4,512,1024]{2,1,0:T(8,128)} %fusion.344, f32[4,512,1024]{2,1,0:T(8,128)} %copy-done.3, f32[4,512]{1,0:T(4,128)S(1)} %log_add_fusion.2, pred[512,1024]{1,0:T(8,128)(4,1)S(1)} %copy-done.25), kind=kOutput, calls=%fused_computation.57 | convolution fusion | flops 358616064 | bytes 18620416 | tf_op jit(solution)/shard_map/hqk,khd->qhd/dot_general | solution.py:291
  834.2 23.3 %fusion.26 = f32[4,80,1024]{2,1,0:T(8,128)} fusion(f32[4,512,1024]{2,1,0:T(8,128)} %fusion.346, f32[4,512,1024]{2,1,0:T(8,128)} %copy-done.2, f32[4,512]{1,0:T(4,128)S(1)} %log_add_fusion.3, pred[512,1024]{1,0:T(8,128)(4,1)S(1)} %copy-done.23, bf16[1024,4,80]{0,2,1:T(8,128)(2,1)S(1)} %copy-done.31), kind=kOutput, calls=%fused_computation.53 | convolution fusion | flops 358616064 | bytes 36257792 | tf_op jit(solution)/shard_map/hqk,qhd->khd/dot_general | solution.py:293
  857.6 24.0 %maximum_multiply_fusion.5 = (f32[1024,4,80]{0,2,1:T(8,128)}, f32[1024,4,80]{0,2,1:T(8,128)}, f32[1024,4,80]{0,2,1:T(8,128)}) fusion(f32[512,4,80]{0,2,1:T(8,128)} %bitcast.335, f32[512,4,80]{0,2,1:T(8,128)} %bitcast.333, f32[1024,80]{0,1:T(8,128)S(1)} %copy-done.42, f32[4,80,1024]{2,1,0:T(8,128)} %fusion.26, f32[4,512,1024]{2,1,0:T(8,128)} %fusion.344, ...), kind=kOutput, calls=%fused_computation.241 | convolution fusion | flops 359926784 | bytes 41828352 | tf_op jit(solution)/shard_map/hqk,qhd->khd/dot_general | solution.py:293
  885.1 5.0 fusion.104
  895.2 5.0 convolution_convert_fusion.5
  901.7 5.9 convolution_convert_fusion.6
  908.0 6.8 convolution_convert_fusion.8
  920.9 58.5 %reduce-scatter.41.cloned.1.call-done = bf16[160,1280]{1,0:T(8,128)(2,1)} async-done(((bf16[1280,1280]{1,0:T(8,128)(2,1)}), bf16[160,1280]{1,0:T(8,128)(2,1)}) %reduce-scatter.41.cloned.1.call-update) | async-done | bytes 409616 | tf_op jit(solution)/shard_map/reduce_scatter | solution.py:92
  982.6 63.3 %reduce-scatter.39.cloned.1.call-done = bf16[320,160]{0,1:T(8,128)(2,1)} async-done(((bf16[320,1280]{0,1:T(8,128)(2,1)}), bf16[320,160]{0,1:T(8,128)(2,1)}) %reduce-scatter.39.cloned.1.call-update) | async-done | bytes 102416 | tf_op jit(solution)/shard_map/reduce_scatter | solution.py:89
  1045.9 66.4 %reduce-scatter.37.cloned.1.call-done = bf16[320,160]{0,1:T(8,128)(2,1)} async-done(((bf16[320,1280]{0,1:T(8,128)(2,1)}), bf16[320,160]{0,1:T(8,128)(2,1)}) %reduce-scatter.37.cloned.1.call-update) | async-done | bytes 102416 | tf_op jit(solution)/shard_map/reduce_scatter | solution.py:89
  1114.0 73.9 %reduce-scatter.35.cloned.1.call-done = bf16[160,3,320]{2,0,1:T(8,128)(2,1)} async-done(((bf16[1280,3,320]{2,0,1:T(8,128)(2,1)}), bf16[160,3,320]{2,0,1:T(8,128)(2,1)}) %reduce-scatter.35.cloned.1.call-update) | async-done | bytes 307216 | tf_op jit(solution)/shard_map/reduce_scatter | solution.py:86
  1187.9 75.8 %reduce-scatter.33.cloned.1.call-done = bf16[160,3,320]{2,0,1:T(8,128)(2,1)} async-done(((bf16[1280,3,320]{2,0,1:T(8,128)(2,1)}), bf16[160,3,320]{2,0,1:T(8,128)(2,1)}) %reduce-scatter.33.cloned.1.call-update) | async-done | bytes 307216 | tf_op jit(solution)/shard_map/reduce_scatter | solution.py:86
  1265.7 33.9 %reduce-scatter.31.cloned.1.call-done = bf16[256,1280]{1,0:T(8,128)(2,1)} async-done(((bf16[1024,1280]{1,0:T(8,128)(2,1)}), bf16[256,1280]{1,0:T(8,128)(2,1)}) %reduce-scatter.31.cloned.1.call-update) | async-done | bytes 655376 | tf_op jit(solution)/shard_map/reduce_scatter | solution.py:313
  1299.6 36.9 %reduce-scatter.27.cloned.1.call-done = bf16[256,1280]{1,0:T(8,128)(2,1)} async-done(((bf16[1024,1280]{1,0:T(8,128)(2,1)}), bf16[256,1280]{1,0:T(8,128)(2,1)}) %reduce-scatter.27.cloned.1.call-update) | async-done | bytes 655376 | tf_op jit(solution)/shard_map/reduce_scatter | solution.py:313
  1343.9 124.5 %all-reduce.20.cloned.1.call-done = (f32[1280]{0:T(1024)}, f32[1280]{0:T(1024)}, f32[3840]{0:T(1024)}, f32[1280]{0:T(1024)}, f32[1280]{0:T(1024)}, /*index=5*/f32[1280]{0:T(1024)}, f32[5120]{0:T(1024)}, f32[1280]{0:T(1024)}) async-done(((f32[1280]{0:T(1024)}, f32[1280]{0:T(1024)}, f32[3840]{0:T(1024)}, f32[1280]{0:T(1024)}, f32[1280]{0:T(1024)}, /*index=5*/f32[1280]{0:T(1024)}, f32[5120]{0:T(1024)}, ...) | async-done | bytes 66576
  (422 shorter events, 140.6 us)
Async XLA Ops:
  7.2 56.3 %copy-start = (bf16[2,256,1280]{2,1,0:T(8,128)(2,1)S(1)}, bf16[2,256,1280]{2,1,0:T(8,128)(2,1)}, u32[]{:S(2)}) copy-start(bf16[2,256,1280]{2,1,0:T(8,128)(2,1)} %param.18) | copy-start | bytes 3932164
  7.2 102.4 %all-gather.14.cloned.1.call-start = ((), (), s32[]{:S(2)}) async-start(), calls=%async_computation.17 | async-start | bytes 3317760 | tf_op jit(solution)/shard_map/all_gather | solution.py:77
  7.9 107.0 %all-gather.12.cloned.1.call-start = ((), (), s32[]{:S(2)}) async-start(), calls=%async_computation.16 | async-start | bytes 3276800 | tf_op jit(solution)/shard_map/all_gather | solution.py:180
  65.2 60.6 %all-gather.22.cloned.1.call-start = ((), (), s32[]{:S(2)}) async-start(), calls=%async_computation.23 | async-start | bytes 3276800 | tf_op jit(solution)/shard_map/all_gather | solution.py:180
  65.9 122.8 %reduce-scatter.21.cloned.1.call-start = ((), (), s32[]{:S(2)}) async-start(), calls=%async_computation.24 | async-start | bytes 3276800 | tf_op jit(solution)/shard_map/reduce_scatter | solution.py:212
  69.1 62.3 %copy-start.20 = (f32[1024,80]{0,1:T(8,128)}, f32[1024,80]{0,1:T(8,128)S(1)}, u32[]{:S(2)}) copy-start(f32[1024,80]{0,1:T(8,128)S(1)} %get-tuple-element.119) | copy-start | bytes 983044
  71.3 82.9 %copy-start.18 = (f32[1024,80]{0,1:T(8,128)}, f32[1024,80]{0,1:T(8,128)S(1)}, u32[]{:S(2)}) copy-start(f32[1024,80]{0,1:T(8,128)S(1)} %get-tuple-element.121) | copy-start | bytes 983044
  71.9 98.7 %copy-start.22 = (pred[512,1024]{1,0:T(8,128)(4,1)}, pred[512,1024]{1,0:T(8,128)(4,1)S(1)}, u32[]{:S(2)}) copy-start(pred[512,1024]{1,0:T(8,128)(4,1)S(1)} %fusion.134) | copy-start | bytes 1572868
  72.5 73.3 %copy-start.26 = (pred[512,1024]{1,0:T(8,128)(4,1)}, pred[512,1024]{1,0:T(8,128)(4,1)S(1)}, u32[]{:S(2)}) copy-start(pred[512,1024]{1,0:T(8,128)(4,1)S(1)} %fusion.136) | copy-start | bytes 1572868
  73.1 93.2 %copy-start.24 = (pred[512,1024]{1,0:T(8,128)(4,1)}, pred[512,1024]{1,0:T(8,128)(4,1)S(1)}, u32[]{:S(2)}) copy-start(pred[512,1024]{1,0:T(8,128)(4,1)S(1)} %fusion.135) | copy-start | bytes 1572868
  131.0 14.9 %copy-start.10 = (f32[1024,960]{0,1:T(8,128)}, f32[1024,960]{0,1:T(8,128)S(1)}, u32[]{:S(2)}) copy-start(f32[1024,960]{0,1:T(8,128)S(1)} %broadcast_add_fusion) | copy-start | bytes 11796484
  133.2 8.3 copy-start.16
  133.2 8.3 copy-start.32
  154.1 71.6 %reduce-scatter.17.cloned.1.call-start = ((), (), s32[]{:S(2)}) async-start(), calls=%async_computation.18 | async-start | bytes 3276800 | tf_op jit(solution)/shard_map/reduce_scatter | solution.py:212
  161.1 9.5 copy-start.2
  177.5 111.6 %all-gather.18.cloned.1.call-start = ((), (), s32[]{:S(2)}) async-start(), calls=%async_computation.20 | async-start | bytes 3686400 | tf_op jit(solution)/shard_map/all_gather | solution.py:79
  178.1 137.4 %all-gather.24.cloned.1.call-start = ((), (), s32[]{:S(2)}) async-start(), calls=%async_computation.25 | async-start | bytes 3276800 | tf_op jit(solution)/shard_map/all_gather | solution.py:220
  188.7 38.8 %copy-start.6 = (bf16[256,1280]{1,0:T(8,128)(2,1)S(1)}, bf16[256,1280]{1,0:T(8,128)(2,1)}, u32[]{:S(2)}) copy-start(bf16[256,1280]{1,0:T(8,128)(2,1)} %reduce-scatter.21.cloned.1.call-done) | copy-start | bytes 1966084
  230.0 113.2 %all-gather.30.cloned.1.call-start = ((), (), s32[]{:S(2)}) async-start(), calls=%async_computation.31 | async-start | bytes 3276800 | tf_op jit(solution)/shard_map/all_gather | solution.py:240
  234.1 172.9 %all-gather.20.cloned.1.call-start = ((), (), s32[]{:S(2)}) async-start(), calls=%async_computation.21 | async-start | bytes 3686400 | tf_op jit(solution)/shard_map/all_gather | solution.py:80
  234.8 198.4 %all-gather.16.cloned.1.call-start = ((), (), s32[]{:S(2)}) async-start(), calls=%async_computation.19 | async-start | bytes 3276800 | tf_op jit(solution)/shard_map/all_gather | solution.py:220
  235.4 225.5 %all-gather.26.cloned.1.call-start = ((), (), s32[]{:S(2)}) async-start(), calls=%async_computation.27 | async-start | bytes 3276800 | tf_op jit(solution)/shard_map/all_gather | solution.py:240
  236.1 261.7 %reduce-scatter.29.cloned.1.call-start = ((), (), s32[]{:S(2)}) async-start(), calls=%async_computation.32 | async-start | bytes 3276800 | tf_op jit(solution)/shard_map/reduce_scatter | solution.py:248
  406.9 11.1 copy-start.98
  422.9 111.9 %reduce-scatter.25.cloned.1.call-start = ((), (), s32[]{:S(2)}) async-start(), calls=%async_computation.28 | async-start | bytes 3276800 | tf_op jit(solution)/shard_map/reduce_scatter | solution.py:248
  460.9 11.3 copy-start.99
  477.0 94.7 %reduce-scatter.23.cloned.1.call-start = ((), (), s32[]{:S(2)}) async-start(), calls=%async_computation.26 | async-start | bytes 3276800 | tf_op jit(solution)/shard_map/reduce_scatter | solution.py:225
  486.5 9.6 copy-start.96
  486.5 122.2 %reduce-scatter.19.cloned.1.call-start = ((), (), s32[]{:S(2)}) async-start(), calls=%async_computation.22 | async-start | bytes 3276800 | tf_op jit(solution)/shard_map/reduce_scatter | solution.py:225
  496.1 153.7 %all-gather.32.cloned.1.call-start = ((), (), s32[]{:S(2)}) async-start(), calls=%async_computation.33 | async-start | bytes 3276800 | tf_op jit(solution)/shard_map/all_gather | solution.py:260
  538.2 70.5 %copy-start.37 = (bf16[256,1280]{1,0:T(8,128)(2,1)S(1)}, bf16[256,1280]{1,0:T(8,128)(2,1)}, u32[]{:S(2)}) copy-start(bf16[256,1280]{1,0:T(8,128)(2,1)} %reduce-scatter.25.cloned.1.call-done) | copy-start | bytes 1966084
  577.6 175.9 %all-gather.28.cloned.1.call-start = ((), (), s32[]{:S(2)}) async-start(), calls=%async_computation.29 | async-start | bytes 3276800 | tf_op jit(solution)/shard_map/all_gather | solution.py:260
  614.7 304.0 %reduce-scatter.47.cloned.1.call-start = ((), (), s32[]{:S(2)}) async-start(), calls=%async_computation.42 | async-start | bytes 3686400 | tf_op jit(solution)/shard_map/reduce_scatter | solution.py:95
  624.0 294.7 %reduce-scatter.45.cloned.1.call-start = ((), (), s32[]{:S(2)}) async-start(), calls=%async_computation.41 | async-start | bytes 3686400 | tf_op jit(solution)/shard_map/reduce_scatter | solution.py:95
  633.1 287.9 %reduce-scatter.43.cloned.1.call-start = ((), (), s32[]{:S(2)}) async-start(), calls=%async_computation.40 | async-start | bytes 3686400 | tf_op jit(solution)/shard_map/reduce_scatter | solution.py:92
  641.0 338.5 %reduce-scatter.41.cloned.1.call-start = ((), (), s32[]{:S(2)}) async-start(), calls=%async_computation.39 | async-start | bytes 3686400 | tf_op jit(solution)/shard_map/reduce_scatter | solution.py:92
  649.0 396.9 %reduce-scatter.39.cloned.1.call-start = ((), (), s32[]{:S(2)}) async-start(), calls=%async_computation.38 | async-start | bytes 1105920 | tf_op jit(solution)/shard_map/reduce_scatter | solution.py:89
  653.1 52.0 %copy-start.45 = (bf16[512,320]{0,1:T(8,128)(2,1)}, bf16[512,320]{0,1:T(8,128)(2,1)S(1)}, u32[]{:S(2)}) copy-start(bf16[512,320]{0,1:T(8,128)(2,1)S(1)} %get-tuple-element.114) | copy-start | bytes 983044
  659.2 18.0 %copy-start.33 = (bf16[1024,4,80]{0,2,1:T(8,128)(2,1)S(1)}, bf16[1024,4,80]{0,2,1:T(8,128)(2,1)}, u32[]{:S(2)}) copy-start(bf16[1024,4,80]{0,2,1:T(8,128)(2,1)} %copy-done.32) | copy-start | bytes 1966084
  711.1 18.3 %copy-start.44 = (f32[1024,80]{0,1:T(8,128)S(1)}, f32[1024,80]{0,1:T(8,128)}, u32[]{:S(2)}) copy-start(f32[1024,80]{0,1:T(8,128)} %get-tuple-element.120) | copy-start | bytes 983044
  711.1 401.2 %reduce-scatter.37.cloned.1.call-start = ((), (), s32[]{:S(2)}) async-start(), calls=%async_computation.37 | async-start | bytes 1105920 | tf_op jit(solution)/shard_map/reduce_scatter | solution.py:89
  729.4 24.1 %copy-start.58 = (bf16[1024,4,80]{0,2,1:T(8,128)(2,1)S(1)}, bf16[1024,4,80]{0,2,1:T(8,128)(2,1)}, u32[]{:S(2)}) copy-start(bf16[1024,4,80]{0,2,1:T(8,128)(2,1)} %copy-done.57) | copy-start | bytes 1966084
  772.6 415.2 %reduce-scatter.35.cloned.1.call-start = ((), (), s32[]{:S(2)}) async-start(), calls=%async_computation.36 | async-start | bytes 3317760 | tf_op jit(solution)/shard_map/reduce_scatter | solution.py:86
  791.2 472.5 %reduce-scatter.33.cloned.1.call-start = ((), (), s32[]{:S(2)}) async-start(), calls=%async_computation.35 | async-start | bytes 3317760 | tf_op jit(solution)/shard_map/reduce_scatter | solution.py:86
  816.2 18.0 %copy-start.31 = (bf16[1024,4,80]{0,2,1:T(8,128)(2,1)S(1)}, bf16[1024,4,80]{0,2,1:T(8,128)(2,1)}, u32[]{:S(2)}) copy-start(bf16[1024,4,80]{0,2,1:T(8,128)(2,1)} %copy-done.30) | copy-start | bytes 1966084
  834.2 23.3 %copy-start.42 = (f32[1024,80]{0,1:T(8,128)S(1)}, f32[1024,80]{0,1:T(8,128)}, u32[]{:S(2)}) copy-start(f32[1024,80]{0,1:T(8,128)} %get-tuple-element.122) | copy-start | bytes 983044
  857.5 25.6 %copy-start.19 = (f32[1024,80]{0,1:T(8,128)S(1)}, f32[1024,80]{0,1:T(8,128)}, u32[]{:S(2)}) copy-start(f32[1024,80]{0,1:T(8,128)} %copy-done.18) | copy-start | bytes 983044
  900.2 399.4 %reduce-scatter.31.cloned.1.call-start = ((), (), s32[]{:S(2)}) async-start(), calls=%async_computation.34 | async-start | bytes 3276800 | tf_op jit(solution)/shard_map/reduce_scatter | solution.py:313
  907.7 428.8 %reduce-scatter.27.cloned.1.call-start = ((), (), s32[]{:S(2)}) async-start(), calls=%async_computation.30 | async-start | bytes 3276800 | tf_op jit(solution)/shard_map/reduce_scatter | solution.py:313
  908.0 7.7 copy-start.75
  908.0 8.3 copy-start.73
  908.0 8.3 copy-start.74
  908.0 8.9 copy-start.69
  908.0 8.9 copy-start.70
  914.8 553.6 %all-reduce.20.cloned.1.call-start = ((), (), s32[]{:S(2)}) async-start(), calls=%async_computation.43 | async-start | bytes 172032
  915.0 66.5 %copy-start.62 = (f32[5120]{0:T(1024)}, f32[5120]{0:T(1024)S(1)}, u32[]{:S(2)}) copy-start(f32[5120]{0:T(1024)S(1)} %add_dynamic-update-slice_fusion) | copy-start | bytes 61444
  918.7 417.9 %copy-start.1 = (bf16[2,256,1280]{2,1,0:T(8,128)(2,1)S(1)}, bf16[2,256,1280]{2,1,0:T(8,128)(2,1)}, u32[]{:S(2)}) copy-start(bf16[2,256,1280]{2,1,0:T(8,128)(2,1)} %param.18) | copy-start | bytes 3932164
  918.7 417.9 %copy-start.61 = (f32[1280]{0:T(1024)S(1)}, f32[1280]{0:T(1024)}, u32[]{:S(2)}) copy-start(f32[1280]{0:T(1024)} %copy-done.60) | copy-start | bytes 15364
  918.7 417.9 %copy-start.84 = (f32[256]{0:T(256)S(1)}, f32[256]{0:T(256)}, u32[]{:S(2)}) copy-start(f32[256]{0:T(256)} %copy-done.83) | copy-start | bytes 3076
  918.7 417.9 %copy-start.86 = (f32[256]{0:T(256)S(1)}, f32[256]{0:T(256)}, u32[]{:S(2)}) copy-start(f32[256]{0:T(256)} %copy-done.85) | copy-start | bytes 3076
  918.7 417.9 %copy-start.88 = (f32[256]{0:T(256)S(1)}, f32[256]{0:T(256)}, u32[]{:S(2)}) copy-start(f32[256]{0:T(256)} %copy-done.87) | copy-start | bytes 3076
  918.7 417.9 %copy-start.90 = (f32[256]{0:T(256)S(1)}, f32[256]{0:T(256)}, u32[]{:S(2)}) copy-start(f32[256]{0:T(256)} %copy-done.89) | copy-start | bytes 3076
  920.9 419.4 %copy-start.12 = (f32[256,1280]{1,0:T(8,128)S(1)}, f32[256,1280]{1,0:T(8,128)}, u32[]{:S(2)}) copy-start(f32[256,1280]{1,0:T(8,128)} %copy-done.11) | copy-start | bytes 3932164
  1299.6 40.7 %copy-start.36 = (bf16[256,1280]{1,0:T(8,128)(2,1)S(1)}, bf16[256,1280]{1,0:T(8,128)(2,1)}, u32[]{:S(2)}) copy-start(bf16[256,1280]{1,0:T(8,128)(2,1)} %reduce-scatter.31.cloned.1.call-done) | copy-start | bytes 1966084
  (71 other events, 227.1 us)
Sparse Core Ops, SparseCore 0:
  10.2 61.4 all-gather.13
  73.8 24.2 all-gather.11
  100.2 25.5 all-gather.21
  154.2 34.4 reduce-scatter.20
  191.1 34.4 reduce-scatter.16
  227.7 61.4 all-gather.17
  291.3 24.2 all-gather.23
  317.7 25.5 all-gather.29
  345.4 61.4 all-gather.19
  408.9 24.2 all-gather.15
  435.3 25.5 all-gather.25
  463.2 34.4 reduce-scatter.28
  500.3 34.4 reduce-scatter.24
  537.2 34.4 reduce-scatter.22
  574.1 34.4 reduce-scatter.18
  610.7 25.5 all-gather.31
  638.2 25.5 all-gather.27
  667.2 76.5 reduce-scatter.46
  747.4 74.8 reduce-scatter.44
  825.7 75.0 reduce-scatter.42
  904.4 75.0 reduce-scatter.40
  982.8 63.0 reduce-scatter.38
  1049.3 63.0 reduce-scatter.36
  1115.7 72.0 reduce-scatter.34
  1191.4 72.1 reduce-scatter.32
  1266.0 33.5 reduce-scatter.30
  1302.0 34.4 reduce-scatter.26
  1342.9 125.4 all-reduce.19
where the time goes:
time: 1490 us
  waiting for transfers between devices  880 us (59%)
  matrix products  380 us (26%)
  other arithmetic  81.2 us (5%)
  blocking collectives  80.3 us (5%)
  local copies, waits for them, and re-layouts  44.2 us (3%)
  between operations  16.2 us (1%)
    reduce_scatter x2, waiting for transfers between devices, reduce_grads(): lax.psum_scatter(grad_qkv.astype(jnp.bfloat16), 'dp', scatter_dimension=0...  150 us
    reduce_scatter x2, waiting for transfers between devices, reduce_grads(): lax.psum_scatter(grad_proj.astype(jnp.bfloat16), 'dp', scatter_dimension=...  130 us
    unnamed x29, waiting for transfers between devices  129 us
    dot_general x4, matrix products, on_device(): jnp.einsum('hqk,qhd->khd', score_grad, queries_bf[row_lower:row_upper], p...  94.9 us
    dot_general x4, matrix products, on_device(): jnp.einsum('hqk,khd->qhd', score_grad, keys_bf, preferred_element_type=f32)  72 us
    reduce_scatter x2, waiting for transfers between devices, on_device(): lax.psum_scatter(jnp.einsum('se,de->sd', grad_linear, w_qkv_flat, preferr...  70.8 us
    reduce_scatter x2, waiting for transfers between devices, on_device(): lax.psum_scatter(jnp.dot(activated, w_fc2, preferred_element_type=f32).as...  64.6 us
    all_gather x1, waiting for transfers between devices, gather_weights(): lax.all_gather(fc2_weight, 'dp', axis=1, tiled=True)  63.7 us
  transfers between devices with their start and end apart: 28, of which 21 were waited for; matrix products, arithmetic and copies ran while one was open for 30% of the time, Pallas kernels for 0%

commit v1 on v0

v1 whole, which is shorter than its diff:
```python
import functools
import math

import jax
import jax.numpy as jnp
from jax import lax
from jax.sharding import PartitionSpec as P

HEAD_DIM = 80


norm_eps = 1e-06
masked_score = -1e30


def layer_norm(values, gain_row, shift_row):
    center = values - jnp.mean(values, axis=-1, keepdims=True)
    spread = jnp.mean(center * center, axis=-1, keepdims=True)
    scaled = lax.rsqrt(spread + norm_eps)
    normed = center * scaled
    return (normed * gain_row + shift_row, normed, scaled)


def norm_back(grad_rows, normed, scaled, gain_row):
    grad_hat = grad_rows * gain_row
    mean_one = jnp.mean(grad_hat, axis=-1, keepdims=True)
    mean_two = jnp.mean(grad_hat * normed, axis=-1, keepdims=True)
    return scaled * (grad_hat - mean_one - normed * mean_two)


def rotate_half(values):
    middle = values.shape[-1] // 2
    return jnp.concatenate([-values[..., middle:], values[..., :middle]], axis=-1)


def rotary_tables(row_places, col_places, head_size):
    quarter = head_size // 4
    freqs_base = 10000.0 ** (-(4.0 * jnp.arange(quarter, dtype=jnp.float32)) / head_size)
    angles = jnp.concatenate(
        [
            row_places.astype(jnp.float32)[:, None] * freqs_base[None, :],
            col_places.astype(jnp.float32)[:, None] * freqs_base[None, :],
        ],
        axis=-1,
    )
    angles = jnp.concatenate([angles, angles], axis=-1)[:, None, :]
    return (jnp.cos(angles), jnp.sin(angles))


def rotary_apply(values, cos_table, sin_table):
    return values * cos_table + rotate_half(values) * sin_table


def rotary_back(grad_rows, cos_table, sin_table):
    return grad_rows * cos_table - rotate_half(grad_rows * sin_table)


def key_window(row_ids, row_lengths):
    slot_ids = jnp.arange(row_lengths.shape[0], dtype=jnp.int32)
    offsets = jnp.cumsum(row_lengths) - row_lengths
    picked = (row_ids[:, None] == slot_ids[None, :]).astype(jnp.int32)
    window_start = jnp.sum(picked * offsets[None, :], axis=1)
    return (window_start, window_start + jnp.sum(picked * row_lengths[None, :], axis=1))


def flip_pairs(count, step):
    return [(place, place ^ step) for place in range(count)]


def relative_order(count):
    order = [0]
    step = count // 2
    while step >= 1:
        order = order + [place ^ step for place in order]
        step //= 2
    return order


def gather_rows(rows, count):
    step = count // 2
    while step >= 1:
        received = lax.ppermute(rows, "tensor", flip_pairs(count, step))
        rows = jnp.concatenate([rows, received], axis=0)
        step //= 2
    return rows


def scatter_product(product, rows, count):
    half = rows.shape[0] // 2
    sent = product(rows[half:]).astype(jnp.bfloat16)
    received = lax.ppermute(sent, "tensor", flip_pairs(count, 1))
    total = product(rows[:half]) + received.astype(jnp.float32)
    step = 2
    while step < count:
        half = half // 2
        received = lax.ppermute(
            total[half:].astype(jnp.bfloat16), "tensor", flip_pairs(count, step)
        )
        total = total[:half] + received.astype(jnp.float32)
        step *= 2
    return total


def gather_small(vectors, dp_count, tensor_count):
    count = dp_count * tensor_count
    place = lax.axis_index("dp") * tensor_count + lax.axis_index("tensor")
    packed = jnp.concatenate(vectors, axis=0)
    width = packed.shape[0]
    table = lax.dynamic_update_slice_in_dim(
        jnp.zeros((count, width), packed.dtype), packed[None], place, 0
    )
    step = 1
    while step < count:
        table = table + lax.ppermute(table, ("dp", "tensor"), flip_pairs(count, step))
        step *= 2
    parts = []
    offset = 0
    for vector in vectors:
        size = vector.shape[0]
        parts.append(table[:, offset : offset + size].reshape(count * size))
        offset += size
    return parts


def scatter_small(vectors, dp_count, tensor_count):
    count = dp_count * tensor_count
    place = lax.axis_index("dp") * tensor_count + lax.axis_index("tensor")
    table = jnp.concatenate([vector.reshape(count, -1) for vector in vectors], axis=1)
    near = lax.bitwise_xor(jnp.arange(count, dtype=jnp.int32), place.astype(jnp.int32))
    table = jnp.take(table, near, axis=0)
    step = count // 2
    while step >= 1:
        received = lax.ppermute(table[step:], ("dp", "tensor"), flip_pairs(count, step))
        table = table[:step] + received
        step //= 2
    parts = []
    offset = 0
    for vector in vectors:
        size = vector.shape[0] // count
        parts.append(table[0, offset : offset + size])
        offset += size
    return parts


def block_scores(query_block, keys_bf, start_block, stop_block, key_places, score_scale):
    scores = (
        jnp.einsum("qhd,khd->hqk", query_block, keys_bf, preferred_element_type=jnp.float32)
        * score_scale
    )
    inside = (key_places[None, :] >= start_block[:, None]) & (
        key_places[None, :] < stop_block[:, None]
    )
    return jnp.where(inside[None], scores, masked_score)


def attend_forward(linear, tables, score_scale):
    cos_table, sin_table, start_all, stop_all, key_places = tables
    row_length = linear.shape[0]
    block_rows = min(512, row_length)
    queries_bf = rotary_apply(linear[:, 0], cos_table, sin_table).astype(jnp.bfloat16)
    keys_bf = rotary_apply(linear[:, 1], cos_table, sin_table).astype(jnp.bfloat16)
    values_bf = linear[:, 2].astype(jnp.bfloat16)
    context_blocks = []
    logsum_blocks = []
    for lower in range(0, row_length, block_rows):
        upper = lower + block_rows
        scores = block_scores(
            queries_bf[lower:upper],
            keys_bf,
            start_all[lower:upper],
            stop_all[lower:upper],
            key_places,
            score_scale,
        )
        highest = jnp.max(scores, axis=-1, keepdims=True)
        shifted = jnp.exp(scores - highest)
        totals = jnp.sum(shifted, axis=-1, keepdims=True)
        attend = shifted / totals
        logsum_blocks.append(highest + jnp.log(totals))
        context_blocks.append(
            jnp.einsum(
                "hqk,khd->qhd",
                attend.astype(jnp.bfloat16),
                values_bf,
                preferred_element_type=jnp.float32,
            )
        )
    context_bf = jnp.concatenate(context_blocks, axis=0).astype(jnp.bfloat16)
    return context_bf, (queries_bf, keys_bf, values_bf, logsum_blocks)


def attend_back(kept, grad_context, tables, score_scale):
    cos_table, sin_table, start_all, stop_all, key_places = tables
    queries_bf, keys_bf, values_bf, logsum_blocks = kept
    row_length, head_count, _ = queries_bf.shape
    block_rows = min(512, row_length)
    grad_keys = jnp.zeros((row_length, head_count, HEAD_DIM), jnp.float32)
    grad_values = jnp.zeros((row_length, head_count, HEAD_DIM), jnp.float32)
    query_grad_blocks = []
    for block_index, lower in enumerate(range(0, row_length, block_rows)):
        upper = lower + block_rows
        scores = block_scores(
            queries_bf[lower:upper],
            keys_bf,
            start_all[lower:upper],
            stop_all[lower:upper],
            key_places,
            score_scale,
        )
        attend = jnp.exp(scores - logsum_blocks[block_index])
        context_grad = grad_context[lower:upper]
        grad_values = grad_values + jnp.einsum(
            "hqk,qhd->khd",
            attend.astype(jnp.bfloat16),
            context_grad,
            preferred_element_type=jnp.float32,
        )
        attend_grad = jnp.einsum(
            "qhd,khd->hqk", context_grad, values_bf, preferred_element_type=jnp.float32
        )
        row_inner = jnp.sum(attend * attend_grad, axis=-1, keepdims=True)
        score_grad = (attend * (attend_grad - row_inner) * score_scale).astype(jnp.bfloat16)
        query_grad_blocks.append(
            jnp.einsum("hqk,khd->qhd", score_grad, keys_bf, preferred_element_type=jnp.float32)
        )
        grad_keys = grad_keys + jnp.einsum(
            "hqk,qhd->khd",
            score_grad,
            queries_bf[lower:upper],
            preferred_element_type=jnp.float32,
        )
    grad_queries = jnp.concatenate(query_grad_blocks, axis=0)
    return jnp.stack(
        [
            rotary_back(grad_queries, cos_table, sin_table),
            rotary_back(grad_keys, cos_table, sin_table),
            grad_values,
        ],
        axis=1,
    ).astype(jnp.bfloat16)


def dot_nn(left, right):
    return jnp.dot(left, right, preferred_element_type=jnp.float32)


def dot_nt(left, right):
    return jnp.einsum("sk,nk->sn", left, right, preferred_element_type=jnp.float32)


def dot_tn(left, right):
    return jnp.einsum("sm,sn->mn", left, right, preferred_element_type=jnp.float32)


def on_device(
    dp_count,
    tensor_count,
    tokens,
    pic_ids,
    pos_rows,
    pos_cols,
    lengths,
    ln1_gain,
    ln1_bias,
    qkv_weight,
    qkv_bias,
    proj_weight,
    proj_bias,
    ln2_gain,
    ln2_bias,
    fc1_weight,
    fc1_bias,
    fc2_weight,
    fc2_bias,
    cotangent,
):
    row_total = tokens.shape[0]
    local_rows = tokens.shape[1]
    model_width = tokens.shape[2]
    row_length = pic_ids.shape[1]
    head_width = qkv_weight.shape[2]
    hidden_width = fc1_weight.shape[1]
    head_count = head_width // HEAD_DIM
    score_scale = 1.0 / math.sqrt(HEAD_DIM)
    tensor_place = lax.axis_index("tensor")
    f32 = jnp.float32
    bf16 = jnp.bfloat16
    order = jnp.array(relative_order(tensor_count), jnp.int32)
    block_ids = lax.bitwise_xor(order, tensor_place.astype(jnp.int32))
    all_places = (
        block_ids[:, None] * local_rows + jnp.arange(local_rows, dtype=jnp.int32)[None, :]
    ).reshape(row_length)

    def near_order(values):
        return jnp.take(values.reshape(tensor_count, local_rows), block_ids, axis=0).reshape(
            row_length
        )

    local_places = all_places[:local_rows]
    vectors = gather_small(
        (ln1_gain, ln1_bias, qkv_bias, proj_bias, ln2_gain, ln2_bias, fc1_bias, fc2_bias),
        dp_count,
        tensor_count,
    )
    gain_one, shift_one, qkv_shift, proj_shift, gain_two, shift_two, fc1_shift, fc2_shift = [
        vector_part.astype(f32) for vector_part in vectors
    ]
    qkv_local_shift = lax.dynamic_slice_in_dim(
        qkv_shift.reshape(3, model_width), tensor_place * head_width, head_width, 1
    ).reshape(3 * head_width)
    fc1_local_shift = lax.dynamic_slice_in_dim(
        fc1_shift, tensor_place * hidden_width, hidden_width, 0
    )
    w_qkv = lax.all_gather(qkv_weight, "dp", axis=0, tiled=True)
    w_proj = lax.all_gather(proj_weight, "dp", axis=1, tiled=True)
    w_fc1 = lax.all_gather(fc1_weight, "dp", axis=0, tiled=True)
    w_fc2 = lax.all_gather(fc2_weight, "dp", axis=1, tiled=True)
    w_qkv_flat = w_qkv.reshape(model_width, 3 * head_width)

    outputs = []
    saved = []
    for row in range(row_total):
        tokens_row = tokens[row].astype(f32)
        start_all, stop_all = key_window(near_order(pic_ids[row]), lengths[row])
        cos_table, sin_table = rotary_tables(
            near_order(pos_rows[row]), near_order(pos_cols[row]), HEAD_DIM
        )
        tables = (cos_table, sin_table, start_all, stop_all, all_places)
        pad_rows = (local_places < jnp.sum(lengths[row])).astype(f32)[:, None]
        grad_out = pad_rows * cotangent[row].astype(f32)
        grad_branch = gather_rows(grad_out.astype(bf16), tensor_count)
        normed_one, hat_one, scale_one = layer_norm(tokens_row, gain_one, shift_one)
        lowered_one = gather_rows(normed_one.astype(bf16), tensor_count)
        linear = dot_nn(lowered_one, w_qkv_flat) + qkv_local_shift
        linear = linear.reshape(row_length, 3, head_count, HEAD_DIM)
        context_bf, kept = attend_forward(linear, tables, score_scale)
        context_bf = context_bf.reshape(row_length, head_width)
        attn_branch = scatter_product(
            lambda part: dot_nn(part, w_proj), context_bf, tensor_count
        )
        hidden_row = tokens_row + attn_branch + proj_shift
        normed_two, hat_two, scale_two = layer_norm(hidden_row, gain_two, shift_two)
        lowered_two = gather_rows(normed_two.astype(bf16), tensor_count)
        upward = dot_nn(lowered_two, w_fc1) + fc1_local_shift
        activated = (upward * jax.nn.sigmoid(1.702 * upward)).astype(bf16)
        branch = scatter_product(lambda part: dot_nn(part, w_fc2), activated, tensor_count)
        outputs.append((pad_rows * (hidden_row + branch + fc2_shift)).astype(bf16))
        saved.append(
            (
                tables,
                grad_out,
                grad_branch,
                hat_one,
                scale_one,
                lowered_one,
                context_bf,
                kept,
                hat_two,
                scale_two,
                lowered_two,
                upward,
                activated,
            )
        )

    token_grads = []
    totals = None
    for row in range(row_total):
        (
            tables,
            grad_out,
            grad_branch,
            hat_one,
            scale_one,
            lowered_one,
            context_bf,
            kept,
            hat_two,
            scale_two,
            lowered_two,
            upward,
            activated,
        ) = saved[row]
        micro_fc2 = dot_tn(activated, grad_branch)
        sigmoid_up = jax.nn.sigmoid(1.702 * upward)
        grad_up = (
            dot_nt(grad_branch, w_fc2)
            * (sigmoid_up + 1.702 * upward * sigmoid_up * (1.0 - sigmoid_up))
        ).astype(bf16)
        micro_fc1 = dot_tn(lowered_two, grad_up)
        grad_normed_two = scatter_product(
            lambda part: dot_nt(part, w_fc1), grad_up, tensor_count
        )
        grad_hidden = grad_out + norm_back(grad_normed_two, hat_two, scale_two, gain_two)
        grad_attn = gather_rows(grad_hidden.astype(bf16), tensor_count)
        micro_proj = dot_tn(context_bf, grad_attn)
        grad_context = (
            dot_nt(grad_attn, w_proj).astype(bf16).reshape(row_length, head_count, HEAD_DIM)
        )
        grad_linear = attend_back(kept, grad_context, tables, score_scale).reshape(
            row_length, 3 * head_width
        )
        micro_qkv = dot_tn(lowered_one, grad_linear)
        grad_normed_one = scatter_product(
            lambda part: dot_nt(part, w_qkv_flat), grad_linear, tensor_count
        )
        token_grads.append(
            (grad_hidden + norm_back(grad_normed_one, hat_one, scale_one, gain_one)).astype(bf16)
        )
        parts = (
            jnp.sum(grad_normed_one * hat_one, axis=0),
            jnp.sum(grad_normed_one, axis=0),
            jnp.sum(grad_linear.astype(f32), axis=0),
            jnp.sum(grad_hidden, axis=0),
            jnp.sum(grad_normed_two * hat_two, axis=0),
            jnp.sum(grad_normed_two, axis=0),
            jnp.sum(grad_up.astype(f32), axis=0),
            jnp.sum(grad_out, axis=0),
            micro_qkv,
            micro_proj,
            micro_fc1,
            micro_fc2,
        )
        totals = parts if totals is None else tuple(a + b for a, b in zip(totals, parts))

    grad_fc2 = lax.psum_scatter(
        totals[11].astype(bf16), "dp", scatter_dimension=1, tiled=True
    ).astype(f32)
    grad_fc1 = lax.psum_scatter(
        totals[10].astype(bf16), "dp", scatter_dimension=0, tiled=True
    ).astype(f32)
    grad_proj = lax.psum_scatter(
        totals[9].astype(bf16), "dp", scatter_dimension=1, tiled=True
    ).astype(f32)
    grad_qkv = lax.psum_scatter(
        totals[8].reshape(model_width, 3, head_width).astype(bf16),
        "dp",
        scatter_dimension=0,
        tiled=True,
    ).astype(f32)
    qkv_full_grad = lax.dynamic_update_slice_in_dim(
        jnp.zeros((3, model_width), f32),
        totals[2].reshape(3, head_width),
        tensor_place * head_width,
        1,
    ).reshape(3 * model_width)
    fc1_full_grad = lax.dynamic_update_slice_in_dim(
        jnp.zeros((fc1_shift.shape[0],), f32), totals[6], tensor_place * hidden_width, 0
    )
    small_out = scatter_small(
        (
            totals[0],
            totals[1],
            qkv_full_grad,
            totals[3],
            totals[4],
            totals[5],
            fc1_full_grad,
            totals[7],
        ),
        dp_count,
        tensor_count,
    )
    return (
        jnp.stack(outputs, axis=0),
        jnp.stack(token_grads, axis=0),
        small_out[0],
        small_out[1],
        grad_qkv,
        small_out[2],
        grad_proj,
        small_out[3],
        small_out[4],
        small_out[5],
        grad_fc1,
        small_out[6],
        grad_fc2,
        small_out[7],
    )


def solution(mesh):
    placed = (
        P("dp", "tensor", None),
        P("dp", None),
        P("dp", None),
        P("dp", None),
        P("dp", None),
        P(("dp", "tensor")),
        P(("dp", "tensor")),
        P("dp", None, "tensor"),
        P(("dp", "tensor")),
        P("tensor", "dp"),
        P(("dp", "tensor")),
        P(("dp", "tensor")),
        P(("dp", "tensor")),
        P("dp", "tensor"),
        P(("dp", "tensor")),
        P("tensor", "dp"),
        P(("dp", "tensor")),
        P("dp", "tensor", None),
    )
    return jax.shard_map(
        functools.partial(on_device, mesh.shape["dp"], mesh.shape["tensor"]),
        mesh=mesh,
        in_specs=placed,
        out_specs=(
            P("dp", "tensor", None),
            P("dp", "tensor", None),
            P(("dp", "tensor")),
            P(("dp", "tensor")),
            P("dp", None, "tensor"),
            P(("dp", "tensor")),
            P("tensor", "dp"),
            P(("dp", "tensor")),
            P(("dp", "tensor")),
            P(("dp", "tensor")),
            P("dp", "tensor"),
            P(("dp", "tensor")),
            P("tensor", "dp"),
            P(("dp", "tensor")),
        ),
        check_vma=False,
    )
```

time: 1490 us -> 907 us (0.61)
  waiting for transfers between devices: 880 us -> 336 us
  blocking collectives: 80.3 us -> 34.9 us
  starting transfers between devices: 3.34 us -> 41.5 us
  matrix products: 380 us -> 353 us
    reduce_scatter x16 -> x4, waiting for transfers between devices: 560 us -> 87.3 us  [the longest x1 73.9 us: on_device(): lax.psum_scatter(totals[8].reshape(model_width, 3, head_width).astype(bf1...]
    ppermute x0 -> x42, waiting for transfers between devices: none -> 248 us  [the longest x16 122 us: gather_rows(): received = lax.ppermute(rows, 'tensor', flip_pairs(count, step))]
    all_gather x11 -> x3, waiting for transfers between devices: 192 us -> 0.1 us  [the longest x1 0.1 us: on_device(): w_fc2 = lax.all_gather(fc2_weight, 'dp', axis=1, tiled=True)]
    unnamed x29 -> x7, waiting for transfers between devices: 129 us -> 0.78 us
    unnamed x1 -> x0, blocking collectives: 45.2 us -> none
    ppermute x0 -> x42, starting transfers between devices: none -> 41.3 us  [the longest x16 13.1 us: gather_rows(): received = lax.ppermute(rows, 'tensor', flip_pairs(count, step))]
    dot_general x44 -> x52, matrix products: 373 us -> 345 us  [the longest x4 98 us: attend_back(): jnp.einsum('hqk,qhd->khd', score_grad, queries_bf[lower:upper], preferred...]
    unnamed x238 -> x293, local copies, waits for them, and re-layouts: 37.2 us -> 21.1 us
  transfers between devices with their start and end apart: 28 -> 49, of which waited for: 21 -> 31; matrix products, arithmetic and copies ran while one was open for 30% -> 31% of each run, Pallas kernels for 0% -> 0%
where the time goes in v1:
time: 907 us; the launch traced here: 902 us
  matrix products  353 us (39%)
  waiting for transfers between devices  336 us (37%)
  other arithmetic  69.4 us (8%)
  local copies, waits for them, and re-layouts  50.6 us (6%)
  starting transfers between devices  41.5 us (5%)
  blocking collectives  34.9 us (4%)
  between operations  16.7 us (2%)
    ppermute x16, waiting for transfers between devices, gather_rows(): received = lax.ppermute(rows, 'tensor', flip_pairs(count, step))  122 us
    ppermute x8, waiting for transfers between devices, scatter_product(): lax.ppermute(total[half:].astype(jnp.bfloat16), 'tensor', flip_pairs(coun...  107 us
    dot_general x4, matrix products, attend_back(): jnp.einsum('hqk,qhd->khd', score_grad, queries_bf[lower:upper], preferred...  98 us
    dot_general x4, matrix products, attend_back(): jnp.einsum('hqk,khd->qhd', score_grad, keys_bf, preferred_element_type=jn...  81.6 us
    reduce_scatter x1, waiting for transfers between devices, on_device(): lax.psum_scatter(totals[8].reshape(model_width, 3, head_width).astype(bf1...  73.9 us
    dot_general x8, matrix products, dot_tn(): jnp.einsum('sm,sn->mn', left, right, preferred_element_type=jnp.float32)  39.8 us
    dot_general x12, matrix products, dot_nt(): jnp.einsum('sk,nk->sn', left, right, preferred_element_type=jnp.float32)  37.3 us
    dot_general x12, matrix products, dot_nn(): return jnp.dot(left, right, preferred_element_type=jnp.float32)  37.1 us
  transfers between devices with their start and end apart: 49, of which 31 were waited for; matrix products, arithmetic and copies ran while one was open for 31% of the time, Pallas kernels for 0%

profile of v1, /device:TPU:0, one launch (start us, length us, event | category | flops | bytes accessed | tf_op | source)
XLA Modules:
  0.0 902.3 jit_solution(6582707140440420876)
XLA Ops:
  8.0 5.4 concatenate.178
  37.9 2.9 collective-permute-start.4
  46.2 12.2 %collective-permute-done.5 = bf16[256,1280]{1,0:T(8,128)(2,1)S(1)} collective-permute-done((bf16[256,1280]{1,0:T(8,128)(2,1)S(1)}, bf16[256,1280]{1,0:T(8,128)(2,1)S(1)}, u32[]{:S(2)}, u32[]{:S(2)}) %collective-permute-start.5) | collective-permute-done | bytes 655392 | tf_op jit(solution)/shard_map/ppermute | solution.py:82
  61.5 34.9 %all_gather.13 = bf16[320,1280]{0,1:T(8,128)(2,1)S(1)} all-gather(bf16[320,160]{0,1:T(8,128)(2,1)S(1)} %copy-done.90), channel_id=1, replica_groups=mesh['dp'=8,'tensor'=4] {'dp'}, dimensions={1}, use_global_device_ids=true | all-gather | bytes 921600 | tf_op jit(solution)/shard_map/all_gather | solution.py:315
  96.5 3.1 compare_and_fusion
  100.0 5.3 copy.38
  105.2 5.4 broadcast_add_fusion.1
  118.4 2.8 fusion.243
  124.2 2.9 fusion.10
  127.5 2.8 fusion.244
  134.4 15.5 %collective-permute-done.8 = bf16[256,1280]{1,0:T(8,128)(2,1)} collective-permute-done((bf16[256,1280]{1,0:T(8,128)(2,1)S(1)}, bf16[256,1280]{1,0:T(8,128)(2,1)}, u32[]{:S(2)}, u32[]{:S(2)}) %collective-permute-start.8) | collective-permute-done | bytes 655392 | tf_op jit(solution)/shard_map/ppermute | solution.py:96
  155.0 13.6 %collective-permute-done.9 = bf16[256,1280]{1,0:T(8,128)(2,1)S(1)} collective-permute-done((bf16[256,1280]{1,0:T(8,128)(2,1)S(1)}, bf16[256,1280]{1,0:T(8,128)(2,1)S(1)}, u32[]{:S(2)}, u32[]{:S(2)}) %collective-permute-start.9) | collective-permute-done | bytes 655392 | tf_op jit(solution)/shard_map/ppermute | solution.py:82
  172.3 16.0 %collective-permute-done.21 = bf16[256,1280]{1,0:T(8,128)(2,1)} collective-permute-done((bf16[256,1280]{1,0:T(8,128)(2,1)}, bf16[256,1280]{1,0:T(8,128)(2,1)}, u32[]{:S(2)}, u32[]{:S(2)}) %collective-permute-start.21) | collective-permute-done | bytes 655392 | tf_op jit(solution)/shard_map/ppermute | solution.py:82
  190.8 9.7 %multiply_convert_fusion.7 = (bf16[1024,1280]{1,0:T(8,128)(2,1)}, f32[1024,1280]{1,0:T(8,128)}) fusion(f32[1280]{0:T(1024)S(1)} %dynamic_slice.7, bf16[1280,1280]{1,0:T(8,128)(2,1)} %all-gather.6.cloned.1.call-done, bf16[512,1280]{1,0:T(8,128)(2,1)} %collective-permute-done.10, bf16[256,1280]{1,0:T(8,128)(2,1)} %copy-done.66, bf16[256,1280]{1,0:T(8,128)(2,1)} %copy-done.41), kind=kOutput, calls=%fused_computation.57 | convolution fusion | flops 3372482560 | bytes 13767680 | tf_op jit(solution)/shard_map/dot_general | solution.py:244
  200.6 9.6 %convert_reduce_fusion.1 = (f32[1280]{0:T(1024)}, bf16[1024,1280]{1,0:T(8,128)(2,1)S(1)}) fusion(f32[1024,1280]{1,0:T(8,128)} %get-tuple-element.160, f32[1280]{0:T(1024)S(1)} %dynamic_slice.7, bf16[1280,1280]{0,1:T(8,128)(2,1)} %all-gather.8.cloned.1.call-done, bf16[512,1280]{1,0:T(8,128)(2,1)} %collective-permute-done.22, ...), kind=kOutput, calls=%fused_computation.52 | convolution fusion | flops 3380345600 | bytes 13772800 | tf_op jit(solution)/shard_map/sk,nk->sn/dot_general | solution.py:248
  213.9 3.0 convolution_convert_fusion.6
  222.8 4.9 convert_add_fusion.6
  228.8 10.7 %collective-permute-done.24 = bf16[256,1280]{1,0:T(8,128)(2,1)} collective-permute-done((bf16[256,1280]{1,0:T(8,128)(2,1)}, bf16[256,1280]{1,0:T(8,128)(2,1)}, u32[]{:S(2)}, u32[]{:S(2)}) %collective-permute-start.24) | collective-permute-done | bytes 655392 | tf_op jit(solution)/shard_map/ppermute | solution.py:96
  241.8 10.7 %collective-permute-done.12 = bf16[256,1280]{1,0:T(8,128)(2,1)S(1)} collective-permute-done((bf16[256,1280]{1,0:T(8,128)(2,1)S(1)}, bf16[256,1280]{1,0:T(8,128)(2,1)S(1)}, u32[]{:S(2)}, u32[]{:S(2)}) %collective-permute-start.12) | collective-permute-done | bytes 655392 | tf_op jit(solution)/shard_map/ppermute | solution.py:96
  252.6 3.8 fusion.235
  259.0 14.4 %collective-permute-done.25 = bf16[256,1280]{1,0:T(8,128)(2,1)S(1)} collective-permute-done((bf16[256,1280]{1,0:T(8,128)(2,1)S(1)}, bf16[256,1280]{1,0:T(8,128)(2,1)S(1)}, u32[]{:S(2)}, u32[]{:S(2)}) %collective-permute-start.25) | collective-permute-done | bytes 655392 | tf_op jit(solution)/shard_map/ppermute | solution.py:82
  273.6 3.0 collective-permute-done.26
  278.5 5.9 fusion.392
  284.4 22.6 %fusion.31 = f32[4,80,512]{2,1,0:T(8,128)} fusion(bf16[1024,4,80]{0,2,1:T(8,128)(2,1)S(1)} %get-tuple-element.65, f32[4,512,1024]{2,1,0:T(8,128)} %fusion.392, f32[4,512,1024]{2,1,0:T(8,128)} %copy-done.5, f32[4,512]{1,0:T(4,128)S(1)} %log_add_fusion.3, pred[512,1024]{1,0:T(8,128)(4,1)} %get-tuple-element.118), kind=kOutput, calls=%fused_computation.62 | convolution fusion | flops 358616064 | bytes 18620416 | tf_op jit(solution)/shard_map/hqk,khd->qhd/dot_general | solution.py:224
  307.0 23.7 %fusion.28 = f32[4,80,1024]{2,1,0:T(8,128)} fusion(f32[4,512,1024]{2,1,0:T(8,128)} %fusion.392, f32[4,512,1024]{2,1,0:T(8,128)} %copy-done.5, f32[4,512]{1,0:T(4,128)S(1)} %log_add_fusion.3, pred[512,1024]{1,0:T(8,128)(4,1)} %get-tuple-element.118, bf16[1024,4,80]{0,2,1:T(8,128)(2,1)} %copy-done.39), kind=kOutput, calls=%fused_computation.61 | convolution fusion | flops 358616064 | bytes 36257792 | tf_op jit(solution)/shard_map/hqk,qhd->khd/dot_general | solution.py:226
  330.7 6.2 fusion.390
  336.9 5.2 fusion.106
  342.2 3.4 fusion.154
  345.6 22.8 %fusion.38 = f32[4,80,512]{2,1,0:T(8,128)} fusion(bf16[1024,4,80]{0,2,1:T(8,128)(2,1)S(1)} %get-tuple-element.65, f32[4,512,1024]{2,1,0:T(8,128)} %fusion.390, f32[4,512,1024]{2,1,0:T(8,128)} %copy-done.4, f32[4,512]{1,0:T(4,128)S(1)} %log_add_fusion.2, pred[512,1024]{1,0:T(8,128)(4,1)} %get-tuple-element.120), kind=kOutput, calls=%fused_computation.65 | convolution fusion | flops 358616064 | bytes 18620416 | tf_op jit(solution)/shard_map/hqk,khd->qhd/dot_general | solution.py:224
  368.3 25.7 %maximum_multiply_fusion.5 = (f32[1024,4,80]{0,2,1:T(8,128)}, f32[1024,4,80]{0,2,1:T(8,128)}, f32[1024,4,80]{0,2,1:T(8,128)}) fusion(f32[512,4,80]{0,2,1:T(8,128)} %bitcast.333, f32[512,4,80]{0,2,1:T(8,128)} %bitcast.331, f32[1024,80]{0,1:T(8,128)S(1)} %copy-done.56, f32[4,80,1024]{2,1,0:T(8,128)} %fusion.28, f32[4,512,1024]{2,1,0:T(8,128)} %fusion.390, ...), kind=kOutput, calls=%fused_computation.265 | convolution fusion | flops 359926784 | bytes 41828352 | tf_op jit(solution)/shard_map/hqk,qhd->khd/dot_general | solution.py:226
  402.9 2.9 collective-permute-done.27
  409.3 15.0 %collective-permute-done.28 = bf16[256,1280]{1,0:T(8,128)(2,1)S(1)} collective-permute-done((bf16[256,1280]{1,0:T(8,128)(2,1)S(1)}, bf16[256,1280]{1,0:T(8,128)(2,1)S(1)}, u32[]{:S(2)}, u32[]{:S(2)}) %collective-permute-start.28) | collective-permute-done | bytes 655392 | tf_op jit(solution)/shard_map/ppermute | solution.py:96
  429.3 14.2 %collective-permute-done.13 = bf16[256,1280]{1,0:T(8,128)(2,1)S(1)} collective-permute-done((bf16[256,1280]{1,0:T(8,128)(2,1)S(1)}, bf16[256,1280]{1,0:T(8,128)(2,1)S(1)}, u32[]{:S(2)}, u32[]{:S(2)}) %collective-permute-start.13) | collective-permute-done | bytes 655392 | tf_op jit(solution)/shard_map/ppermute | solution.py:82
  446.7 2.7 broadcast_add_fusion
  456.5 2.8 fusion.241
  465.6 2.8 fusion.242
  471.2 15.3 %collective-permute-done.16 = bf16[256,1280]{1,0:T(8,128)(2,1)S(1)} collective-permute-done((bf16[256,1280]{1,0:T(8,128)(2,1)S(1)}, bf16[256,1280]{1,0:T(8,128)(2,1)S(1)}, u32[]{:S(2)}, u32[]{:S(2)}) %collective-permute-start.16) | collective-permute-done | bytes 655392 | tf_op jit(solution)/shard_map/ppermute | solution.py:96
  489.3 14.4 %collective-permute-done.17 = bf16[256,1280]{1,0:T(8,128)(2,1)S(1)} collective-permute-done((bf16[256,1280]{1,0:T(8,128)(2,1)S(1)}, bf16[256,1280]{1,0:T(8,128)(2,1)S(1)}, u32[]{:S(2)}, u32[]{:S(2)}) %collective-permute-start.17) | collective-permute-done | bytes 655392 | tf_op jit(solution)/shard_map/ppermute | solution.py:82
  505.7 15.3 %collective-permute-done.29 = bf16[256,1280]{1,0:T(8,128)(2,1)S(1)} collective-permute-done((bf16[256,1280]{1,0:T(8,128)(2,1)S(1)}, bf16[256,1280]{1,0:T(8,128)(2,1)S(1)}, u32[]{:S(2)}, u32[]{:S(2)}) %collective-permute-start.29) | collective-permute-done | bytes 655392 | tf_op jit(solution)/shard_map/ppermute | solution.py:82
  521.2 4.0 multiply_convert_fusion.6
  525.3 7.0 convert_reduce_fusion
  543.6 13.5 %collective-permute-done.32 = bf16[256,1280]{1,0:T(8,128)(2,1)S(1)} collective-permute-done((bf16[256,1280]{1,0:T(8,128)(2,1)S(1)}, bf16[256,1280]{1,0:T(8,128)(2,1)S(1)}, u32[]{:S(2)}, u32[]{:S(2)}) %collective-permute-start.32) | collective-permute-done | bytes 655392 | tf_op jit(solution)/shard_map/ppermute | solution.py:96
  557.8 12.8 %collective-permute-done.20 = bf16[256,1280]{1,0:T(8,128)(2,1)S(1)} collective-permute-done((bf16[256,1280]{1,0:T(8,128)(2,1)S(1)}, bf16[256,1280]{1,0:T(8,128)(2,1)S(1)}, u32[]{:S(2)}, u32[]{:S(2)}) %collective-permute-start.20) | collective-permute-done | bytes 655392 | tf_op jit(solution)/shard_map/ppermute | solution.py:96
  574.2 14.4 %collective-permute-done.33 = bf16[256,1280]{1,0:T(8,128)(2,1)S(1)} collective-permute-done((bf16[256,1280]{1,0:T(8,128)(2,1)S(1)}, bf16[256,1280]{1,0:T(8,128)(2,1)S(1)}, u32[]{:S(2)}, u32[]{:S(2)}) %collective-permute-start.33) | collective-permute-done | bytes 655392 | tf_op jit(solution)/shard_map/ppermute | solution.py:82
  588.8 3.0 collective-permute-done.34
  596.2 6.3 fusion.245
  602.6 7.7 fusion.9
  611.3 6.2 fusion.246
  617.6 7.2 fusion.8
  628.5 5.9 fusion.386
  634.4 18.3 %fusion.45 = f32[4,80,512]{2,1,0:T(8,128)} fusion(bf16[1024,4,80]{0,2,1:T(8,128)(2,1)S(1)} %get-tuple-element.63, f32[4,512,1024]{2,1,0:T(8,128)} %fusion.386, f32[4,512,1024]{2,1,0:T(8,128)} %copy-done.3, f32[4,512]{1,0:T(4,128)S(1)} %log_add_fusion.1, pred[512,1024]{1,0:T(8,128)(4,1)S(1)} %copy-done.27), kind=kOutput, calls=%fused_computation.68 | convolution fusion | flops 358616064 | bytes 18620416 | tf_op jit(solution)/shard_map/hqk,khd->qhd/dot_general | solution.py:224
  652.7 6.0 fusion.384
  658.6 17.9 %fusion.52 = f32[4,80,512]{2,1,0:T(8,128)} fusion(bf16[1024,4,80]{0,2,1:T(8,128)(2,1)S(1)} %get-tuple-element.63, f32[4,512,1024]{2,1,0:T(8,128)} %fusion.384, f32[4,512,1024]{2,1,0:T(8,128)} %copy-done.2, f32[4,512]{1,0:T(4,128)S(1)} %log_add_fusion, pred[512,1024]{1,0:T(8,128)(4,1)S(1)} %copy-done.29), kind=kOutput, calls=%fused_computation.71 | convolution fusion | flops 358616064 | bytes 18620416 | tf_op jit(solution)/shard_map/hqk,khd->qhd/dot_general | solution.py:224
  676.6 23.8 %fusion.42 = f32[4,80,1024]{2,1,0:T(8,128)} fusion(f32[4,512,1024]{2,1,0:T(8,128)} %fusion.386, f32[4,512,1024]{2,1,0:T(8,128)} %copy-done.3, f32[4,512]{1,0:T(4,128)S(1)} %log_add_fusion.1, pred[512,1024]{1,0:T(8,128)(4,1)S(1)} %copy-done.27, bf16[1024,4,80]{0,2,1:T(8,128)(2,1)S(1)} %copy-done.38), kind=kOutput, calls=%fused_computation.67 | convolution fusion | flops 358616064 | bytes 36257792 | tf_op jit(solution)/shard_map/hqk,qhd->khd/dot_general | solution.py:226
  700.4 24.9 %maximum_multiply_fusion.7 = (f32[1024,4,80]{0,2,1:T(8,128)}, f32[1024,4,80]{0,2,1:T(8,128)}, f32[1024,4,80]{0,2,1:T(8,128)}) fusion(f32[512,4,80]{0,2,1:T(8,128)} %bitcast.337, f32[512,4,80]{0,2,1:T(8,128)S(1)} %bitcast.335, f32[1024,80]{0,1:T(8,128)S(1)} %copy-done.58, f32[4,80,1024]{2,1,0:T(8,128)} %fusion.42, f32[4,512,1024]{2,1,0:T(8,128)} %fusion.384, ...), kind=kOutput, calls=%fused_computation.272 | convolution fusion | flops 359926784 | bytes 41828352 | tf_op jit(solution)/shard_map/hqk,qhd->khd/dot_general | solution.py:226
  728.6 5.0 fusion.102
  743.9 5.5 add_convert_fusion
  749.4 5.3 copy.39
  754.8 3.8 convert_add_fusion
  763.4 13.9 %collective-permute-done.36 = bf16[256,1280]{1,0:T(8,128)(2,1)S(1)} collective-permute-done((bf16[256,1280]{1,0:T(8,128)(2,1)S(1)}, bf16[256,1280]{1,0:T(8,128)(2,1)S(1)}, u32[]{:S(2)}, u32[]{:S(2)}) %collective-permute-start.36) | collective-permute-done | bytes 655392 | tf_op jit(solution)/shard_map/ppermute | solution.py:96
  788.3 3.2 collective-permute-done.38
  792.1 3.1 collective-permute-done.39
  804.0 13.5 %reduce-scatter.9.cloned.1.call-done = bf16[160,1280]{1,0:T(8,128)(2,1)} async-done(((bf16[1280,1280]{1,0:T(8,128)(2,1)}), bf16[160,1280]{1,0:T(8,128)(2,1)}) %reduce-scatter.9.cloned.1.call-update) | async-done | bytes 409616 | tf_op jit(solution)/shard_map/reduce_scatter | solution.py:429
  819.4 73.9 %reduce-scatter.5.cloned.1.call-done = bf16[160,3,320]{2,0,1:T(8,128)(2,1)} async-done(((bf16[1280,3,320]{2,0,1:T(8,128)(2,1)}), bf16[160,3,320]{2,0,1:T(8,128)(2,1)}) %reduce-scatter.5.cloned.1.call-update) | async-done | bytes 307216 | tf_op jit(solution)/shard_map/reduce_scatter | solution.py:435
  (582 shorter events, 185.7 us)
Async XLA Ops:
  7.2 28.6 %copy-start.121 = (s32[4]{0:T(128)S(1)}, s32[4]{0:T(128)}, u32[]{:S(2)}) copy-start(s32[4]{0:T(128)} %constant.100.clone) | copy-start | bytes 52
  7.2 92.7 %all-gather.4.cloned.1.call-start = ((), (), s32[]{:S(2)}) async-start(), calls=%async_computation.4 | async-start | bytes 3317760 | tf_op jit(solution)/shard_map/all_gather | solution.py:314
  7.9 182.8 %all-gather.6.cloned.1.call-start = ((), (), s32[]{:S(2)}) async-start(), calls=%async_computation.5 | async-start | bytes 3686400 | tf_op jit(solution)/shard_map/all_gather | solution.py:316
  13.5 11.3 %collective-permute-start = (bf16[32,520]{1,0:T(8,128)(2,1)S(1)}, bf16[32,520]{1,0:T(8,128)(2,1)S(1)}, u32[]{:S(2)}, u32[]{:S(2)}) collective-permute-start(bf16[32,520]{1,0:T(8,128)(2,1)S(1)} %dynamic_update_slice.11), channel_id=1, source_target_pairs={{0,1},{1,0},{2,3},{3,2},{4,5},{5,4},{6,7},{7,6},{8,9},{9,8},{10,11... | collective-permute-start | bytes 99848 | tf_op jit(solution)/shard_map/ppermute | solution.py:114
  14.1 186.5 %all-gather.8.cloned.1.call-start = ((), (), s32[]{:S(2)}) async-start(), calls=%async_computation.6 | async-start | bytes 3686400 | tf_op jit(solution)/shard_map/all_gather | solution.py:317
  24.8 34.8 %copy-start.106 = (f32[256]{0:T(256)}, f32[256]{0:T(256)S(1)}, u32[]{:S(2)}) copy-start(f32[256]{0:T(256)S(1)} %broadcast_multiply_fusion.17) | copy-start | bytes 3076
  24.9 4.8 collective-permute-start.1
  29.7 4.1 collective-permute-start.2
  33.8 4.1 collective-permute-start.3
  37.9 5.2 collective-permute-start.4
  43.7 61.5 %copy-start.47 = (bf16[256,1280]{1,0:T(8,128)(2,1)}, bf16[256,1280]{1,0:T(8,128)(2,1)S(1)}, u32[]{:S(2)}) copy-start(bf16[256,1280]{1,0:T(8,128)(2,1)S(1)} %fusion.185) | copy-start | bytes 1966084
  43.7 14.6 %collective-permute-start.5 = (bf16[256,1280]{1,0:T(8,128)(2,1)S(1)}, bf16[256,1280]{1,0:T(8,128)(2,1)S(1)}, u32[]{:S(2)}, u32[]{:S(2)}) collective-permute-start(bf16[256,1280]{1,0:T(8,128)(2,1)S(1)} %fusion.185), channel_id=1, source_target_pairs={{0,2},{1,3},{2,0},{3,1},{4,6},{5,7},{6,4},{7,5},{8,10},{9,11},{10,... | collective-permute-start | bytes 1966088 | tf_op jit(solution)/shard_map/ppermute | solution.py:82
  59.6 45.6 %collective-permute-start.6 = (bf16[512,1280]{1,0:T(8,128)(2,1)}, bf16[512,1280]{1,0:T(8,128)(2,1)}, u32[]{:S(2)}, u32[]{:S(2)}) collective-permute-start(bf16[512,1280]{1,0:T(8,128)(2,1)} %pad_maximum_fusion.8), channel_id=1, source_target_pairs={{0,1},{1,0},{2,3},{3,2},{4,5},{5,4},{6,7},{7,6},{8,9},{9,8},{10,11... | collective-permute-start | bytes 3932168 | tf_op jit(solution)/shard_map/ppermute | solution.py:82
  61.5 49.6 %copy-start.20 = (f32[1024,80]{0,1:T(8,128)}, f32[1024,80]{0,1:T(8,128)S(1)}, u32[]{:S(2)}) copy-start(f32[1024,80]{0,1:T(8,128)S(1)} %get-tuple-element.107) | copy-start | bytes 983044
  96.5 33.9 %copy-start.6 = (bf16[320,1280]{0,1:T(8,128)(2,1)}, bf16[320,1280]{0,1:T(8,128)(2,1)S(1)}, u32[]{:S(2)}) copy-start(bf16[320,1280]{0,1:T(8,128)(2,1)S(1)} %all_gather.13) | copy-start | bytes 2457604
  122.1 8.3 collective-permute-start.7
  132.8 17.1 %collective-permute-start.8 = (bf16[256,1280]{1,0:T(8,128)(2,1)S(1)}, bf16[256,1280]{1,0:T(8,128)(2,1)}, u32[]{:S(2)}, u32[]{:S(2)}) collective-permute-start(bf16[256,1280]{1,0:T(8,128)(2,1)S(1)} %slice.833), channel_id=1, source_target_pairs={{0,2},{1,3},{2,0},{3,1},{4,6},{5,7},{6,4},{7,5},{8,10},{9,11},{10,... | collective-permute-start | bytes 1966088 | tf_op jit(solution)/shard_map/ppermute | solution.py:96
  134.1 651.9 %reduce-scatter.7.cloned.1.call-start = ((), (), s32[]{:S(2)}) async-start(), calls=%async_computation.8 | async-start | bytes 1105920 | tf_op jit(solution)/shard_map/reduce_scatter | solution.py:432
  152.4 16.2 %collective-permute-start.9 = (bf16[256,1280]{1,0:T(8,128)(2,1)S(1)}, bf16[256,1280]{1,0:T(8,128)(2,1)S(1)}, u32[]{:S(2)}, u32[]{:S(2)}) collective-permute-start(bf16[256,1280]{1,0:T(8,128)(2,1)S(1)} %add_convert_fusion.2), channel_id=1, source_target_pairs={{0,2},{1,3},{2,0},{3,1},{4,6},{5,7},{6,4},{7,5},{8,10},{9,11},{10,... | collective-permute-start | bytes 1966088 | tf_op jit(solution)/shard_map/ppermute | solution.py:82
  155.0 97.6 %copy-start.115 = (f32[1,256]{1,0:T(1,128)}, f32[1,256]{1,0:T(1,128)S(1)}, u32[]{:S(2)}) copy-start(f32[1,256]{1,0:T(1,128)S(1)} %get-tuple-element.115) | copy-start | bytes 3076
  169.8 20.9 %collective-permute-start.10 = (bf16[512,1280]{1,0:T(8,128)(2,1)}, bf16[512,1280]{1,0:T(8,128)(2,1)}, u32[]{:S(2)}, u32[]{:S(2)}) collective-permute-start(bf16[512,1280]{1,0:T(8,128)(2,1)} %pad_maximum_fusion.9), channel_id=1, source_target_pairs={{0,1},{1,0},{2,3},{3,2},{4,5},{5,4},{6,7},{7,6},{8,9},{9,8},{10,11... | collective-permute-start | bytes 3932168 | tf_op jit(solution)/shard_map/ppermute | solution.py:82
  170.9 17.5 %collective-permute-start.21 = (bf16[256,1280]{1,0:T(8,128)(2,1)}, bf16[256,1280]{1,0:T(8,128)(2,1)}, u32[]{:S(2)}, u32[]{:S(2)}) collective-permute-start(bf16[256,1280]{1,0:T(8,128)(2,1)} %fusion.240), channel_id=1, source_target_pairs={{0,2},{1,3},{2,0},{3,1},{4,6},{5,7},{6,4},{7,5},{8,10},{9,11},{10,... | collective-permute-start | bytes 1966088 | tf_op jit(solution)/shard_map/ppermute | solution.py:82
  190.8 9.7 %collective-permute-start.22 = (bf16[512,1280]{1,0:T(8,128)(2,1)}, bf16[512,1280]{1,0:T(8,128)(2,1)}, u32[]{:S(2)}, u32[]{:S(2)}) collective-permute-start(bf16[512,1280]{1,0:T(8,128)(2,1)} %pad_maximum_fusion.13), channel_id=1, source_target_pairs={{0,1},{1,0},{2,3},{3,2},{4,5},{5,4},{6,7},{7,6},{8,9},{9,8},{10,11... | collective-permute-start | bytes 3932168 | tf_op jit(solution)/shard_map/ppermute | solution.py:82
  212.2 5.1 collective-permute-start.23
  216.9 6.0 collective-permute-start.11
  221.6 17.9 %collective-permute-start.24 = (bf16[256,1280]{1,0:T(8,128)(2,1)}, bf16[256,1280]{1,0:T(8,128)(2,1)}, u32[]{:S(2)}, u32[]{:S(2)}) collective-permute-start(bf16[256,1280]{1,0:T(8,128)(2,1)} %slice.829), channel_id=1, source_target_pairs={{0,2},{1,3},{2,0},{3,1},{4,6},{5,7},{6,4},{7,5},{8,10},{9,11},{10,... | collective-permute-start | bytes 1966088 | tf_op jit(solution)/shard_map/ppermute | solution.py:96
  222.8 29.7 %copy-start.97 = (f32[1280]{0:T(1024)}, f32[1280]{0:T(1024)S(1)}, u32[]{:S(2)}) copy-start(f32[1280]{0:T(1024)S(1)} %reshape.947) | copy-start | bytes 15364
  227.8 24.8 %copy-start.25 = (bf16[2,256,1280]{2,1,0:T(8,128)(2,1)S(1)}, bf16[2,256,1280]{2,1,0:T(8,128)(2,1)}, u32[]{:S(2)}) copy-start(bf16[2,256,1280]{2,1,0:T(8,128)(2,1)} %param.38) | copy-start | bytes 3932164
  227.9 24.7 %collective-permute-start.12 = (bf16[256,1280]{1,0:T(8,128)(2,1)S(1)}, bf16[256,1280]{1,0:T(8,128)(2,1)S(1)}, u32[]{:S(2)}, u32[]{:S(2)}) collective-permute-start(bf16[256,1280]{1,0:T(8,128)(2,1)S(1)} %slice.832), channel_id=1, source_target_pairs={{0,2},{1,3},{2,0},{3,1},{4,6},{5,7},{6,4},{7,5},{8,10},{9,11},{10,... | collective-permute-start | bytes 1966088 | tf_op jit(solution)/shard_map/ppermute | solution.py:96
  257.5 16.0 %collective-permute-start.25 = (bf16[256,1280]{1,0:T(8,128)(2,1)S(1)}, bf16[256,1280]{1,0:T(8,128)(2,1)S(1)}, u32[]{:S(2)}, u32[]{:S(2)}) collective-permute-start(bf16[256,1280]{1,0:T(8,128)(2,1)S(1)} %convert_element_type.479), channel_id=1, source_target_pairs={{0,2},{1,3},{2,0},{3,1},{4,6},{5,7},{6,4},{7,5},{8,10},{9,11},{10,... | collective-permute-start | bytes 1966088 | tf_op jit(solution)/shard_map/ppermute | solution.py:82
  273.5 3.1 collective-permute-start.26
  402.7 3.1 collective-permute-start.27
  407.5 16.8 %collective-permute-start.28 = (bf16[256,1280]{1,0:T(8,128)(2,1)S(1)}, bf16[256,1280]{1,0:T(8,128)(2,1)S(1)}, u32[]{:S(2)}, u32[]{:S(2)}) collective-permute-start(bf16[256,1280]{1,0:T(8,128)(2,1)S(1)} %slice.828), channel_id=1, source_target_pairs={{0,2},{1,3},{2,0},{3,1},{4,6},{5,7},{6,4},{7,5},{8,10},{9,11},{10,... | collective-permute-start | bytes 1966088 | tf_op jit(solution)/shard_map/ppermute | solution.py:96
  427.5 16.0 %collective-permute-start.13 = (bf16[256,1280]{1,0:T(8,128)(2,1)S(1)}, bf16[256,1280]{1,0:T(8,128)(2,1)S(1)}, u32[]{:S(2)}, u32[]{:S(2)}) collective-permute-start(bf16[256,1280]{1,0:T(8,128)(2,1)S(1)} %get-tuple-element.75), channel_id=1, source_target_pairs={{0,2},{1,3},{2,0},{3,1},{4,6},{5,7},{6,4},{7,5},{8,10},{9,11},{10,... | collective-permute-start | bytes 1966088 | tf_op jit(solution)/shard_map/ppermute | solution.py:82
  443.6 3.1 collective-permute-start.14
  460.2 8.2 collective-permute-start.15
  469.4 17.1 %collective-permute-start.16 = (bf16[256,1280]{1,0:T(8,128)(2,1)S(1)}, bf16[256,1280]{1,0:T(8,128)(2,1)S(1)}, u32[]{:S(2)}, u32[]{:S(2)}) collective-permute-start(bf16[256,1280]{1,0:T(8,128)(2,1)S(1)} %slice.831), channel_id=1, source_target_pairs={{0,2},{1,3},{2,0},{3,1},{4,6},{5,7},{6,4},{7,5},{8,10},{9,11},{10,... | collective-permute-start | bytes 1966088 | tf_op jit(solution)/shard_map/ppermute | solution.py:96
  487.5 33.7 %copy-start.45 = (bf16[256,1280]{1,0:T(8,128)(2,1)}, bf16[256,1280]{1,0:T(8,128)(2,1)S(1)}, u32[]{:S(2)}) copy-start(bf16[256,1280]{1,0:T(8,128)(2,1)S(1)} %add_convert_fusion.1) | copy-start | bytes 1966084
  487.5 33.8 %copy-start.123 = (bf16[1280,1280]{1,0:T(8,128)(2,1)S(1)}, bf16[1280,1280]{1,0:T(8,128)(2,1)}, u32[]{:S(2)}) copy-start(bf16[1280,1280]{1,0:T(8,128)(2,1)} %all-gather.6.cloned.1.call-done) | copy-start | bytes 9830404
  487.5 16.2 %collective-permute-start.17 = (bf16[256,1280]{1,0:T(8,128)(2,1)S(1)}, bf16[256,1280]{1,0:T(8,128)(2,1)S(1)}, u32[]{:S(2)}, u32[]{:S(2)}) collective-permute-start(bf16[256,1280]{1,0:T(8,128)(2,1)S(1)} %add_convert_fusion.1), channel_id=1, source_target_pairs={{0,2},{1,3},{2,0},{3,1},{4,6},{5,7},{6,4},{7,5},{8,10},{9,11},{10,... | collective-permute-start | bytes 1966088 | tf_op jit(solution)/shard_map/ppermute | solution.py:82
  503.8 17.4 %collective-permute-start.18 = (bf16[512,1280]{1,0:T(8,128)(2,1)S(1)}, bf16[512,1280]{1,0:T(8,128)(2,1)S(1)}, u32[]{:S(2)}, u32[]{:S(2)}) collective-permute-start(bf16[512,1280]{1,0:T(8,128)(2,1)S(1)} %pad_maximum_fusion.11), channel_id=1, source_target_pairs={{0,1},{1,0},{2,3},{3,2},{4,5},{5,4},{6,7},{7,6},{8,9},{9,8},{10,11... | collective-permute-start | bytes 3932168 | tf_op jit(solution)/shard_map/ppermute | solution.py:82
  503.9 17.1 %collective-permute-start.29 = (bf16[256,1280]{1,0:T(8,128)(2,1)S(1)}, bf16[256,1280]{1,0:T(8,128)(2,1)S(1)}, u32[]{:S(2)}, u32[]{:S(2)}) collective-permute-start(bf16[256,1280]{1,0:T(8,128)(2,1)S(1)} %copy-done.53), channel_id=1, source_target_pairs={{0,2},{1,3},{2,0},{3,1},{4,6},{5,7},{6,4},{7,5},{8,10},{9,11},{10,... | collective-permute-start | bytes 1966088 | tf_op jit(solution)/shard_map/ppermute | solution.py:82
  521.1 4.2 collective-permute-start.30
  534.3 3.2 collective-permute-start.31
  536.7 4.5 collective-permute-start.19
  539.5 17.7 %collective-permute-start.32 = (bf16[256,1280]{1,0:T(8,128)(2,1)S(1)}, bf16[256,1280]{1,0:T(8,128)(2,1)S(1)}, u32[]{:S(2)}, u32[]{:S(2)}) collective-permute-start(bf16[256,1280]{1,0:T(8,128)(2,1)S(1)} %slice.827), channel_id=1, source_target_pairs={{0,2},{1,3},{2,0},{3,1},{4,6},{5,7},{6,4},{7,5},{8,10},{9,11},{10,... | collective-permute-start | bytes 1966088 | tf_op jit(solution)/shard_map/ppermute | solution.py:96
  543.2 27.4 %copy-start.26 = (bf16[2,256,1280]{2,1,0:T(8,128)(2,1)S(1)}, bf16[2,256,1280]{2,1,0:T(8,128)(2,1)}, u32[]{:S(2)}) copy-start(bf16[2,256,1280]{2,1,0:T(8,128)(2,1)} %param.38) | copy-start | bytes 3932164
  543.2 27.4 %copy-start.98 = (f32[1280]{0:T(1024)S(1)}, f32[1280]{0:T(1024)}, u32[]{:S(2)}) copy-start(f32[1280]{0:T(1024)} %copy-done.97) | copy-start | bytes 15364
  543.2 27.4 %copy-start.116 = (f32[1,256]{1,0:T(1,128)S(1)}, f32[1,256]{1,0:T(1,128)}, u32[]{:S(2)}) copy-start(f32[1,256]{1,0:T(1,128)} %copy-done.115) | copy-start | bytes 3076
  543.3 27.3 %collective-permute-start.20 = (bf16[256,1280]{1,0:T(8,128)(2,1)S(1)}, bf16[256,1280]{1,0:T(8,128)(2,1)S(1)}, u32[]{:S(2)}, u32[]{:S(2)}) collective-permute-start(bf16[256,1280]{1,0:T(8,128)(2,1)S(1)} %slice.830), channel_id=1, source_target_pairs={{0,2},{1,3},{2,0},{3,1},{4,6},{5,7},{6,4},{7,5},{8,10},{9,11},{10,... | collective-permute-start | bytes 1966088 | tf_op jit(solution)/shard_map/ppermute | solution.py:96
  572.4 16.2 %collective-permute-start.33 = (bf16[256,1280]{1,0:T(8,128)(2,1)S(1)}, bf16[256,1280]{1,0:T(8,128)(2,1)S(1)}, u32[]{:S(2)}, u32[]{:S(2)}) collective-permute-start(bf16[256,1280]{1,0:T(8,128)(2,1)S(1)} %convert_element_type.497), channel_id=1, source_target_pairs={{0,2},{1,3},{2,0},{3,1},{4,6},{5,7},{6,4},{7,5},{8,10},{9,11},{10,... | collective-permute-start | bytes 1966088 | tf_op jit(solution)/shard_map/ppermute | solution.py:82
  588.8 3.1 collective-permute-start.34
  596.2 205.9 %reduce-scatter.11.cloned.1.call-start = ((), (), s32[]{:S(2)}) async-start(), calls=%async_computation.10 | async-start | bytes 3686400 | tf_op jit(solution)/shard_map/reduce_scatter | solution.py:426
  610.3 207.2 %reduce-scatter.9.cloned.1.call-start = ((), (), s32[]{:S(2)}) async-start(), calls=%async_computation.9 | async-start | bytes 3686400 | tf_op jit(solution)/shard_map/reduce_scatter | solution.py:429
  624.8 268.5 %reduce-scatter.5.cloned.1.call-start = ((), (), s32[]{:S(2)}) async-start(), calls=%async_computation.7 | async-start | bytes 3317760 | tf_op jit(solution)/shard_map/reduce_scatter | solution.py:435
  676.5 23.8 %copy-start.58 = (f32[1024,80]{0,1:T(8,128)S(1)}, f32[1024,80]{0,1:T(8,128)}, u32[]{:S(2)}) copy-start(f32[1024,80]{0,1:T(8,128)} %copy-done.57) | copy-start | bytes 983044
  676.6 23.8 %copy-start.78 = (f32[4,80,512]{2,1,0:T(8,128)S(1)}, f32[4,80,512]{2,1,0:T(8,128)}, u32[]{:S(2)}) copy-start(f32[4,80,512]{2,1,0:T(8,128)} %fusion.45) | copy-start | bytes 1966084
  741.0 13.7 %collective-permute-start.35 = (bf16[512,1280]{1,0:T(8,128)(2,1)}, bf16[512,1280]{1,0:T(8,128)(2,1)}, u32[]{:S(2)}, u32[]{:S(2)}) collective-permute-start(bf16[512,1280]{1,0:T(8,128)(2,1)} %convolution_convert_fusion), channel_id=1, source_target_pairs={{0,1},{1,0},{2,3},{3,2},{4,5},{5,4},{6,7},{7,6},{8,9},{9,8},{10,11... | collective-permute-start | bytes 3932168 | tf_op jit(solution)/shard_map/ppermute | solution.py:91
  760.2 17.1 %collective-permute-start.36 = (bf16[256,1280]{1,0:T(8,128)(2,1)S(1)}, bf16[256,1280]{1,0:T(8,128)(2,1)S(1)}, u32[]{:S(2)}, u32[]{:S(2)}) collective-permute-start(bf16[256,1280]{1,0:T(8,128)(2,1)S(1)} %slice.826), channel_id=1, source_target_pairs={{0,2},{1,3},{2,0},{3,1},{4,6},{5,7},{6,4},{7,5},{8,10},{9,11},{10,... | collective-permute-start | bytes 1966088 | tf_op jit(solution)/shard_map/ppermute | solution.py:96
  781.2 6.4 collective-permute-start.37
  787.7 3.8 collective-permute-start.38
  791.5 3.7 collective-permute-start.39
  795.3 3.7 collective-permute-start.40
  799.0 1.3 collective-permute-start.41
  (128 other events, 1127.8 us)
Sparse Core Ops, SparseCore 0:
  10.2 63.4 all-gather.3
  75.9 62.2 all-gather.5
  140.4 60.1 all-gather.7
  596.3 63.6 reduce-scatter.6
  663.4 75.4 reduce-scatter.10
  742.4 75.0 reduce-scatter.8
  821.0 72.1 reduce-scatter.4

commit v2 on v1

--- a/solution.py
+++ b/solution.py
@@ -4,13 +4,14 @@
 import jax
 import jax.numpy as jnp
 from jax import lax
+from jax.experimental import pallas as pl
+from jax.experimental.pallas import tpu as pltpu
 from jax.sharding import PartitionSpec as P
 
 HEAD_DIM = 80
 
 
 norm_eps = 1e-06
-masked_score = -1e30
 
 
 def layer_norm(values, gain_row, shift_row):
@@ -26,41 +27,6 @@
     mean_one = jnp.mean(grad_hat, axis=-1, keepdims=True)
     mean_two = jnp.mean(grad_hat * normed, axis=-1, keepdims=True)
     return scaled * (grad_hat - mean_one - normed * mean_two)
-
-
-def rotate_half(values):
-    middle = values.shape[-1] // 2
-    return jnp.concatenate([-values[..., middle:], values[..., :middle]], axis=-1)
-
-
-def rotary_tables(row_places, col_places, head_size):
-    quarter = head_size // 4
-    freqs_base = 10000.0 ** (-(4.0 * jnp.arange(quarter, dtype=jnp.float32)) / head_size)
-    angles = jnp.concatenate(
-        [
-            row_places.astype(jnp.float32)[:, None] * freqs_base[None, :],
-            col_places.astype(jnp.float32)[:, None] * freqs_base[None, :],
-        ],
-        axis=-1,
-    )
-    angles = jnp.concatenate([angles, angles], axis=-1)[:, None, :]
-    return (jnp.cos(angles), jnp.sin(angles))
-
-
-def rotary_apply(values, cos_table, sin_table):
-    return values * cos_table + rotate_half(values) * sin_table
-
-
-def rotary_back(grad_rows, cos_table, sin_table):
-    return grad_rows * cos_table - rotate_half(grad_rows * sin_table)
-
-
-def key_window(row_ids, row_lengths):
-    slot_ids = jnp.arange(row_lengths.shape[0], dtype=jnp.int32)
-    offsets = jnp.cumsum(row_lengths) - row_lengths
-    picked = (row_ids[:, None] == slot_ids[None, :]).astype(jnp.int32)
-    window_start = jnp.sum(picked * offsets[None, :], axis=1)
-    return (window_start, window_start + jnp.sum(picked * row_lengths[None, :], axis=1))
 
 
 def flip_pairs(count, step):
@@ -142,102 +108,223 @@
     return parts
 
 
-def block_scores(query_block, keys_bf, start_block, stop_block, key_places, score_scale):
-    scores = (
-        jnp.einsum("qhd,khd->hqk", query_block, keys_bf, preferred_element_type=jnp.float32)
-        * score_scale
-    )
-    inside = (key_places[None, :] >= start_block[:, None]) & (
-        key_places[None, :] < stop_block[:, None]
-    )
-    return jnp.where(inside[None], scores, masked_score)
-
-
-def attend_forward(linear, tables, score_scale):
-    cos_table, sin_table, start_all, stop_all, key_places = tables
+LANES = 128
+away = 2.0 ** 66
+log2_e = 1.4426950408889634
+
+
+def fold_lanes(values):
+    quarter_turn = HEAD_DIM // 2
+    return (
+        pltpu.roll(values, LANES - quarter_turn, 1),
+        pltpu.roll(values, quarter_turn, 1),
+    )
+
+
+def nt_product(left, right):
+    return lax.dot_general(
+        left, right, (((1,), (1,)), ((), ())), preferred_element_type=jnp.float32
+    )
+
+
+def attend_forward_kernel(
+    block_rows,
+    score_scale,
+    lin_q_ref,
+    lin_k_ref,
+    lin_v_ref,
+    cos_ref,
+    sin_low_ref,
+    sin_high_ref,
+    query_slot_ref,
+    key_slot_ref,
+    query_ref,
+    key_ref,
+    value_ref,
+    context_ref,
+    stat_ref,
+):
+    row_length = lin_q_ref.shape[0]
+
+    def turned(values, slots):
+        low, high = fold_lanes(values)
+        return (
+            values * cos_ref[...] + low * sin_low_ref[...] + high * sin_high_ref[...] + slots
+        ).astype(jnp.bfloat16)
+
+    query_ref[...] = turned(lin_q_ref[...], query_slot_ref[...])
+    keys = turned(lin_k_ref[...], key_slot_ref[...])
+    key_ref[...] = keys
+    values = lin_v_ref[...].astype(jnp.bfloat16)
+    value_ref[...] = values
+    values_t = values.T
+    for lower in range(0, row_length, block_rows):
+        block = slice(lower, lower + block_rows)
+        scores = nt_product(keys, query_ref[block, :])
+        highest = jnp.max(scores, axis=0, keepdims=True)
+        shifted = jnp.exp2((scores - highest) * (score_scale * log2_e))
+        inverse = 1.0 / jnp.sum(shifted, axis=0, keepdims=True)
+        attend = (shifted * inverse).astype(jnp.bfloat16)
+        context_t = jnp.dot(values_t, attend, preferred_element_type=jnp.float32)
+        context_ref[block, :] = context_t.T.astype(jnp.bfloat16)
+        stat_ref[0, 0:1, block] = highest
+        stat_ref[0, 1:2, block] = inverse
+
+
+def attend_back_kernel(
+    block_rows,
+    score_scale,
+    query_ref,
+    key_ref,
+    value_ref,
+    grad_ref,
+    stat_ref,
+    cos_ref,
+    sin_low_ref,
+    sin_high_ref,
+    grad_linear_ref,
+    key_sum_ref,
+    value_sum_ref,
+):
+    row_length = query_ref.shape[0]
+    head = pl.program_id(0)
+    heads = pl.num_programs(0)
+    keys = key_ref[...]
+    keys_t = keys.T
+    values = value_ref[...]
+
+    def columns(kind):
+        return pl.ds(pl.multiple_of((kind * heads + head) * LANES, LANES), LANES)
+
+    def unturned(grads, block):
+        low, high = fold_lanes(grads)
+        return (
+            grads * cos_ref[block, :] - low * sin_low_ref[block, :] - high * sin_high_ref[block, :]
+        ).astype(jnp.bfloat16)
+
+    for lower in range(0, row_length, block_rows):
+        block = slice(lower, lower + block_rows)
+        queries = query_ref[block, :]
+        grads = grad_ref[block, :]
+        scores = nt_product(keys, queries)
+        attend = (
+            jnp.exp2((scores - stat_ref[0, 0:1, block]) * (score_scale * log2_e))
+            * stat_ref[0, 1:2, block]
+        )
+        value_part = jnp.dot(
+            attend.astype(jnp.bfloat16), grads, preferred_element_type=jnp.float32
+        )
+        attend_grad = nt_product(values, grads)
+        inner = jnp.sum(attend * attend_grad, axis=0, keepdims=True)
+        score_grad = (attend * (attend_grad - inner) * score_scale).astype(jnp.bfloat16)
+        key_part = jnp.dot(score_grad, queries, preferred_element_type=jnp.float32)
+        query_t = jnp.dot(keys_t, score_grad, preferred_element_type=jnp.float32)
+        grad_linear_ref[block, columns(0)] = unturned(query_t.T, block)
+        if lower == 0:
+            key_sum_ref[...] = key_part
+            value_sum_ref[...] = value_part
+        else:
+            key_sum_ref[...] += key_part
+            value_sum_ref[...] += value_part
+    grad_linear_ref[:, columns(1)] = unturned(key_sum_ref[...], slice(None))
+    grad_linear_ref[:, columns(2)] = value_sum_ref[...].astype(jnp.bfloat16)
+
+
+def head_spec(row_length, shift):
+    return pl.BlockSpec((row_length, LANES), lambda head: (0, head + shift))
+
+
+def whole_spec(shape):
+    return pl.BlockSpec(shape, lambda head: (0,) * len(shape))
+
+
+def attend_forward(linear, tables, head_count, score_scale):
     row_length = linear.shape[0]
-    block_rows = min(512, row_length)
-    queries_bf = rotary_apply(linear[:, 0], cos_table, sin_table).astype(jnp.bfloat16)
-    keys_bf = rotary_apply(linear[:, 1], cos_table, sin_table).astype(jnp.bfloat16)
-    values_bf = linear[:, 2].astype(jnp.bfloat16)
-    context_blocks = []
-    logsum_blocks = []
-    for lower in range(0, row_length, block_rows):
-        upper = lower + block_rows
-        scores = block_scores(
-            queries_bf[lower:upper],
-            keys_bf,
-            start_all[lower:upper],
-            stop_all[lower:upper],
-            key_places,
-            score_scale,
-        )
-        highest = jnp.max(scores, axis=-1, keepdims=True)
-        shifted = jnp.exp(scores - highest)
-        totals = jnp.sum(shifted, axis=-1, keepdims=True)
-        attend = shifted / totals
-        logsum_blocks.append(highest + jnp.log(totals))
-        context_blocks.append(
-            jnp.einsum(
-                "hqk,khd->qhd",
-                attend.astype(jnp.bfloat16),
-                values_bf,
-                preferred_element_type=jnp.float32,
-            )
-        )
-    context_bf = jnp.concatenate(context_blocks, axis=0).astype(jnp.bfloat16)
-    return context_bf, (queries_bf, keys_bf, values_bf, logsum_blocks)
-
-
-def attend_back(kept, grad_context, tables, score_scale):
-    cos_table, sin_table, start_all, stop_all, key_places = tables
-    queries_bf, keys_bf, values_bf, logsum_blocks = kept
-    row_length, head_count, _ = queries_bf.shape
-    block_rows = min(512, row_length)
-    grad_keys = jnp.zeros((row_length, head_count, HEAD_DIM), jnp.float32)
-    grad_values = jnp.zeros((row_length, head_count, HEAD_DIM), jnp.float32)
-    query_grad_blocks = []
-    for block_index, lower in enumerate(range(0, row_length, block_rows)):
-        upper = lower + block_rows
-        scores = block_scores(
-            queries_bf[lower:upper],
-            keys_bf,
-            start_all[lower:upper],
-            stop_all[lower:upper],
-            key_places,
-            score_scale,
-        )
-        attend = jnp.exp(scores - logsum_blocks[block_index])
-        context_grad = grad_context[lower:upper]
-        grad_values = grad_values + jnp.einsum(
-            "hqk,qhd->khd",
-            attend.astype(jnp.bfloat16),
-            context_grad,
-            preferred_element_type=jnp.float32,
-        )
-        attend_grad = jnp.einsum(
-            "qhd,khd->hqk", context_grad, values_bf, preferred_element_type=jnp.float32
-        )
-        row_inner = jnp.sum(attend * attend_grad, axis=-1, keepdims=True)
-        score_grad = (attend * (attend_grad - row_inner) * score_scale).astype(jnp.bfloat16)
-        query_grad_blocks.append(
-            jnp.einsum("hqk,khd->qhd", score_grad, keys_bf, preferred_element_type=jnp.float32)
-        )
-        grad_keys = grad_keys + jnp.einsum(
-            "hqk,qhd->khd",
-            score_grad,
-            queries_bf[lower:upper],
-            preferred_element_type=jnp.float32,
-        )
-    grad_queries = jnp.concatenate(query_grad_blocks, axis=0)
-    return jnp.stack(
+    block_rows = min(256, row_length)
+    cos_table, sin_low, sin_high, query_slots, key_slots = tables
+    table = whole_spec((row_length, LANES))
+    headed = jax.ShapeDtypeStruct((row_length, head_count * LANES), jnp.bfloat16)
+    area = head_count * row_length * row_length
+    queries, keys, values, context, stats = pl.pallas_call(
+        functools.partial(attend_forward_kernel, block_rows, score_scale),
+        grid=(head_count,),
+        in_specs=[
+            head_spec(row_length, 0),
+            head_spec(row_length, head_count),
+            head_spec(row_length, 2 * head_count),
+        ]
+        + [table] * 5,
+        out_specs=[head_spec(row_length, 0)] * 4
+        + [pl.BlockSpec((1, 2, row_length), lambda head: (head, 0, 0))],
+        out_shape=[headed] * 4
+        + [jax.ShapeDtypeStruct((head_count, 2, row_length), jnp.float32)],
+        cost_estimate=pl.CostEstimate(
+            flops=4 * area * LANES,
+            bytes_accessed=20 * row_length * head_count * LANES,
+            transcendentals=area,
+        ),
+        name="attend_forward",
+    )(linear, linear, linear, cos_table, sin_low, sin_high, query_slots, key_slots)
+    return context, (queries, keys, values, stats)
+
+
+def attend_back(kept, grad_context, tables, head_count, score_scale):
+    queries, keys, values, stats = kept
+    row_length = queries.shape[0]
+    block_rows = min(256, row_length)
+    cos_table, sin_low, sin_high = tables[:3]
+    table = whole_spec((row_length, LANES))
+    area = head_count * row_length * row_length
+    return pl.pallas_call(
+        functools.partial(attend_back_kernel, block_rows, score_scale),
+        grid=(head_count,),
+        in_specs=[head_spec(row_length, 0)] * 4
+        + [pl.BlockSpec((1, 2, row_length), lambda head: (head, 0, 0))]
+        + [table] * 3,
+        out_specs=whole_spec((row_length, 3 * head_count * LANES)),
+        out_shape=jax.ShapeDtypeStruct((row_length, 3 * head_count * LANES), jnp.bfloat16),
+        scratch_shapes=[
+            pltpu.VMEM((row_length, LANES), jnp.float32),
+            pltpu.VMEM((row_length, LANES), jnp.float32),
+        ],
+        cost_estimate=pl.CostEstimate(
+            flops=10 * area * LANES,
+            bytes_accessed=14 * row_length * head_count * LANES,
+            transcendentals=area,
+        ),
+        name="attend_back",
+    )(queries, keys, values, grad_context, stats, cos_table, sin_low, sin_high)
+
+
+def head_tables(row_places, col_places, row_ids, row_lengths, key_places):
+    quarter = HEAD_DIM // 4
+    half = HEAD_DIM // 2
+    slots = row_lengths.shape[0]
+    freqs_base = 10000.0 ** (-(4.0 * jnp.arange(quarter, dtype=jnp.float32)) / HEAD_DIM)
+    angles = jnp.concatenate(
         [
-            rotary_back(grad_queries, cos_table, sin_table),
-            rotary_back(grad_keys, cos_table, sin_table),
-            grad_values,
+            row_places.astype(jnp.float32)[:, None] * freqs_base[None, :],
+            col_places.astype(jnp.float32)[:, None] * freqs_base[None, :],
         ],
-        axis=1,
-    ).astype(jnp.bfloat16)
+        axis=-1,
+    )
+    cosine = jnp.cos(angles)
+    sine = jnp.sin(angles)
+
+    def lanes(values, before):
+        return jnp.pad(values, ((0, 0), (before, LANES - before - values.shape[1])))
+
+    same = row_ids[:, None] == jnp.arange(slots, dtype=jnp.int32)[None, :]
+    filled = (key_places < jnp.sum(row_lengths))[:, None]
+    low_sine = lanes(sine, 0)
+    high_sine = lanes(sine, half)
+    return (
+        lanes(jnp.concatenate([cosine, cosine], axis=-1), 0),
+        -low_sine,
+        high_sine,
+        lanes(same.astype(jnp.float32), HEAD_DIM),
+        lanes(jnp.where(same & filled, 0.0, -away), HEAD_DIM),
+    )
 
 
 def dot_nn(left, right):
@@ -315,26 +402,35 @@
     w_proj = lax.all_gather(proj_weight, "dp", axis=1, tiled=True)
     w_fc1 = lax.all_gather(fc1_weight, "dp", axis=0, tiled=True)
     w_fc2 = lax.all_gather(fc2_weight, "dp", axis=1, tiled=True)
-    w_qkv_flat = w_qkv.reshape(model_width, 3 * head_width)
+    spare = LANES - HEAD_DIM
+    w_qkv_flat = jnp.pad(
+        w_qkv.reshape(model_width, 3 * head_count, HEAD_DIM), ((0, 0), (0, 0), (0, spare))
+    ).reshape(model_width, 3 * head_count * LANES)
+    w_proj = jnp.pad(
+        w_proj.reshape(head_count, HEAD_DIM, model_width), ((0, 0), (0, spare), (0, 0))
+    ).reshape(head_count * LANES, model_width)
+    qkv_local_shift = jnp.pad(
+        qkv_local_shift.reshape(3 * head_count, HEAD_DIM), ((0, 0), (0, spare))
+    ).reshape(3 * head_count * LANES)
 
     outputs = []
     saved = []
     for row in range(row_total):
         tokens_row = tokens[row].astype(f32)
-        start_all, stop_all = key_window(near_order(pic_ids[row]), lengths[row])
-        cos_table, sin_table = rotary_tables(
-            near_order(pos_rows[row]), near_order(pos_cols[row]), HEAD_DIM
-        )
-        tables = (cos_table, sin_table, start_all, stop_all, all_places)
+        tables = head_tables(
+            near_order(pos_rows[row]),
+            near_order(pos_cols[row]),
+            near_order(pic_ids[row]),
+            lengths[row],
+            all_places,
+        )
         pad_rows = (local_places < jnp.sum(lengths[row])).astype(f32)[:, None]
         grad_out = pad_rows * cotangent[row].astype(f32)
         grad_branch = gather_rows(grad_out.astype(bf16), tensor_count)
         normed_one, hat_one, scale_one = layer_norm(tokens_row, gain_one, shift_one)
         lowered_one = gather_rows(normed_one.astype(bf16), tensor_count)
         linear = dot_nn(lowered_one, w_qkv_flat) + qkv_local_shift
-        linear = linear.reshape(row_length, 3, head_count, HEAD_DIM)
-        context_bf, kept = attend_forward(linear, tables, score_scale)
-        context_bf = context_bf.reshape(row_length, head_width)
+        context_bf, kept = attend_forward(linear, tables, head_count, score_scale)
         attn_branch = scatter_product(
             lambda part: dot_nn(part, w_proj), context_bf, tensor_count
         )
@@ -394,12 +490,8 @@
         grad_hidden = grad_out + norm_back(grad_normed_two, hat_two, scale_two, gain_two)
         grad_attn = gather_rows(grad_hidden.astype(bf16), tensor_count)
         micro_proj = dot_tn(context_bf, grad_attn)
-        grad_context = (
-            dot_nt(grad_attn, w_proj).astype(bf16).reshape(row_length, head_count, HEAD_DIM)
-        )
-        grad_linear = attend_back(kept, grad_context, tables, score_scale).reshape(
-            row_length, 3 * head_width
-        )
+        grad_context = dot_nt(grad_attn, w_proj).astype(bf16)
+        grad_linear = attend_back(kept, grad_context, tables, head_count, score_scale)
         micro_qkv = dot_tn(lowered_one, grad_linear)
         grad_normed_one = scatter_product(
             lambda part: dot_nt(part, w_qkv_flat), grad_linear, tensor_count
@@ -430,17 +522,25 @@
         totals[10].astype(bf16), "dp", scatter_dimension=0, tiled=True
     ).astype(f32)
     grad_proj = lax.psum_scatter(
-        totals[9].astype(bf16), "dp", scatter_dimension=1, tiled=True
+        totals[9]
+        .reshape(head_count, LANES, model_width)[:, :HEAD_DIM]
+        .reshape(head_width, model_width)
+        .astype(bf16),
+        "dp",
+        scatter_dimension=1, tiled=True
     ).astype(f32)
     grad_qkv = lax.psum_scatter(
-        totals[8].reshape(model_width, 3, head_width).astype(bf16),
+        totals[8]
+        .reshape(model_width, 3 * head_count, LANES)[:, :, :HEAD_DIM]
+        .reshape(model_width, 3, head_width)
+        .astype(bf16),
         "dp",
         scatter_dimension=0,
         tiled=True,
     ).astype(f32)
     qkv_full_grad = lax.dynamic_update_slice_in_dim(
         jnp.zeros((3, model_width), f32),
-        totals[2].reshape(3, head_width),
+        totals[2].reshape(3 * head_count, LANES)[:, :HEAD_DIM].reshape(3, head_width),
         tensor_place * head_width,
         1,
     ).reshape(3 * model_width)

time: 907 us -> 841 us (0.927)
  matrix products: 353 us -> 138 us
  Pallas kernels: 0 us -> 76 us
  waiting for transfers between devices: 336 us -> 392 us
  local copies, waits for them, and re-layouts: 50.6 us -> 72.1 us
    dot_general x24 -> x0, matrix products: 238 us -> none  [the longest x4 98 us: attend_back(): jnp.einsum('hqk,qhd->khd', score_grad, queries_bf[lower:upper], preferred...]
    reduce_scatter x1, waiting for transfers between devices: 0.01 us -> 76.8 us  [on_device(): lax.psum_scatter(totals[11].astype(bf16), 'dp', scatter_dimension=1, tile...]
    pallas_call x0 -> x4, Pallas kernels: none -> 76 us  [the longest x2 41.7 us: attend_back(): pl.pallas_call(functools.partial(attend_back_kernel, block_rows, score_sc...]
    reduce_scatter x2 -> x0, waiting for transfers between devices: 73.9 us -> none  [the longest x1 73.9 us: on_device(): lax.psum_scatter(totals[8].reshape(model_width, 3, head_width).astype(bf1...]
    unnamed x7 -> x9, waiting for transfers between devices: 0.78 us -> 72.4 us
    reduce_scatter x1, waiting for transfers between devices: 13.5 us -> 1.36 us  [on_device(): lax.psum_scatter(totals[10].astype(bf16), 'dp', scatter_dimension=0, tile...]
    ppermute x16, waiting for transfers between devices: 122 us -> 110 us  [gather_rows(): received = lax.ppermute(rows, 'tensor', flip_pairs(count, step))]
    dot_general x12, matrix products: 37.3 us -> 47.7 us  [dot_nt(): jnp.einsum('sk,nk->sn', left, right, preferred_element_type=jnp.float32)]
  transfers between devices with their start and end apart: 49 -> 49, of which waited for: 31 -> 32; matrix products, arithmetic and copies ran while one was open for 31% -> 24% of each run, Pallas kernels for 0% -> 5%
where the time goes in v2:
time: 841 us; the launch traced here: 837 us
  waiting for transfers between devices  392 us (47%)
  matrix products  138 us (16%)
  Pallas kernels  76 us (9%)
  local copies, waits for them, and re-layouts  72.1 us (9%)
  other arithmetic  62.3 us (7%)
  blocking collectives  40.6 us (5%)
  starting transfers between devices  39.3 us (5%)
  between operations  16.3 us (2%)
    ppermute x16, waiting for transfers between devices, gather_rows(): received = lax.ppermute(rows, 'tensor', flip_pairs(count, step))  110 us
    ppermute x8, waiting for transfers between devices, scatter_product(): lax.ppermute(total[half:].astype(jnp.bfloat16), 'tensor', flip_pairs(coun...  107 us
    reduce_scatter x1, waiting for transfers between devices, on_device(): lax.psum_scatter(totals[11].astype(bf16), 'dp', scatter_dimension=1, tile...  76.8 us
    unnamed x9, waiting for transfers between devices  72.4 us
    dot_general x12, matrix products, dot_nt(): jnp.einsum('sk,nk->sn', left, right, preferred_element_type=jnp.float32)  47.7 us
    dot_general x12, matrix products, dot_nn(): return jnp.dot(left, right, preferred_element_type=jnp.float32)  47.2 us
    dot_general x8, matrix products, dot_tn(): jnp.einsum('sm,sn->mn', left, right, preferred_element_type=jnp.float32)  43.5 us
    pallas_call x2, Pallas kernels, attend_back(): pl.pallas_call(functools.partial(attend_back_kernel, block_rows, score_sc...  41.7 us
  transfers between devices with their start and end apart: 49, of which 32 were waited for; matrix products, arithmetic and copies ran while one was open for 24% of the time, Pallas kernels for 5%

profile of v2, /device:TPU:0, one launch (start us, length us, event | category | flops | bytes accessed | tf_op | source)
XLA Modules:
  0.0 837.1 jit_solution(2596828197450667762)
XLA Ops:
  8.0 5.4 concatenate.74
  24.6 2.6 collective-permute-start.1
  37.6 2.9 collective-permute-start.4
  46.4 40.6 %all_gather.13 = bf16[320,1280]{0,1:T(8,128)(2,1)S(1)} all-gather(bf16[320,160]{0,1:T(8,128)(2,1)S(1)} %copy-done.59), channel_id=1, replica_groups=mesh['dp'=8,'tensor'=4] {'dp'}, dimensions={1}, use_global_device_ids=true | all-gather | bytes 921600 | tf_op jit(solution)/shard_map/all_gather | solution.py:402
  94.3 2.7 sin.6
  103.4 5.3 copy.48
  110.9 8.6 %convolution_add_fusion.4.lin_q_ref.lin_k_ref.lin_v_ref = f32[1024,1536]{1,0:T(8,128)} fusion(bf16[1280,1536]{0,1:T(8,128)(2,1)S(1)} %bitcast.199, f32[1536]{0:T(1024)S(1)} %pad_bitcast_fusion, bf16[512,1280]{1,0:T(8,128)(2,1)} %collective-permute-done.6, bf16[256,1280]{1,0:T(8,128)(2,1)S(1)} %copy-done.38, bf16[256,1280]{1,0:T(8,128)(2,1)S(1)} %copy-done.28), kind=kOutput, calls=%fused_computation.24 | convolution fusion | flops 4035969024 | bytes 12851200 | tf_op jit(solution)/shard_map/dot_general | solution.py:331
  119.5 17.1 %attend_forward.2 = (bf16[1024,512]{1,0:T(8,128)(2,1)}, bf16[1024,512]{1,0:T(8,128)(2,1)}, bf16[1024,512]{1,0:T(8,128)(2,1)}, bf16[1024,512]{1,0:T(8,128)(2,1)}, f32[4,2,1024]{2,1,0:T(2,128)}) custom-call(f32[1024,1536]{1,0:T(8,128)} %convolution_add_fusion.4.lin_q_ref.lin_k_ref.lin_v_ref, f32[1024,1536]{1,0:T(8,128)} %convolution_add_fusion.4.lin_q_ref.lin_k_ref.lin_v_ref, ...), custom_call_target="tpu_custom_call" | custom-call | flops 2147483648 | bytes 10485760 | tf_op jit(solution)/shard_map/attend_forward/pallas_call | solution.py:248
  139.1 2.7 collective-permute-done.7
  145.9 15.4 %collective-permute-done.8 = bf16[256,1280]{1,0:T(8,128)(2,1)S(1)} collective-permute-done((bf16[256,1280]{1,0:T(8,128)(2,1)S(1)}, bf16[256,1280]{1,0:T(8,128)(2,1)S(1)}, u32[]{:S(2)}, u32[]{:S(2)}) %collective-permute-start.8) | collective-permute-done | bytes 655392 | tf_op jit(solution)/shard_map/ppermute | solution.py:62
  166.1 13.7 %collective-permute-done.9 = bf16[256,1280]{1,0:T(8,128)(2,1)S(1)} collective-permute-done((bf16[256,1280]{1,0:T(8,128)(2,1)S(1)}, bf16[256,1280]{1,0:T(8,128)(2,1)S(1)}, u32[]{:S(2)}, u32[]{:S(2)}) %collective-permute-start.9) | collective-permute-done | bytes 655392 | tf_op jit(solution)/shard_map/ppermute | solution.py:48
  183.3 16.1 %collective-permute-done.21 = bf16[256,1280]{1,0:T(8,128)(2,1)} collective-permute-done((bf16[256,1280]{1,0:T(8,128)(2,1)}, bf16[256,1280]{1,0:T(8,128)(2,1)}, u32[]{:S(2)}, u32[]{:S(2)}) %collective-permute-start.21) | collective-permute-done | bytes 655392 | tf_op jit(solution)/shard_map/ppermute | solution.py:48
  199.5 2.4 pad_maximum_fusion.13
  201.9 9.5 %multiply_convert_fusion.3 = (bf16[1024,1280]{1,0:T(8,128)(2,1)}, f32[1024,1280]{1,0:T(8,128)}) fusion(f32[1280]{0:T(1024)S(1)} %dynamic_slice.7, bf16[1280,1280]{1,0:T(8,128)(2,1)} %all-gather.6.cloned.1.call-done, bf16[512,1280]{1,0:T(8,128)(2,1)} %collective-permute-done.10, bf16[256,1280]{1,0:T(8,128)(2,1)} %copy-done.40, ...), kind=kOutput, calls=%fused_computation.21 | convolution fusion | flops 3372482560 | bytes 13767680 | tf_op jit(solution)/shard_map/dot_general | solution.py:331
  212.4 9.6 %convert_reduce_fusion.3 = (f32[1280]{0:T(1024)}, bf16[1024,1280]{1,0:T(8,128)(2,1)S(1)}) fusion(f32[1024,1280]{1,0:T(8,128)} %get-tuple-element.158, f32[1280]{0:T(1024)S(1)} %dynamic_slice.7, bf16[1280,1280]{0,1:T(8,128)(2,1)} %all-gather.8.cloned.1.call-done, bf16[512,1280]{1,0:T(8,128)(2,1)} %collective-permute-done.22, ...), kind=kOutput, calls=%fused_computation.16 | convolution fusion | flops 3380345600 | bytes 13772800 | tf_op jit(solution)/shard_map/sk,nk->sn/dot_general | solution.py:335
  225.7 3.0 convolution_convert_fusion.6
  234.6 5.1 convert_add_fusion.6
  240.5 10.4 %collective-permute-done.24 = bf16[256,1280]{1,0:T(8,128)(2,1)S(1)} collective-permute-done((bf16[256,1280]{1,0:T(8,128)(2,1)}, bf16[256,1280]{1,0:T(8,128)(2,1)S(1)}, u32[]{:S(2)}, u32[]{:S(2)}) %collective-permute-start.24) | collective-permute-done | bytes 655392 | tf_op jit(solution)/shard_map/ppermute | solution.py:62
  252.0 12.4 %collective-permute-done.12 = bf16[256,1280]{1,0:T(8,128)(2,1)S(1)} collective-permute-done((bf16[256,1280]{1,0:T(8,128)(2,1)S(1)}, bf16[256,1280]{1,0:T(8,128)(2,1)S(1)}, u32[]{:S(2)}, u32[]{:S(2)}) %collective-permute-start.12) | collective-permute-done | bytes 655392 | tf_op jit(solution)/shard_map/ppermute | solution.py:62
  264.5 2.9 fusion.78
  270.0 14.8 %collective-permute-done.25 = bf16[256,1280]{1,0:T(8,128)(2,1)S(1)} collective-permute-done((bf16[256,1280]{1,0:T(8,128)(2,1)S(1)}, bf16[256,1280]{1,0:T(8,128)(2,1)S(1)}, u32[]{:S(2)}, u32[]{:S(2)}) %collective-permute-start.25) | collective-permute-done | bytes 655392 | tf_op jit(solution)/shard_map/ppermute | solution.py:48
  285.0 3.0 collective-permute-done.26
  288.0 2.5 convolution_convert_fusion.9.grad_ref
  290.5 20.9 %attend_back.2 = bf16[1024,1536]{1,0:T(8,128)(2,1)} custom-call(bf16[1024,512]{1,0:T(8,128)(2,1)} %get-tuple-element.27.query_ref, bf16[1024,512]{1,0:T(8,128)(2,1)} %get-tuple-element.28.key_ref, bf16[1024,512]{1,0:T(8,128)(2,1)} %get-tuple-element.29.value_ref, bf16[1024,512]{1,0:T(8,128)(2,1)} %convolution_convert_fusion.9.grad_ref, ...), custom_call_target="tpu_custom_call" | custom-call | flops 5368709120 | bytes 7340032 | tf_op jit(solution)/shard_map/attend_back/pallas_call | solution.py:278
  311.4 4.9 convolution_convert_fusion.2
  316.6 2.9 collective-permute-done.27
  323.3 15.3 %collective-permute-done.28 = bf16[256,1280]{1,0:T(8,128)(2,1)S(1)} collective-permute-done((bf16[256,1280]{1,0:T(8,128)(2,1)S(1)}, bf16[256,1280]{1,0:T(8,128)(2,1)S(1)}, u32[]{:S(2)}, u32[]{:S(2)}) %collective-permute-start.28) | collective-permute-done | bytes 655392 | tf_op jit(solution)/shard_map/ppermute | solution.py:62
  343.3 14.5 %collective-permute-done.13 = bf16[256,1280]{1,0:T(8,128)(2,1)S(1)} collective-permute-done((bf16[256,1280]{1,0:T(8,128)(2,1)S(1)}, bf16[256,1280]{1,0:T(8,128)(2,1)S(1)}, u32[]{:S(2)}, u32[]{:S(2)}) %collective-permute-start.13) | collective-permute-done | bytes 655392 | tf_op jit(solution)/shard_map/ppermute | solution.py:48
  363.9 3.5 sin.7
  368.7 2.4 select_maximum_fusion.cos_ref
  372.4 2.3 fusion.141
  374.8 7.6 convolution_add_fusion.3.lin_q_ref.lin_k_ref.lin_v_ref
  382.4 17.3 %attend_forward.3 = (bf16[1024,512]{1,0:T(8,128)(2,1)}, bf16[1024,512]{1,0:T(8,128)(2,1)}, bf16[1024,512]{1,0:T(8,128)(2,1)}, bf16[1024,512]{1,0:T(8,128)(2,1)}, f32[4,2,1024]{2,1,0:T(2,128)}) custom-call(f32[1024,1536]{1,0:T(8,128)} %convolution_add_fusion.3.lin_q_ref.lin_k_ref.lin_v_ref, f32[1024,1536]{1,0:T(8,128)} %convolution_add_fusion.3.lin_q_ref.lin_k_ref.lin_v_ref, ...), custom_call_target="tpu_custom_call" | custom-call | flops 2147483648 | bytes 10485760 | tf_op jit(solution)/shard_map/attend_forward/pallas_call | solution.py:248
  402.2 2.7 collective-permute-done.15
  407.4 15.5 %collective-permute-done.16 = bf16[256,1280]{1,0:T(8,128)(2,1)S(1)} collective-permute-done((bf16[256,1280]{1,0:T(8,128)(2,1)S(1)}, bf16[256,1280]{1,0:T(8,128)(2,1)S(1)}, u32[]{:S(2)}, u32[]{:S(2)}) %collective-permute-start.16) | collective-permute-done | bytes 655392 | tf_op jit(solution)/shard_map/ppermute | solution.py:62
  425.5 14.7 %collective-permute-done.17 = bf16[256,1280]{1,0:T(8,128)(2,1)S(1)} collective-permute-done((bf16[256,1280]{1,0:T(8,128)(2,1)S(1)}, bf16[256,1280]{1,0:T(8,128)(2,1)S(1)}, u32[]{:S(2)}, u32[]{:S(2)}) %collective-permute-start.17) | collective-permute-done | bytes 655392 | tf_op jit(solution)/shard_map/ppermute | solution.py:48
  441.9 15.6 %collective-permute-done.29 = bf16[256,1280]{1,0:T(8,128)(2,1)S(1)} collective-permute-done((bf16[256,1280]{1,0:T(8,128)(2,1)S(1)}, bf16[256,1280]{1,0:T(8,128)(2,1)S(1)}, u32[]{:S(2)}, u32[]{:S(2)}) %collective-permute-start.29) | collective-permute-done | bytes 655392 | tf_op jit(solution)/shard_map/ppermute | solution.py:48
  457.7 4.0 multiply_convert_fusion.2
  461.7 7.0 convert_reduce_fusion.2
  480.0 13.5 %collective-permute-done.32 = bf16[256,1280]{1,0:T(8,128)(2,1)S(1)} collective-permute-done((bf16[256,1280]{1,0:T(8,128)(2,1)S(1)}, bf16[256,1280]{1,0:T(8,128)(2,1)S(1)}, u32[]{:S(2)}, u32[]{:S(2)}) %collective-permute-start.32) | collective-permute-done | bytes 655392 | tf_op jit(solution)/shard_map/ppermute | solution.py:62
  494.2 12.8 %collective-permute-done.20 = bf16[256,1280]{1,0:T(8,128)(2,1)S(1)} collective-permute-done((bf16[256,1280]{1,0:T(8,128)(2,1)S(1)}, bf16[256,1280]{1,0:T(8,128)(2,1)S(1)}, u32[]{:S(2)}, u32[]{:S(2)}) %collective-permute-start.20) | collective-permute-done | bytes 655392 | tf_op jit(solution)/shard_map/ppermute | solution.py:62
  510.3 14.7 %collective-permute-done.33 = bf16[256,1280]{1,0:T(8,128)(2,1)S(1)} collective-permute-done((bf16[256,1280]{1,0:T(8,128)(2,1)S(1)}, bf16[256,1280]{1,0:T(8,128)(2,1)S(1)}, u32[]{:S(2)}, u32[]{:S(2)}) %collective-permute-start.33) | collective-permute-done | bytes 655392 | tf_op jit(solution)/shard_map/ppermute | solution.py:48
  525.2 3.0 collective-permute-done.34
  533.9 6.4 fusion.86
  540.3 7.2 fusion.1
  548.7 6.0 fusion.85
  554.7 7.6 fusion.2
  563.2 2.5 convert_reduce_fusion.1
  565.7 2.5 convolution_convert_fusion.8.grad_ref
  568.2 20.8 %attend_back.3 = bf16[1024,1536]{1,0:T(8,128)(2,1)} custom-call(bf16[1024,512]{1,0:T(8,128)(2,1)} %get-tuple-element.31.query_ref, bf16[1024,512]{1,0:T(8,128)(2,1)} %get-tuple-element.32.key_ref, bf16[1024,512]{1,0:T(8,128)(2,1)} %get-tuple-element.33.value_ref, bf16[1024,512]{1,0:T(8,128)(2,1)} %convolution_convert_fusion.8.grad_ref, ...), custom_call_target="tpu_custom_call" | custom-call | flops 5368709120 | bytes 7340032 | tf_op jit(solution)/shard_map/attend_back/pallas_call | solution.py:278
  589.1 6.0 convolution_convert_fusion
  595.3 5.8 fusion.88
  601.1 7.4 fusion
  608.5 6.6 copy.56
  615.0 3.3 slice.373
  618.3 4.5 copy.63
  622.9 5.4 convert_add_fusion
  631.8 2.4 convert_reduce_fusion
  634.7 12.0 %collective-permute-done.36 = bf16[256,1280]{1,0:T(8,128)(2,1)S(1)} collective-permute-done((bf16[256,1280]{1,0:T(8,128)(2,1)S(1)}, bf16[256,1280]{1,0:T(8,128)(2,1)S(1)}, u32[]{:S(2)}, u32[]{:S(2)}) %collective-permute-start.36) | collective-permute-done | bytes 655392 | tf_op jit(solution)/shard_map/ppermute | solution.py:62
  653.3 2.3 pad_maximum_fusion.12
  658.9 4.7 collective-permute-done.38
  664.2 3.1 collective-permute-done.39
  677.4 76.8 %reduce-scatter.11.cloned.1.call-done = bf16[1280,160]{0,1:T(8,128)(2,1)} async-done(((bf16[1280,1280]{0,1:T(8,128)(2,1)}), bf16[1280,160]{0,1:T(8,128)(2,1)}) %reduce-scatter.11.cloned.1.call-update) | async-done | bytes 409616 | tf_op jit(solution)/shard_map/reduce_scatter | solution.py:518
  756.1 71.6 %reduce-scatter.13.cloned.1.call-done = bf16[160,960]{1,0:T(8,128)(2,1)} async-done(((bf16[1280,960]{1,0:T(8,128)(2,1)}), bf16[160,960]{1,0:T(8,128)(2,1)}) %reduce-scatter.13.cloned.1.call-update) | async-done | bytes 307216
  (497 shorter events, 152.3 us)
Async XLA Ops:
  7.2 96.2 %all-gather.4.cloned.1.call-start = ((), (), s32[]{:S(2)}) async-start(), calls=%async_computation.4 | async-start | bytes 3317760 | tf_op jit(solution)/shard_map/all_gather | solution.py:401
  7.9 194.0 %all-gather.6.cloned.1.call-start = ((), (), s32[]{:S(2)}) async-start(), calls=%async_computation.5 | async-start | bytes 3686400 | tf_op jit(solution)/shard_map/all_gather | solution.py:403
  13.5 32.9 %copy-start.59 = (bf16[320,160]{0,1:T(8,128)(2,1)S(1)}, bf16[320,160]{0,1:T(8,128)(2,1)}, u32[]{:S(2)}) copy-start(bf16[320,160]{0,1:T(8,128)(2,1)} %param.30) | copy-start | bytes 307204
  13.5 11.1 %collective-permute-start = (bf16[32,520]{1,0:T(8,128)(2,1)S(1)}, bf16[32,520]{1,0:T(8,128)(2,1)S(1)}, u32[]{:S(2)}, u32[]{:S(2)}) collective-permute-start(bf16[32,520]{1,0:T(8,128)(2,1)S(1)} %dynamic_update_slice.11), channel_id=1, source_target_pairs={{0,1},{1,0},{2,3},{3,2},{4,5},{5,4},{6,7},{7,6},{8,9},{9,8},{10,11... | collective-permute-start | bytes 99848 | tf_op jit(solution)/shard_map/ppermute | solution.py:80
  14.1 198.3 %all-gather.8.cloned.1.call-start = ((), (), s32[]{:S(2)}) async-start(), calls=%async_computation.6 | async-start | bytes 3686400 | tf_op jit(solution)/shard_map/all_gather | solution.py:404
  24.6 4.8 collective-permute-start.1
  29.4 4.1 collective-permute-start.2
  31.3 56.9 %copy-start.79 = (f32[256]{0:T(256)}, f32[256]{0:T(256)S(1)}, u32[]{:S(2)}) copy-start(f32[256]{0:T(256)S(1)} %broadcast_multiply_fusion.15) | copy-start | bytes 3076
  33.5 4.1 collective-permute-start.3
  37.6 5.1 collective-permute-start.4
  40.5 47.7 %copy-start.84 = (f32[256]{0:T(256)}, f32[256]{0:T(256)S(1)}, u32[]{:S(2)}) copy-start(f32[256]{0:T(256)S(1)} %add_rsqrt_fusion.3) | copy-start | bytes 3076
  43.5 44.7 %copy-start.64 = (f32[1280]{0:T(1024)}, f32[1280]{0:T(1024)S(1)}, u32[]{:S(2)}) copy-start(f32[1280]{0:T(1024)S(1)} %reshape.351) | copy-start | bytes 15364
  43.6 296.5 %copy-start.54 = (f32[1280]{0:T(1024)}, f32[1280]{0:T(1024)S(1)}, u32[]{:S(2)}) copy-start(f32[1280]{0:T(1024)S(1)} %reshape.350) | copy-start | bytes 15364
  43.9 44.4 %copy-start.27 = (bf16[256,1280]{1,0:T(8,128)(2,1)}, bf16[256,1280]{1,0:T(8,128)(2,1)S(1)}, u32[]{:S(2)}) copy-start(bf16[256,1280]{1,0:T(8,128)(2,1)S(1)} %fusion.40) | copy-start | bytes 1966084
  44.0 43.1 %collective-permute-start.5 = (bf16[256,1280]{1,0:T(8,128)(2,1)S(1)}, bf16[256,1280]{1,0:T(8,128)(2,1)S(1)}, u32[]{:S(2)}, u32[]{:S(2)}) collective-permute-start(bf16[256,1280]{1,0:T(8,128)(2,1)S(1)} %fusion.40), channel_id=1, source_target_pairs={{0,2},{1,3},{2,0},{3,1},{4,6},{5,7},{6,4},{7,5},{8,10},{9,11},{10,... | collective-permute-start | bytes 1966088 | tf_op jit(solution)/shard_map/ppermute | solution.py:48
  88.2 22.6 %collective-permute-start.6 = (bf16[512,1280]{1,0:T(8,128)(2,1)}, bf16[512,1280]{1,0:T(8,128)(2,1)}, u32[]{:S(2)}, u32[]{:S(2)}) collective-permute-start(bf16[512,1280]{1,0:T(8,128)(2,1)} %pad_maximum_fusion.8), channel_id=1, source_target_pairs={{0,1},{1,0},{2,3},{3,2},{4,5},{5,4},{6,7},{7,6},{8,9},{9,8},{10,11... | collective-permute-start | bytes 3932168 | tf_op jit(solution)/shard_map/ppermute | solution.py:48
  90.3 51.5 %copy-start.1 = (bf16[4,128,1280]{2,1,0:T(8,128)(2,1)}, bf16[4,128,1280]{2,1,0:T(8,128)(2,1)S(1)}, u32[]{:S(2)}) copy-start(bf16[4,128,1280]{2,1,0:T(8,128)(2,1)S(1)} %pad.59) | copy-start | bytes 3932164
  138.5 3.2 collective-permute-start.7
  144.2 17.1 %collective-permute-start.8 = (bf16[256,1280]{1,0:T(8,128)(2,1)S(1)}, bf16[256,1280]{1,0:T(8,128)(2,1)S(1)}, u32[]{:S(2)}, u32[]{:S(2)}) collective-permute-start(bf16[256,1280]{1,0:T(8,128)(2,1)S(1)} %slice.566), channel_id=1, source_target_pairs={{0,2},{1,3},{2,0},{3,1},{4,6},{5,7},{6,4},{7,5},{8,10},{9,11},{10,... | collective-permute-start | bytes 1966088 | tf_op jit(solution)/shard_map/ppermute | solution.py:62
  145.3 510.3 %reduce-scatter.15.cloned.1.call-start = ((), (), s32[]{:S(2)}) async-start(), calls=%async_computation.10 | async-start | bytes 1105920
  163.5 38.4 %copy-start.22 = (bf16[256,1280]{1,0:T(8,128)(2,1)}, bf16[256,1280]{1,0:T(8,128)(2,1)S(1)}, u32[]{:S(2)}) copy-start(bf16[256,1280]{1,0:T(8,128)(2,1)S(1)} %add_convert_fusion.1) | copy-start | bytes 1966084
  163.6 16.2 %collective-permute-start.9 = (bf16[256,1280]{1,0:T(8,128)(2,1)S(1)}, bf16[256,1280]{1,0:T(8,128)(2,1)S(1)}, u32[]{:S(2)}, u32[]{:S(2)}) collective-permute-start(bf16[256,1280]{1,0:T(8,128)(2,1)S(1)} %add_convert_fusion.1), channel_id=1, source_target_pairs={{0,2},{1,3},{2,0},{3,1},{4,6},{5,7},{6,4},{7,5},{8,10},{9,11},{10,... | collective-permute-start | bytes 1966088 | tf_op jit(solution)/shard_map/ppermute | solution.py:48
  166.1 98.4 %copy-start.88 = (f32[1,256]{1,0:T(1,128)}, f32[1,256]{1,0:T(1,128)S(1)}, u32[]{:S(2)}) copy-start(f32[1,256]{1,0:T(1,128)S(1)} %get-tuple-element.137) | copy-start | bytes 3076
  181.0 20.9 %collective-permute-start.10 = (bf16[512,1280]{1,0:T(8,128)(2,1)}, bf16[512,1280]{1,0:T(8,128)(2,1)}, u32[]{:S(2)}, u32[]{:S(2)}) collective-permute-start(bf16[512,1280]{1,0:T(8,128)(2,1)} %pad_maximum_fusion.9), channel_id=1, source_target_pairs={{0,1},{1,0},{2,3},{3,2},{4,5},{5,4},{6,7},{7,6},{8,9},{9,8},{10,11... | collective-permute-start | bytes 3932168 | tf_op jit(solution)/shard_map/ppermute | solution.py:48
  182.0 17.5 %collective-permute-start.21 = (bf16[256,1280]{1,0:T(8,128)(2,1)}, bf16[256,1280]{1,0:T(8,128)(2,1)}, u32[]{:S(2)}, u32[]{:S(2)}) collective-permute-start(bf16[256,1280]{1,0:T(8,128)(2,1)} %fusion.83), channel_id=1, source_target_pairs={{0,2},{1,3},{2,0},{3,1},{4,6},{5,7},{6,4},{7,5},{8,10},{9,11},{10,... | collective-permute-start | bytes 1966088 | tf_op jit(solution)/shard_map/ppermute | solution.py:48
  183.3 29.1 %copy-start.93 = (f32[1280]{0:T(1024)}, f32[1280]{0:T(1024)S(1)}, u32[]{:S(2)}) copy-start(f32[1280]{0:T(1024)S(1)} %dynamic_slice.7) | copy-start | bytes 15364
  201.9 9.5 %collective-permute-start.22 = (bf16[512,1280]{1,0:T(8,128)(2,1)}, bf16[512,1280]{1,0:T(8,128)(2,1)}, u32[]{:S(2)}, u32[]{:S(2)}) collective-permute-start(bf16[512,1280]{1,0:T(8,128)(2,1)} %pad_maximum_fusion.13), channel_id=1, source_target_pairs={{0,1},{1,0},{2,3},{3,2},{4,5},{5,4},{6,7},{7,6},{8,9},{9,8},{10,11... | collective-permute-start | bytes 3932168 | tf_op jit(solution)/shard_map/ppermute | solution.py:48
  224.0 4.7 collective-permute-start.23
  228.7 5.9 collective-permute-start.11
  233.0 17.8 %collective-permute-start.24 = (bf16[256,1280]{1,0:T(8,128)(2,1)}, bf16[256,1280]{1,0:T(8,128)(2,1)S(1)}, u32[]{:S(2)}, u32[]{:S(2)}) collective-permute-start(bf16[256,1280]{1,0:T(8,128)(2,1)} %slice.562), channel_id=1, source_target_pairs={{0,2},{1,3},{2,0},{3,1},{4,6},{5,7},{6,4},{7,5},{8,10},{9,11},{10,... | collective-permute-start | bytes 1966088 | tf_op jit(solution)/shard_map/ppermute | solution.py:62
  234.6 29.8 %copy-start.66 = (f32[1280]{0:T(1024)}, f32[1280]{0:T(1024)S(1)}, u32[]{:S(2)}) copy-start(f32[1280]{0:T(1024)S(1)} %reshape.357) | copy-start | bytes 15364
  239.9 24.6 %collective-permute-start.12 = (bf16[256,1280]{1,0:T(8,128)(2,1)S(1)}, bf16[256,1280]{1,0:T(8,128)(2,1)S(1)}, u32[]{:S(2)}, u32[]{:S(2)}) collective-permute-start(bf16[256,1280]{1,0:T(8,128)(2,1)S(1)} %slice.565), channel_id=1, source_target_pairs={{0,2},{1,3},{2,0},{3,1},{4,6},{5,7},{6,4},{7,5},{8,10},{9,11},{10,... | collective-permute-start | bytes 1966088 | tf_op jit(solution)/shard_map/ppermute | solution.py:62
  268.5 16.3 %collective-permute-start.25 = (bf16[256,1280]{1,0:T(8,128)(2,1)S(1)}, bf16[256,1280]{1,0:T(8,128)(2,1)S(1)}, u32[]{:S(2)}, u32[]{:S(2)}) collective-permute-start(bf16[256,1280]{1,0:T(8,128)(2,1)S(1)} %convert_element_type.411), channel_id=1, source_target_pairs={{0,2},{1,3},{2,0},{3,1},{4,6},{5,7},{6,4},{7,5},{8,10},{9,11},{10,... | collective-permute-start | bytes 1966088 | tf_op jit(solution)/shard_map/ppermute | solution.py:48
  284.9 3.1 collective-permute-start.26
  316.4 3.1 collective-permute-start.27
  321.8 16.8 %collective-permute-start.28 = (bf16[256,1280]{1,0:T(8,128)(2,1)S(1)}, bf16[256,1280]{1,0:T(8,128)(2,1)S(1)}, u32[]{:S(2)}, u32[]{:S(2)}) collective-permute-start(bf16[256,1280]{1,0:T(8,128)(2,1)S(1)} %slice.561), channel_id=1, source_target_pairs={{0,2},{1,3},{2,0},{3,1},{4,6},{5,7},{6,4},{7,5},{8,10},{9,11},{10,... | collective-permute-start | bytes 1966088 | tf_op jit(solution)/shard_map/ppermute | solution.py:62
  341.7 33.0 %copy-start.24 = (bf16[256,1280]{1,0:T(8,128)(2,1)}, bf16[256,1280]{1,0:T(8,128)(2,1)S(1)}, u32[]{:S(2)}) copy-start(bf16[256,1280]{1,0:T(8,128)(2,1)S(1)} %get-tuple-element.121) | copy-start | bytes 1966084
  341.8 16.0 %collective-permute-start.13 = (bf16[256,1280]{1,0:T(8,128)(2,1)S(1)}, bf16[256,1280]{1,0:T(8,128)(2,1)S(1)}, u32[]{:S(2)}, u32[]{:S(2)}) collective-permute-start(bf16[256,1280]{1,0:T(8,128)(2,1)S(1)} %get-tuple-element.121), channel_id=1, source_target_pairs={{0,2},{1,3},{2,0},{3,1},{4,6},{5,7},{6,4},{7,5},{8,10},{9,11},{10,... | collective-permute-start | bytes 1966088 | tf_op jit(solution)/shard_map/ppermute | solution.py:48
  359.7 15.0 %collective-permute-start.14 = (bf16[512,1280]{1,0:T(8,128)(2,1)}, bf16[512,1280]{1,0:T(8,128)(2,1)}, u32[]{:S(2)}, u32[]{:S(2)}) collective-permute-start(bf16[512,1280]{1,0:T(8,128)(2,1)} %pad_maximum_fusion.10), channel_id=1, source_target_pairs={{0,1},{1,0},{2,3},{3,2},{4,5},{5,4},{6,7},{7,6},{8,9},{9,8},{10,11... | collective-permute-start | bytes 3932168 | tf_op jit(solution)/shard_map/ppermute | solution.py:48
  401.6 3.2 collective-permute-start.15
  405.8 17.1 %collective-permute-start.16 = (bf16[256,1280]{1,0:T(8,128)(2,1)S(1)}, bf16[256,1280]{1,0:T(8,128)(2,1)S(1)}, u32[]{:S(2)}, u32[]{:S(2)}) collective-permute-start(bf16[256,1280]{1,0:T(8,128)(2,1)S(1)} %slice.564), channel_id=1, source_target_pairs={{0,2},{1,3},{2,0},{3,1},{4,6},{5,7},{6,4},{7,5},{8,10},{9,11},{10,... | collective-permute-start | bytes 1966088 | tf_op jit(solution)/shard_map/ppermute | solution.py:62
  423.9 33.8 %copy-start.26 = (bf16[256,1280]{1,0:T(8,128)(2,1)}, bf16[256,1280]{1,0:T(8,128)(2,1)S(1)}, u32[]{:S(2)}) copy-start(bf16[256,1280]{1,0:T(8,128)(2,1)S(1)} %add_convert_fusion) | copy-start | bytes 1966084
  423.9 33.8 %copy-start.94 = (f32[1280]{0:T(1024)S(1)}, f32[1280]{0:T(1024)}, u32[]{:S(2)}) copy-start(f32[1280]{0:T(1024)} %copy-done.93) | copy-start | bytes 15364
  423.9 33.8 %copy-start.101 = (bf16[1280,1280]{1,0:T(8,128)(2,1)S(1)}, bf16[1280,1280]{1,0:T(8,128)(2,1)}, u32[]{:S(2)}) copy-start(bf16[1280,1280]{1,0:T(8,128)(2,1)} %all-gather.6.cloned.1.call-done) | copy-start | bytes 9830404
  423.9 16.2 %collective-permute-start.17 = (bf16[256,1280]{1,0:T(8,128)(2,1)S(1)}, bf16[256,1280]{1,0:T(8,128)(2,1)S(1)}, u32[]{:S(2)}, u32[]{:S(2)}) collective-permute-start(bf16[256,1280]{1,0:T(8,128)(2,1)S(1)} %add_convert_fusion), channel_id=1, source_target_pairs={{0,2},{1,3},{2,0},{3,1},{4,6},{5,7},{6,4},{7,5},{8,10},{9,11},{10,... | collective-permute-start | bytes 1966088 | tf_op jit(solution)/shard_map/ppermute | solution.py:48
  440.2 17.4 %collective-permute-start.18 = (bf16[512,1280]{1,0:T(8,128)(2,1)S(1)}, bf16[512,1280]{1,0:T(8,128)(2,1)S(1)}, u32[]{:S(2)}, u32[]{:S(2)}) collective-permute-start(bf16[512,1280]{1,0:T(8,128)(2,1)S(1)} %pad_maximum_fusion.11), channel_id=1, source_target_pairs={{0,1},{1,0},{2,3},{3,2},{4,5},{5,4},{6,7},{7,6},{8,9},{9,8},{10,11... | collective-permute-start | bytes 3932168 | tf_op jit(solution)/shard_map/ppermute | solution.py:48
  440.3 17.1 %collective-permute-start.29 = (bf16[256,1280]{1,0:T(8,128)(2,1)S(1)}, bf16[256,1280]{1,0:T(8,128)(2,1)S(1)}, u32[]{:S(2)}, u32[]{:S(2)}) collective-permute-start(bf16[256,1280]{1,0:T(8,128)(2,1)S(1)} %copy-done.34), channel_id=1, source_target_pairs={{0,2},{1,3},{2,0},{3,1},{4,6},{5,7},{6,4},{7,5},{8,10},{9,11},{10,... | collective-permute-start | bytes 1966088 | tf_op jit(solution)/shard_map/ppermute | solution.py:48
  457.6 4.1 collective-permute-start.30
  470.6 3.2 collective-permute-start.31
  473.1 4.3 collective-permute-start.19
  475.8 17.7 %collective-permute-start.32 = (bf16[256,1280]{1,0:T(8,128)(2,1)S(1)}, bf16[256,1280]{1,0:T(8,128)(2,1)S(1)}, u32[]{:S(2)}, u32[]{:S(2)}) collective-permute-start(bf16[256,1280]{1,0:T(8,128)(2,1)S(1)} %slice.560), channel_id=1, source_target_pairs={{0,2},{1,3},{2,0},{3,1},{4,6},{5,7},{6,4},{7,5},{8,10},{9,11},{10,... | collective-permute-start | bytes 1966088 | tf_op jit(solution)/shard_map/ppermute | solution.py:62
  479.4 27.6 %collective-permute-start.20 = (bf16[256,1280]{1,0:T(8,128)(2,1)S(1)}, bf16[256,1280]{1,0:T(8,128)(2,1)S(1)}, u32[]{:S(2)}, u32[]{:S(2)}) collective-permute-start(bf16[256,1280]{1,0:T(8,128)(2,1)S(1)} %slice.563), channel_id=1, source_target_pairs={{0,2},{1,3},{2,0},{3,1},{4,6},{5,7},{6,4},{7,5},{8,10},{9,11},{10,... | collective-permute-start | bytes 1966088 | tf_op jit(solution)/shard_map/ppermute | solution.py:62
  508.8 16.2 %collective-permute-start.33 = (bf16[256,1280]{1,0:T(8,128)(2,1)S(1)}, bf16[256,1280]{1,0:T(8,128)(2,1)S(1)}, u32[]{:S(2)}, u32[]{:S(2)}) collective-permute-start(bf16[256,1280]{1,0:T(8,128)(2,1)S(1)} %convert_element_type.424), channel_id=1, source_target_pairs={{0,2},{1,3},{2,0},{3,1},{4,6},{5,7},{6,4},{7,5},{8,10},{9,11},{10,... | collective-permute-start | bytes 1966088 | tf_op jit(solution)/shard_map/ppermute | solution.py:48
  525.1 3.1 collective-permute-start.34
  533.9 141.6 %reduce-scatter.9.cloned.1.call-start = ((), (), s32[]{:S(2)}) async-start(), calls=%async_computation.7 | async-start | bytes 3686400 | tf_op jit(solution)/shard_map/reduce_scatter | solution.py:521
  547.6 206.6 %reduce-scatter.11.cloned.1.call-start = ((), (), s32[]{:S(2)}) async-start(), calls=%async_computation.8 | async-start | bytes 3686400 | tf_op jit(solution)/shard_map/reduce_scatter | solution.py:518
  562.4 265.4 %reduce-scatter.13.cloned.1.call-start = ((), (), s32[]{:S(2)}) async-start(), calls=%async_computation.9 | async-start | bytes 2949120
  595.1 27.8 %collective-permute-start.35 = (bf16[512,1280]{1,0:T(8,128)(2,1)}, bf16[512,1280]{1,0:T(8,128)(2,1)}, u32[]{:S(2)}, u32[]{:S(2)}) collective-permute-start(bf16[512,1280]{1,0:T(8,128)(2,1)} %convolution_convert_fusion), channel_id=1, source_target_pairs={{0,1},{1,0},{2,3},{3,2},{4,5},{5,4},{6,7},{7,6},{8,9},{9,8},{10,11... | collective-permute-start | bytes 3932168 | tf_op jit(solution)/shard_map/ppermute | solution.py:57
  629.8 16.9 %collective-permute-start.36 = (bf16[256,1280]{1,0:T(8,128)(2,1)S(1)}, bf16[256,1280]{1,0:T(8,128)(2,1)S(1)}, u32[]{:S(2)}, u32[]{:S(2)}) collective-permute-start(bf16[256,1280]{1,0:T(8,128)(2,1)S(1)} %slice.559), channel_id=1, source_target_pairs={{0,2},{1,3},{2,0},{3,1},{4,6},{5,7},{6,4},{7,5},{8,10},{9,11},{10,... | collective-permute-start | bytes 1966088 | tf_op jit(solution)/shard_map/ppermute | solution.py:62
  651.2 6.2 collective-permute-start.37
  658.3 5.3 collective-permute-start.38
  663.6 3.7 collective-permute-start.39
  667.4 3.7 collective-permute-start.40
  671.1 1.3 collective-permute-start.41
  (101 other events, 1030.7 us)
Sparse Core Ops, SparseCore 0:
  10.2 77.2 all-gather.3
  89.7 60.3 all-gather.5
  152.3 60.1 all-gather.7
  534.0 62.8 reduce-scatter.14
  600.3 75.1 reduce-scatter.8
  678.9 75.2 reduce-scatter.10
  757.7 70.0 reduce-scatter.12

commit v3 on v2

--- a/solution.py
+++ b/solution.py
@@ -49,6 +49,10 @@
         rows = jnp.concatenate([rows, received], axis=0)
         step //= 2
     return rows
+
+
+def after(values, earlier):
+    return values if earlier is None else lax.optimization_barrier((values, earlier))[0]
 
 
 def scatter_product(product, rows, count):
@@ -59,12 +63,13 @@
     step = 2
     while step < count:
         half = half // 2
-        received = lax.ppermute(
-            total[half:].astype(jnp.bfloat16), "tensor", flip_pairs(count, step)
-        )
+        sent = total[half:].astype(jnp.bfloat16)
+        received = lax.ppermute(sent, "tensor", flip_pairs(count, step))
+        if step * 2 >= count:
+            received = after(received, (yield sent))
         total = total[:half] + received.astype(jnp.float32)
         step *= 2
-    return total
+    yield total
 
 
 def gather_small(vectors, dp_count, tensor_count):
@@ -109,6 +114,7 @@
 
 
 LANES = 128
+stage_total = 7
 away = 2.0 ** 66
 log2_e = 1.4426950408889634
 
@@ -413,107 +419,111 @@
         qkv_local_shift.reshape(3 * head_count, HEAD_DIM), ((0, 0), (0, spare))
     ).reshape(3 * head_count * LANES)
 
-    outputs = []
-    saved = []
-    for row in range(row_total):
+    def row_stages(row):
         tokens_row = tokens[row].astype(f32)
-        tables = head_tables(
+        tables = all_tables[row]
+        pad_rows = (local_places < jnp.sum(lengths[row])).astype(f32)[:, None]
+        grad_out = pad_rows * cotangent[row].astype(f32)
+        normed_one, hat_one, scale_one = layer_norm(tokens_row, gain_one, shift_one)
+        normed_one = normed_one.astype(bf16)
+        grad_branch = grad_out.astype(bf16)
+        lowered_one = gather_rows(normed_one, tensor_count)
+        earlier = yield normed_one
+
+        lowered_one = after(lowered_one, earlier)
+        linear = dot_nn(lowered_one, w_qkv_flat) + qkv_local_shift
+        context_bf, kept = attend_forward(linear, tables, head_count, score_scale)
+        attn_scatter = scatter_product(
+            lambda part: dot_nn(part, w_proj), context_bf, tensor_count
+        )
+        earlier = yield next(attn_scatter)
+
+        attn_branch = attn_scatter.send(earlier)
+        hidden_row = tokens_row + attn_branch + proj_shift
+        normed_two, hat_two, scale_two = layer_norm(hidden_row, gain_two, shift_two)
+        normed_two = normed_two.astype(bf16)
+        lowered_two = gather_rows(normed_two, tensor_count)
+        grad_branch = gather_rows(after(grad_branch, normed_one), tensor_count)
+        earlier = yield normed_two
+
+        lowered_two = after(lowered_two, earlier)
+        upward = dot_nn(lowered_two, w_fc1) + fc1_local_shift
+        sigmoid_up = jax.nn.sigmoid(1.702 * upward)
+        activated = (upward * sigmoid_up).astype(bf16)
+        grad_up = (
+            dot_nt(grad_branch, w_fc2)
+            * (sigmoid_up + 1.702 * upward * sigmoid_up * (1.0 - sigmoid_up))
+        ).astype(bf16)
+        hidden_scatter = scatter_product(
+            lambda part: dot_nt(part, w_fc1), grad_up, tensor_count
+        )
+        hidden_sent = next(hidden_scatter)
+        branch_scatter = scatter_product(
+            lambda part: dot_nn(part, w_fc2), after(activated, hidden_sent), tensor_count
+        )
+        branch_sent = next(branch_scatter)
+        earlier = yield branch_sent
+
+        grad_normed_two = hidden_scatter.send(earlier)
+        grad_hidden = grad_out + norm_back(grad_normed_two, hat_two, scale_two, gain_two)
+        grad_hidden_bf = grad_hidden.astype(bf16)
+        grad_attn = gather_rows(grad_hidden_bf, tensor_count)
+        earlier = yield grad_hidden_bf
+
+        grad_attn = after(grad_attn, earlier)
+        grad_context = dot_nt(grad_attn, w_proj).astype(bf16)
+        grad_linear = attend_back(kept, grad_context, tables, head_count, score_scale)
+        first_scatter = scatter_product(
+            lambda part: dot_nt(part, w_qkv_flat), grad_linear, tensor_count
+        )
+        earlier = yield next(first_scatter)
+
+        branch = branch_scatter.send(None)
+        output = (pad_rows * (hidden_row + branch + fc2_shift)).astype(bf16)
+        grad_normed_one = first_scatter.send(earlier)
+        token_grad = (
+            grad_hidden + norm_back(grad_normed_one, hat_one, scale_one, gain_one)
+        ).astype(bf16)
+        yield (
+            output,
+            token_grad,
+            (
+                jnp.sum(grad_normed_one * hat_one, axis=0),
+                jnp.sum(grad_normed_one, axis=0),
+                jnp.sum(grad_linear.astype(f32), axis=0),
+                jnp.sum(grad_hidden, axis=0),
+                jnp.sum(grad_normed_two * hat_two, axis=0),
+                jnp.sum(grad_normed_two, axis=0),
+                jnp.sum(grad_up.astype(f32), axis=0),
+                jnp.sum(grad_out, axis=0),
+                dot_tn(lowered_one, grad_linear),
+                dot_tn(context_bf, grad_attn),
+                dot_tn(lowered_two, grad_up),
+                dot_tn(activated, grad_branch),
+            ),
+        )
+
+    all_tables = [
+        head_tables(
             near_order(pos_rows[row]),
             near_order(pos_cols[row]),
             near_order(pic_ids[row]),
             lengths[row],
             all_places,
         )
-        pad_rows = (local_places < jnp.sum(lengths[row])).astype(f32)[:, None]
-        grad_out = pad_rows * cotangent[row].astype(f32)
-        grad_branch = gather_rows(grad_out.astype(bf16), tensor_count)
-        normed_one, hat_one, scale_one = layer_norm(tokens_row, gain_one, shift_one)
-        lowered_one = gather_rows(normed_one.astype(bf16), tensor_count)
-        linear = dot_nn(lowered_one, w_qkv_flat) + qkv_local_shift
-        context_bf, kept = attend_forward(linear, tables, head_count, score_scale)
-        attn_branch = scatter_product(
-            lambda part: dot_nn(part, w_proj), context_bf, tensor_count
-        )
-        hidden_row = tokens_row + attn_branch + proj_shift
-        normed_two, hat_two, scale_two = layer_norm(hidden_row, gain_two, shift_two)
-        lowered_two = gather_rows(normed_two.astype(bf16), tensor_count)
-        upward = dot_nn(lowered_two, w_fc1) + fc1_local_shift
-        activated = (upward * jax.nn.sigmoid(1.702 * upward)).astype(bf16)
-        branch = scatter_product(lambda part: dot_nn(part, w_fc2), activated, tensor_count)
-        outputs.append((pad_rows * (hidden_row + branch + fc2_shift)).astype(bf16))
-        saved.append(
-            (
-                tables,
-                grad_out,
-                grad_branch,
-                hat_one,
-                scale_one,
-                lowered_one,
-                context_bf,
-                kept,
-                hat_two,
-                scale_two,
-                lowered_two,
-                upward,
-                activated,
-            )
-        )
-
-    token_grads = []
-    totals = None
-    for row in range(row_total):
-        (
-            tables,
-            grad_out,
-            grad_branch,
-            hat_one,
-            scale_one,
-            lowered_one,
-            context_bf,
-            kept,
-            hat_two,
-            scale_two,
-            lowered_two,
-            upward,
-            activated,
-        ) = saved[row]
-        micro_fc2 = dot_tn(activated, grad_branch)
-        sigmoid_up = jax.nn.sigmoid(1.702 * upward)
-        grad_up = (
-            dot_nt(grad_branch, w_fc2)
-            * (sigmoid_up + 1.702 * upward * sigmoid_up * (1.0 - sigmoid_up))
-        ).astype(bf16)
-        micro_fc1 = dot_tn(lowered_two, grad_up)
-        grad_normed_two = scatter_product(
-            lambda part: dot_nt(part, w_fc1), grad_up, tensor_count
-        )
-        grad_hidden = grad_out + norm_back(grad_normed_two, hat_two, scale_two, gain_two)
-        grad_attn = gather_rows(grad_hidden.astype(bf16), tensor_count)
-        micro_proj = dot_tn(context_bf, grad_attn)
-        grad_context = dot_nt(grad_attn, w_proj).astype(bf16)
-        grad_linear = attend_back(kept, grad_context, tables, head_count, score_scale)
-        micro_qkv = dot_tn(lowered_one, grad_linear)
-        grad_normed_one = scatter_product(
-            lambda part: dot_nt(part, w_qkv_flat), grad_linear, tensor_count
-        )
-        token_grads.append(
-            (grad_hidden + norm_back(grad_normed_one, hat_one, scale_one, gain_one)).astype(bf16)
-        )
-        parts = (
-            jnp.sum(grad_normed_one * hat_one, axis=0),
-            jnp.sum(grad_normed_one, axis=0),
-            jnp.sum(grad_linear.astype(f32), axis=0),
-            jnp.sum(grad_hidden, axis=0),
-            jnp.sum(grad_normed_two * hat_two, axis=0),
-            jnp.sum(grad_normed_two, axis=0),
-            jnp.sum(grad_up.astype(f32), axis=0),
-            jnp.sum(grad_out, axis=0),
-            micro_qkv,
-            micro_proj,
-            micro_fc1,
-            micro_fc2,
-        )
-        totals = parts if totals is None else tuple(a + b for a, b in zip(totals, parts))
+        for row in range(row_total)
+    ]
+    w_qkv_flat = after(w_qkv_flat, all_tables)
+    stages = [row_stages(row) for row in range(row_total)]
+    tokens_out = [next(stage) for stage in stages]
+    for _ in range(stage_total - 1):
+        for row in range(row_total):
+            tokens_out[row] = stages[row].send(tokens_out[row - 1])
+    outputs = [parts[0] for parts in tokens_out]
+    token_grads = [parts[1] for parts in tokens_out]
+    totals = tokens_out[0][2]
+    for parts in tokens_out[1:]:
+        totals = tuple(first + second for first, second in zip(totals, parts[2]))
 
     grad_fc2 = lax.psum_scatter(
         totals[11].astype(bf16), "dp", scatter_dimension=1, tiled=True

time: 841 us -> 698 us (0.83)
  waiting for transfers between devices: 392 us -> 227 us
  local copies, waits for them, and re-layouts: 72.1 us -> 87.1 us
    reduce_scatter x1 -> x0, waiting for transfers between devices: 76.8 us -> none  [on_device(): lax.psum_scatter(totals[11].astype(bf16), 'dp', scatter_dimension=1, tile...]
    ppermute x16, waiting for transfers between devices: 110 us -> 74.6 us  [gather_rows(): received = lax.ppermute(rows, 'tensor', flip_pairs(count, step))]
    ppermute x8, waiting for transfers between devices: 107 us -> 73.6 us  [scatter_product(): received = lax.ppermute(sent, 'tensor', flip_pairs(count, step))]
    concatenate x8 -> x14, other arithmetic: 6.36 us -> 18.7 us  [gather_rows(): rows = jnp.concatenate([rows, received], axis=0)]
    unnamed x9 -> x10, waiting for transfers between devices: 72.4 us -> 61 us
    unnamed x244 -> x187, local copies, waits for them, and re-layouts: 21.9 us -> 27.7 us
  transfers between devices with their start and end apart: 49 -> 49, of which waited for: 32 -> 25; matrix products, arithmetic and copies ran while one was open for 24% -> 38% of each run, Pallas kernels for 5% -> 11%
where the time goes in v3:
time: 698 us; the launch traced here: 691 us
  waiting for transfers between devices  227 us (33%)
  matrix products  141 us (20%)
  local copies, waits for them, and re-layouts  87.1 us (12%)
  Pallas kernels  75.4 us (11%)
  other arithmetic  70.5 us (10%)
  starting transfers between devices  37.8 us (5%)
  blocking collectives  37.2 us (5%)
  between operations  16.1 us (2%)
    ppermute x16, waiting for transfers between devices, gather_rows(): received = lax.ppermute(rows, 'tensor', flip_pairs(count, step))  74.6 us
    ppermute x8, waiting for transfers between devices, scatter_product(): received = lax.ppermute(sent, 'tensor', flip_pairs(count, step))  73.6 us
    unnamed x10, waiting for transfers between devices  61 us
    dot_general x12, matrix products, dot_nt(): jnp.einsum('sk,nk->sn', left, right, preferred_element_type=jnp.float32)  49 us
    dot_general x12, matrix products, dot_nn(): return jnp.dot(left, right, preferred_element_type=jnp.float32)  46 us
    dot_general x8, matrix products, dot_tn(): jnp.einsum('sm,sn->mn', left, right, preferred_element_type=jnp.float32)  45.6 us
    pallas_call x2, Pallas kernels, attend_back(): pl.pallas_call(functools.partial(attend_back_kernel, block_rows, score_sc...  41.3 us
    all_gather x1, blocking collectives, on_device(): w_proj = lax.all_gather(proj_weight, 'dp', axis=1, tiled=True)  37.2 us
  transfers between devices with their start and end apart: 49, of which 25 were waited for; matrix products, arithmetic and copies ran while one was open for 38% of the time, Pallas kernels for 11%

profile of v3, /device:TPU:0, one launch (start us, length us, event | category | flops | bytes accessed | tf_op | source)
XLA Modules:
  0.0 691.3 jit_solution(11362947717482953362)
XLA Ops:
  8.0 5.4 concatenate.74
  30.9 2.6 collective-permute-start.1
  44.0 3.9 collective-permute-start.4
  49.1 3.2 collective-permute-done.4
  53.9 2.7 fusion.40
  64.0 37.2 %all_gather.13 = bf16[320,1280]{0,1:T(8,128)(2,1)S(1)} all-gather(bf16[320,160]{0,1:T(8,128)(2,1)} %param.30), channel_id=1, replica_groups=mesh['dp'=8,'tensor'=4] {'dp'}, dimensions={1}, use_global_device_ids=true | all-gather | bytes 921600 | tf_op jit(solution)/shard_map/all_gather | solution.py:408
  101.2 2.5 pad_maximum_fusion.6
  111.5 3.5 sin.7
  116.9 3.5 sin.6
  124.6 3.2 fusion.117
  130.8 3.3 pad_maximum_fusion
  134.1 5.3 copy.54
  143.6 6.2 convolution_add_fusion.4.lin_q_ref.lin_k_ref.lin_v_ref
  149.8 17.0 %attend_forward.2 = (bf16[1024,512]{1,0:T(8,128)(2,1)}, bf16[1024,512]{1,0:T(8,128)(2,1)}, bf16[1024,512]{1,0:T(8,128)(2,1)}, bf16[1024,512]{1,0:T(8,128)(2,1)}, f32[4,2,1024]{2,1,0:T(2,128)}) custom-call(f32[1024,1536]{1,0:T(8,128)} %convolution_add_fusion.4.lin_q_ref.lin_k_ref.lin_v_ref, f32[1024,1536]{1,0:T(8,128)} %convolution_add_fusion.4.lin_q_ref.lin_k_ref.lin_v_ref, ...), custom_call_target="tpu_custom_call" | custom-call | flops 2147483648 | bytes 10485760 | tf_op jit(solution)/shard_map/attend_forward/pallas_call | solution.py:254
  175.1 6.6 convolution_add_fusion.3.lin_q_ref.lin_k_ref.lin_v_ref
  181.7 17.1 %attend_forward.3 = (bf16[1024,512]{1,0:T(8,128)(2,1)}, bf16[1024,512]{1,0:T(8,128)(2,1)}, bf16[1024,512]{1,0:T(8,128)(2,1)}, bf16[1024,512]{1,0:T(8,128)(2,1)}, f32[4,2,1024]{2,1,0:T(2,128)}) custom-call(f32[1024,1536]{1,0:T(8,128)} %convolution_add_fusion.3.lin_q_ref.lin_k_ref.lin_v_ref, f32[1024,1536]{1,0:T(8,128)} %convolution_add_fusion.3.lin_q_ref.lin_k_ref.lin_v_ref, ...), custom_call_target="tpu_custom_call" | custom-call | flops 2147483648 | bytes 10485760 | tf_op jit(solution)/shard_map/attend_forward/pallas_call | solution.py:254
  198.8 3.0 convolution_convert_fusion.6
  204.6 15.0 %collective-permute-done.15 = bf16[256,1280]{1,0:T(8,128)(2,1)} collective-permute-done((bf16[256,1280]{1,0:T(8,128)(2,1)S(1)}, bf16[256,1280]{1,0:T(8,128)(2,1)}, u32[]{:S(2)}, u32[]{:S(2)}) %collective-permute-start.15) | collective-permute-done | bytes 655392 | tf_op jit(solution)/shard_map/ppermute | solution.py:48
  225.3 8.4 %collective-permute-done.8 = bf16[256,1280]{1,0:T(8,128)(2,1)} collective-permute-done((bf16[256,1280]{1,0:T(8,128)(2,1)}, bf16[256,1280]{1,0:T(8,128)(2,1)}, u32[]{:S(2)}, u32[]{:S(2)}) %collective-permute-start.8) | collective-permute-done | bytes 655392 | tf_op jit(solution)/shard_map/ppermute | solution.py:67
  239.0 8.6 %collective-permute-done.14 = bf16[256,1280]{1,0:T(8,128)(2,1)S(1)} collective-permute-done((bf16[256,1280]{1,0:T(8,128)(2,1)S(1)}, bf16[256,1280]{1,0:T(8,128)(2,1)S(1)}, u32[]{:S(2)}, u32[]{:S(2)}) %collective-permute-start.14) | collective-permute-done | bytes 655392 | tf_op jit(solution)/shard_map/ppermute | solution.py:67
  247.6 13.5 %collective-permute-done.12 = bf16[256,1280]{1,0:T(8,128)(2,1)S(1)} collective-permute-done((bf16[256,1280]{1,0:T(8,128)(2,1)S(1)}, bf16[256,1280]{1,0:T(8,128)(2,1)S(1)}, u32[]{:S(2)}, u32[]{:S(2)}) %collective-permute-start.12) | collective-permute-done | bytes 655392 | tf_op jit(solution)/shard_map/ppermute | solution.py:48
  265.9 9.7 %multiply_convert_fusion.3 = (bf16[1024,1280]{1,0:T(8,128)(2,1)}, f32[1024,1280]{1,0:T(8,128)}) fusion(f32[1280]{0:T(1024)S(1)} %dynamic_slice.7, bf16[1024,1280]{1,0:T(8,128)(2,1)} %pad_maximum_fusion.2, bf16[1280,1280]{1,0:T(8,128)(2,1)} %all-gather.6.cloned.1.call-done), kind=kOutput, calls=%fused_computation.21 | convolution fusion | flops 3364618240 | bytes 13767680 | tf_op jit(solution)/shard_map/dot_general | solution.py:337
  275.7 9.0 %convert_reduce_fusion.3 = (f32[1280]{0:T(1024)S(1)}, bf16[1024,1280]{1,0:T(8,128)(2,1)S(1)}) fusion(f32[1024,1280]{1,0:T(8,128)} %get-tuple-element.208, f32[1280]{0:T(1024)S(1)} %dynamic_slice.7, bf16[1024,1280]{1,0:T(8,128)(2,1)} %copy-done.58, bf16[1280,1280]{0,1:T(8,128)(2,1)} %all-gather.8.cloned.1.call-done), kind=kOutput, calls=%fused_computation.16 | convolution fusion | flops 3372481280 | bytes 13772800 | tf_op jit(solution)/shard_map/sk,nk->sn/dot_general | solution.py:341
  288.9 15.6 %collective-permute-done.22 = bf16[256,1280]{1,0:T(8,128)(2,1)S(1)} collective-permute-done((bf16[256,1280]{1,0:T(8,128)(2,1)S(1)}, bf16[256,1280]{1,0:T(8,128)(2,1)S(1)}, u32[]{:S(2)}, u32[]{:S(2)}) %collective-permute-start.22) | collective-permute-done | bytes 655392 | tf_op jit(solution)/shard_map/ppermute | solution.py:48
  304.6 13.3 %collective-permute-done.20 = bf16[256,1280]{1,0:T(8,128)(2,1)S(1)} collective-permute-done((bf16[256,1280]{1,0:T(8,128)(2,1)S(1)}, bf16[256,1280]{1,0:T(8,128)(2,1)S(1)}, u32[]{:S(2)}, u32[]{:S(2)}) %collective-permute-start.20) | collective-permute-done | bytes 655392 | tf_op jit(solution)/shard_map/ppermute | solution.py:48
  323.2 2.6 collective-permute-done.18
  328.6 4.0 multiply_convert_fusion.1
  332.6 5.1 convert_reduce_fusion.2
  337.7 2.9 convolution_convert_fusion.3
  340.8 3.7 fusion.122
  344.5 5.3 fusion.2
  349.8 5.6 copy.72
  355.9 4.4 convert_add_fusion.3
  361.3 3.0 convolution_convert_fusion.2
  364.7 8.9 %fusion.121 = f32[1280,1280]{1,0:T(8,128)} fusion(bf16[1024,1280]{1,0:T(8,128)(2,1)} %pad_maximum_fusion.2, bf16[1024,1280]{1,0:T(8,128)(2,1)} %copy-done.78), kind=kOutput, calls=%fused_computation.285 | convolution fusion | flops 3355443200 | bytes 11796480 | tf_op jit(solution)/shard_map/sm,sn->mn/dot_general | solution.py:345
  377.6 4.7 convert_add_fusion.2
  383.0 8.2 %collective-permute-done.27 = bf16[256,1280]{1,0:T(8,128)(2,1)S(1)} collective-permute-done((bf16[256,1280]{1,0:T(8,128)(2,1)S(1)}, bf16[256,1280]{1,0:T(8,128)(2,1)S(1)}, u32[]{:S(2)}, u32[]{:S(2)}) %collective-permute-start.27) | collective-permute-done | bytes 655392 | tf_op jit(solution)/shard_map/ppermute | solution.py:67
  391.9 13.4 %collective-permute-done.19 = bf16[256,1280]{1,0:T(8,128)(2,1)S(1)} collective-permute-done((bf16[256,1280]{1,0:T(8,128)(2,1)}, bf16[256,1280]{1,0:T(8,128)(2,1)S(1)}, u32[]{:S(2)}, u32[]{:S(2)}) %collective-permute-start.19) | collective-permute-done | bytes 655392 | tf_op jit(solution)/shard_map/ppermute | solution.py:67
  409.2 10.1 %collective-permute-done.30 = bf16[256,1280]{1,0:T(8,128)(2,1)S(1)} collective-permute-done((bf16[256,1280]{1,0:T(8,128)(2,1)}, bf16[256,1280]{1,0:T(8,128)(2,1)S(1)}, u32[]{:S(2)}, u32[]{:S(2)}) %collective-permute-start.30) | collective-permute-done | bytes 655392 | tf_op jit(solution)/shard_map/ppermute | solution.py:67
  420.0 13.3 %collective-permute-done.26 = bf16[256,1280]{1,0:T(8,128)(2,1)S(1)} collective-permute-done((bf16[256,1280]{1,0:T(8,128)(2,1)S(1)}, bf16[256,1280]{1,0:T(8,128)(2,1)S(1)}, u32[]{:S(2)}, u32[]{:S(2)}) %collective-permute-start.26) | collective-permute-done | bytes 655392 | tf_op jit(solution)/shard_map/ppermute | solution.py:67
  436.9 10.5 %collective-permute-done.28 = bf16[256,1280]{1,0:T(8,128)(2,1)S(1)} collective-permute-done((bf16[256,1280]{1,0:T(8,128)(2,1)S(1)}, bf16[256,1280]{1,0:T(8,128)(2,1)S(1)}, u32[]{:S(2)}, u32[]{:S(2)}) %collective-permute-start.28) | collective-permute-done | bytes 655392 | tf_op jit(solution)/shard_map/ppermute | solution.py:48
  449.5 5.0 fusion.1
  455.1 5.5 collective-permute-done.33
  464.5 2.6 convolution_convert_fusion.9.grad_ref
  467.1 20.6 %attend_back.2 = bf16[1024,1536]{1,0:T(8,128)(2,1)} custom-call(bf16[1024,512]{1,0:T(8,128)(2,1)} %get-tuple-element.56.query_ref, bf16[1024,512]{1,0:T(8,128)(2,1)} %get-tuple-element.57.key_ref, bf16[1024,512]{1,0:T(8,128)(2,1)} %get-tuple-element.58.value_ref, bf16[1024,512]{1,0:T(8,128)(2,1)} %convolution_convert_fusion.9.grad_ref, ...), custom_call_target="tpu_custom_call" | custom-call | flops 5368709120 | bytes 7340032 | tf_op jit(solution)/shard_map/attend_back/pallas_call | solution.py:284
  487.7 5.0 convolution_convert_fusion.1
  492.7 3.1 fusion.120
  497.6 6.7 fusion.119
  511.8 2.5 convolution_convert_fusion.8.grad_ref
  514.3 20.7 %attend_back.3 = bf16[1024,1536]{1,0:T(8,128)(2,1)} custom-call(bf16[1024,512]{1,0:T(8,128)(2,1)} %get-tuple-element.62.query_ref, bf16[1024,512]{1,0:T(8,128)(2,1)} %get-tuple-element.63.key_ref, bf16[1024,512]{1,0:T(8,128)(2,1)} %get-tuple-element.64.value_ref, bf16[1024,512]{1,0:T(8,128)(2,1)} %convolution_convert_fusion.8.grad_ref, ...), custom_call_target="tpu_custom_call" | custom-call | flops 5368709120 | bytes 7340032 | tf_op jit(solution)/shard_map/attend_back/pallas_call | solution.py:284
  535.0 6.0 convolution_convert_fusion
  544.2 2.4 convert_reduce_fusion
  547.2 11.2 %fusion = bf16[1280,1536]{1,0:T(8,128)(2,1)} fusion(f32[1280,1536]{1,0:T(8,128)} %fusion.119, bf16[1024,1280]{1,0:T(8,128)(2,1)} %copy-done.33, bf16[1024,1536]{1,0:T(8,128)(2,1)} %attend_back.3), kind=kOutput, calls=%fused_computation.10 | convolution fusion | flops 4030464000 | bytes 17563648 | tf_op jit(solution)/shard_map/sm,sn->mn/dot_general | solution.py:345
  558.5 6.3 copy.62
  564.8 3.3 slice.369
  568.1 4.5 copy.74
  572.7 5.4 convert_add_fusion
  578.8 2.5 fusion.46
  581.3 2.5 fusion.45
  583.8 11.6 %collective-permute-done.36 = bf16[256,1280]{1,0:T(8,128)(2,1)S(1)} collective-permute-done((bf16[256,1280]{1,0:T(8,128)(2,1)S(1)}, bf16[256,1280]{1,0:T(8,128)(2,1)S(1)}, u32[]{:S(2)}, u32[]{:S(2)}) %collective-permute-start.36) | collective-permute-done | bytes 655392 | tf_op jit(solution)/shard_map/ppermute | solution.py:67
  604.5 3.4 reduce-scatter.15.cloned.1.call-done
  612.0 2.4 collective-permute-done.38
  615.6 2.6 collective-permute-done.39
  625.0 56.8 %reduce-scatter.13.cloned.1.call-done = bf16[160,960]{1,0:T(8,128)(2,1)} async-done(((bf16[1280,960]{1,0:T(8,128)(2,1)}), bf16[160,960]{1,0:T(8,128)(2,1)}) %reduce-scatter.13.cloned.1.call-update) | async-done | bytes 307216
  (445 shorter events, 157.6 us)
Async XLA Ops:
  7.2 26.3 %copy-start = (bf16[2,256,1280]{2,1,0:T(8,128)(2,1)S(1)}, bf16[2,256,1280]{2,1,0:T(8,128)(2,1)}, u32[]{:S(2)}) copy-start(bf16[2,256,1280]{2,1,0:T(8,128)(2,1)} %param.21) | copy-start | bytes 3932164
  7.2 126.9 %all-gather.4.cloned.1.call-start = ((), (), s32[]{:S(2)}) async-start(), calls=%async_computation.4 | async-start | bytes 3317760 | tf_op jit(solution)/shard_map/all_gather | solution.py:407
  7.9 258.0 %all-gather.6.cloned.1.call-start = ((), (), s32[]{:S(2)}) async-start(), calls=%async_computation.5 | async-start | bytes 3686400 | tf_op jit(solution)/shard_map/all_gather | solution.py:409
  13.5 17.3 %collective-permute-start = (bf16[32,520]{1,0:T(8,128)(2,1)S(1)}, bf16[32,520]{1,0:T(8,128)(2,1)S(1)}, u32[]{:S(2)}, u32[]{:S(2)}) collective-permute-start(bf16[32,520]{1,0:T(8,128)(2,1)S(1)} %dynamic_update_slice.11), channel_id=1, source_target_pairs={{0,1},{1,0},{2,3},{3,2},{4,5},{5,4},{6,7},{7,6},{8,9},{9,8},{10,11... | collective-permute-start | bytes 99848 | tf_op jit(solution)/shard_map/ppermute | solution.py:85
  14.1 39.8 %copy-start.10 = (bf16[2,256,1280]{2,1,0:T(8,128)(2,1)S(1)}, bf16[2,256,1280]{2,1,0:T(8,128)(2,1)}, u32[]{:S(2)}) copy-start(bf16[2,256,1280]{2,1,0:T(8,128)(2,1)} %param.38) | copy-start | bytes 3932164
  14.1 261.6 %all-gather.8.cloned.1.call-start = ((), (), s32[]{:S(2)}) async-start(), calls=%async_computation.6 | async-start | bytes 3686400 | tf_op jit(solution)/shard_map/all_gather | solution.py:410
  17.1 36.7 %copy-start.66 = (f32[256]{0:T(256)}, f32[256]{0:T(256)S(1)}, u32[]{:S(2)}) copy-start(f32[256]{0:T(256)S(1)} %broadcast_multiply_fusion.15) | copy-start | bytes 3076
  30.8 23.0 %copy-start.64 = (f32[256]{0:T(256)}, f32[256]{0:T(256)S(1)}, u32[]{:S(2)}) copy-start(f32[256]{0:T(256)S(1)} %broadcast_multiply_fusion.14) | copy-start | bytes 3076
  30.9 4.8 collective-permute-start.1
  35.7 4.1 collective-permute-start.2
  39.8 4.3 collective-permute-start.3
  44.0 8.3 %collective-permute-start.4 = (bf16[32,520]{1,0:T(8,128)(2,1)S(1)}, bf16[32,520]{1,0:T(8,128)(2,1)S(1)}, u32[]{:S(2)}, u32[]{:S(2)}) collective-permute-start(bf16[32,520]{1,0:T(8,128)(2,1)S(1)} %add.397), channel_id=1, source_target_pairs={{0,16},{1,17},{2,18},{3,19},{4,20},{5,21},{6,22},{7,23},{8,24},{9,... | collective-permute-start | bytes 99848 | tf_op jit(solution)/shard_map/ppermute | solution.py:85
  56.6 44.6 %collective-permute-start.5 = (bf16[256,1280]{1,0:T(8,128)(2,1)}, bf16[256,1280]{1,0:T(8,128)(2,1)}, u32[]{:S(2)}, u32[]{:S(2)}) collective-permute-start(bf16[256,1280]{1,0:T(8,128)(2,1)} %get-tuple-element.169), channel_id=1, source_target_pairs={{0,2},{1,3},{2,0},{3,1},{4,6},{5,7},{6,4},{7,5},{8,10},{9,11},{10,... | collective-permute-start | bytes 1966088 | tf_op jit(solution)/shard_map/ppermute | solution.py:48
  62.9 40.8 %copy-start.45 = (f32[1024,40]{1,0:T(8,128)S(1)}, f32[1024,40]{1,0:T(8,128)}, u32[]{:S(2)}) copy-start(f32[1024,40]{1,0:T(8,128)} %copy.58) | copy-start | bytes 491524
  62.9 40.8 %copy-start.46 = (f32[1024,40]{1,0:T(8,128)S(1)}, f32[1024,40]{1,0:T(8,128)}, u32[]{:S(2)}) copy-start(f32[1024,40]{1,0:T(8,128)} %copy.55) | copy-start | bytes 491524
  103.7 27.1 %collective-permute-start.6 = (bf16[512,1280]{1,0:T(8,128)(2,1)}, bf16[512,1280]{1,0:T(8,128)(2,1)}, u32[]{:S(2)}, u32[]{:S(2)}) collective-permute-start(bf16[512,1280]{1,0:T(8,128)(2,1)} %pad_maximum_fusion.6), channel_id=1, source_target_pairs={{0,1},{1,0},{2,3},{3,2},{4,5},{5,4},{6,7},{7,6},{8,9},{9,8},{10,11... | collective-permute-start | bytes 3932168 | tf_op jit(solution)/shard_map/ppermute | solution.py:48
  106.2 22.0 %collective-permute-start.9 = (bf16[256,1280]{1,0:T(8,128)(2,1)S(1)}, bf16[256,1280]{1,0:T(8,128)(2,1)}, u32[]{:S(2)}, u32[]{:S(2)}) collective-permute-start(bf16[256,1280]{1,0:T(8,128)(2,1)S(1)} %get-tuple-element.170), channel_id=1, source_target_pairs={{0,2},{1,3},{2,0},{3,1},{4,6},{5,7},{6,4},{7,5},{8,10},{9,11},{10,... | collective-permute-start | bytes 1966088 | tf_op jit(solution)/shard_map/ppermute | solution.py:48
  110.3 110.6 %copy-start.6 = (bf16[4,128,1280]{2,1,0:T(8,128)(2,1)}, bf16[4,128,1280]{2,1,0:T(8,128)(2,1)S(1)}, u32[]{:S(2)}) copy-start(bf16[4,128,1280]{2,1,0:T(8,128)(2,1)S(1)} %pad.65) | copy-start | bytes 3932164
  130.4 38.5 %collective-permute-start.10 = (bf16[512,1280]{1,0:T(8,128)(2,1)}, bf16[512,1280]{1,0:T(8,128)(2,1)}, u32[]{:S(2)}, u32[]{:S(2)}) collective-permute-start(bf16[512,1280]{1,0:T(8,128)(2,1)} %pad_maximum_fusion.7), channel_id=1, source_target_pairs={{0,1},{1,0},{2,3},{3,2},{4,5},{5,4},{6,7},{7,6},{8,9},{9,8},{10,11... | collective-permute-start | bytes 3932168 | tf_op jit(solution)/shard_map/ppermute | solution.py:48
  168.7 3.1 collective-permute-start.7
  201.8 19.1 %collective-permute-start.11 = (bf16[512,1280]{1,0:T(8,128)(2,1)}, bf16[512,1280]{1,0:T(8,128)(2,1)}, u32[]{:S(2)}, u32[]{:S(2)}) collective-permute-start(bf16[512,1280]{1,0:T(8,128)(2,1)} %convolution_convert_fusion.6), channel_id=1, source_target_pairs={{0,1},{1,0},{2,3},{3,2},{4,5},{5,4},{6,7},{7,6},{8,9},{9,8},{10,11... | collective-permute-start | bytes 3932168 | tf_op jit(solution)/shard_map/ppermute | solution.py:61
  201.9 17.7 %collective-permute-start.15 = (bf16[256,1280]{1,0:T(8,128)(2,1)S(1)}, bf16[256,1280]{1,0:T(8,128)(2,1)}, u32[]{:S(2)}, u32[]{:S(2)}) collective-permute-start(bf16[256,1280]{1,0:T(8,128)(2,1)S(1)} %copy-done.17), channel_id=1, source_target_pairs={{0,2},{1,3},{2,0},{3,1},{4,6},{5,7},{6,4},{7,5},{8,10},{9,11},{10,... | collective-permute-start | bytes 1966088 | tf_op jit(solution)/shard_map/ppermute | solution.py:48
  203.8 396.4 %reduce-scatter.17.cloned.1.call-start = ((), (), s32[]{:S(2)}) async-start(), calls=%async_computation.10 | async-start | bytes 3686400
  203.9 29.8 %collective-permute-start.8 = (bf16[256,1280]{1,0:T(8,128)(2,1)}, bf16[256,1280]{1,0:T(8,128)(2,1)}, u32[]{:S(2)}, u32[]{:S(2)}) collective-permute-start(bf16[256,1280]{1,0:T(8,128)(2,1)} %slice.560), channel_id=1, source_target_pairs={{0,2},{1,3},{2,0},{3,1},{4,6},{5,7},{6,4},{7,5},{8,10},{9,11},{10,... | collective-permute-start | bytes 1966088 | tf_op jit(solution)/shard_map/ppermute | solution.py:67
  220.8 18.1 %collective-permute-start.16 = (bf16[512,1280]{1,0:T(8,128)(2,1)S(1)}, bf16[512,1280]{1,0:T(8,128)(2,1)S(1)}, u32[]{:S(2)}, u32[]{:S(2)}) collective-permute-start(bf16[512,1280]{1,0:T(8,128)(2,1)S(1)} %pad_maximum_fusion.9), channel_id=1, source_target_pairs={{0,1},{1,0},{2,3},{3,2},{4,5},{5,4},{6,7},{7,6},{8,9},{9,8},{10,11... | collective-permute-start | bytes 3932168 | tf_op jit(solution)/shard_map/ppermute | solution.py:48
  223.3 24.3 %collective-permute-start.14 = (bf16[256,1280]{1,0:T(8,128)(2,1)S(1)}, bf16[256,1280]{1,0:T(8,128)(2,1)S(1)}, u32[]{:S(2)}, u32[]{:S(2)}) collective-permute-start(bf16[256,1280]{1,0:T(8,128)(2,1)S(1)} %slice.559), channel_id=1, source_target_pairs={{0,2},{1,3},{2,0},{3,1},{4,6},{5,7},{6,4},{7,5},{8,10},{9,11},{10,... | collective-permute-start | bytes 1966088 | tf_op jit(solution)/shard_map/ppermute | solution.py:67
  235.7 25.3 %collective-permute-start.12 = (bf16[256,1280]{1,0:T(8,128)(2,1)S(1)}, bf16[256,1280]{1,0:T(8,128)(2,1)S(1)}, u32[]{:S(2)}, u32[]{:S(2)}) collective-permute-start(bf16[256,1280]{1,0:T(8,128)(2,1)S(1)} %add_convert_fusion.1), channel_id=1, source_target_pairs={{0,2},{1,3},{2,0},{3,1},{4,6},{5,7},{6,4},{7,5},{8,10},{9,11},{10,... | collective-permute-start | bytes 1966088 | tf_op jit(solution)/shard_map/ppermute | solution.py:48
  261.2 3.1 collective-permute-start.13
  284.7 33.4 %copy-start.78 = (bf16[1024,1280]{1,0:T(8,128)(2,1)}, bf16[1024,1280]{1,0:T(8,128)(2,1)S(1)}, u32[]{:S(2)}) copy-start(bf16[1024,1280]{1,0:T(8,128)(2,1)S(1)} %get-tuple-element.212) | copy-start | bytes 7864324
  286.6 31.5 %collective-permute-start.17 = (bf16[512,1280]{1,0:T(8,128)(2,1)S(1)}, bf16[512,1280]{1,0:T(8,128)(2,1)S(1)}, u32[]{:S(2)}, u32[]{:S(2)}) collective-permute-start(bf16[512,1280]{1,0:T(8,128)(2,1)S(1)} %convolution_convert_fusion.5), channel_id=1, source_target_pairs={{0,1},{1,0},{2,3},{3,2},{4,5},{5,4},{6,7},{7,6},{8,9},{9,8},{10,11... | collective-permute-start | bytes 3932168 | tf_op jit(solution)/shard_map/ppermute | solution.py:61
  286.8 17.6 %collective-permute-start.22 = (bf16[256,1280]{1,0:T(8,128)(2,1)S(1)}, bf16[256,1280]{1,0:T(8,128)(2,1)S(1)}, u32[]{:S(2)}, u32[]{:S(2)}) collective-permute-start(bf16[256,1280]{1,0:T(8,128)(2,1)S(1)} %copy-done.16), channel_id=1, source_target_pairs={{0,2},{1,3},{2,0},{3,1},{4,6},{5,7},{6,4},{7,5},{8,10},{9,11},{10,... | collective-permute-start | bytes 1966088 | tf_op jit(solution)/shard_map/ppermute | solution.py:48
  288.6 29.3 %collective-permute-start.20 = (bf16[256,1280]{1,0:T(8,128)(2,1)S(1)}, bf16[256,1280]{1,0:T(8,128)(2,1)S(1)}, u32[]{:S(2)}, u32[]{:S(2)}) collective-permute-start(bf16[256,1280]{1,0:T(8,128)(2,1)S(1)} %add_convert_fusion), channel_id=1, source_target_pairs={{0,2},{1,3},{2,0},{3,1},{4,6},{5,7},{6,4},{7,5},{8,10},{9,11},{10,... | collective-permute-start | bytes 1966088 | tf_op jit(solution)/shard_map/ppermute | solution.py:48
  304.5 18.3 %collective-permute-start.23 = (bf16[512,1280]{1,0:T(8,128)(2,1)S(1)}, bf16[512,1280]{1,0:T(8,128)(2,1)S(1)}, u32[]{:S(2)}, u32[]{:S(2)}) collective-permute-start(bf16[512,1280]{1,0:T(8,128)(2,1)S(1)} %pad_maximum_fusion.11), channel_id=1, source_target_pairs={{0,1},{1,0},{2,3},{3,2},{4,5},{5,4},{6,7},{7,6},{8,9},{9,8},{10,11... | collective-permute-start | bytes 3932168 | tf_op jit(solution)/shard_map/ppermute | solution.py:48
  318.0 5.0 collective-permute-start.21
  322.6 3.1 collective-permute-start.18
  340.6 15.3 %collective-permute-start.24 = (bf16[512,1280]{1,0:T(8,128)(2,1)}, bf16[512,1280]{1,0:T(8,128)(2,1)S(1)}, u32[]{:S(2)}, u32[]{:S(2)}) collective-permute-start(bf16[512,1280]{1,0:T(8,128)(2,1)} %convolution_convert_fusion.3), channel_id=1, source_target_pairs={{0,1},{1,0},{2,3},{3,2},{4,5},{5,4},{6,7},{7,6},{8,9},{9,8},{10,11... | collective-permute-start | bytes 3932168 | tf_op jit(solution)/shard_map/ppermute | solution.py:61
  355.4 247.1 %reduce-scatter.11.cloned.1.call-start = ((), (), s32[]{:S(2)}) async-start(), calls=%async_computation.7 | async-start | bytes 3686400 | tf_op jit(solution)/shard_map/reduce_scatter | solution.py:531
  364.2 13.4 %collective-permute-start.25 = (bf16[512,1280]{1,0:T(8,128)(2,1)}, bf16[512,1280]{1,0:T(8,128)(2,1)}, u32[]{:S(2)}, u32[]{:S(2)}) collective-permute-start(bf16[512,1280]{1,0:T(8,128)(2,1)} %convolution_convert_fusion.2), channel_id=1, source_target_pairs={{0,1},{1,0},{2,3},{3,2},{4,5},{5,4},{6,7},{7,6},{8,9},{9,8},{10,11... | collective-permute-start | bytes 3932168 | tf_op jit(solution)/shard_map/ppermute | solution.py:61
  373.6 17.6 %collective-permute-start.27 = (bf16[256,1280]{1,0:T(8,128)(2,1)S(1)}, bf16[256,1280]{1,0:T(8,128)(2,1)S(1)}, u32[]{:S(2)}, u32[]{:S(2)}) collective-permute-start(bf16[256,1280]{1,0:T(8,128)(2,1)S(1)} %slice.558), channel_id=1, source_target_pairs={{0,2},{1,3},{2,0},{3,1},{4,6},{5,7},{6,4},{7,5},{8,10},{9,11},{10,... | collective-permute-start | bytes 1966088 | tf_op jit(solution)/shard_map/ppermute | solution.py:67
  375.4 29.9 %collective-permute-start.19 = (bf16[256,1280]{1,0:T(8,128)(2,1)}, bf16[256,1280]{1,0:T(8,128)(2,1)S(1)}, u32[]{:S(2)}, u32[]{:S(2)}) collective-permute-start(bf16[256,1280]{1,0:T(8,128)(2,1)} %slice.557), channel_id=1, source_target_pairs={{0,2},{1,3},{2,0},{3,1},{4,6},{5,7},{6,4},{7,5},{8,10},{9,11},{10,... | collective-permute-start | bytes 1966088 | tf_op jit(solution)/shard_map/ppermute | solution.py:67
  375.8 43.5 %collective-permute-start.30 = (bf16[256,1280]{1,0:T(8,128)(2,1)}, bf16[256,1280]{1,0:T(8,128)(2,1)S(1)}, u32[]{:S(2)}, u32[]{:S(2)}) collective-permute-start(bf16[256,1280]{1,0:T(8,128)(2,1)} %slice.556), channel_id=1, source_target_pairs={{0,2},{1,3},{2,0},{3,1},{4,6},{5,7},{6,4},{7,5},{8,10},{9,11},{10,... | collective-permute-start | bytes 1966088 | tf_op jit(solution)/shard_map/ppermute | solution.py:67
  382.4 22.9 %copy-start.11 = (bf16[2,256,1280]{2,1,0:T(8,128)(2,1)S(1)}, bf16[2,256,1280]{2,1,0:T(8,128)(2,1)}, u32[]{:S(2)}) copy-start(bf16[2,256,1280]{2,1,0:T(8,128)(2,1)} %param.38) | copy-start | bytes 3932164
  382.4 22.9 %copy-start.48 = (f32[512,1280]{1,0:T(8,128)S(1)}, f32[512,1280]{1,0:T(8,128)}, u32[]{:S(2)}) copy-start(f32[512,1280]{1,0:T(8,128)} %copy-done.47) | copy-start | bytes 7864324
  382.4 22.9 %copy-start.68 = (f32[1,256]{1,0:T(1,128)S(1)}, f32[1,256]{1,0:T(1,128)}, u32[]{:S(2)}) copy-start(f32[1,256]{1,0:T(1,128)} %get-tuple-element.187) | copy-start | bytes 3076
  382.4 22.9 %copy-start.71 = (f32[1,256]{1,0:T(1,128)S(1)}, f32[1,256]{1,0:T(1,128)}, u32[]{:S(2)}) copy-start(f32[1,256]{1,0:T(1,128)} %get-tuple-element.188) | copy-start | bytes 3076
  382.5 50.9 %collective-permute-start.26 = (bf16[256,1280]{1,0:T(8,128)(2,1)S(1)}, bf16[256,1280]{1,0:T(8,128)(2,1)S(1)}, u32[]{:S(2)}, u32[]{:S(2)}) collective-permute-start(bf16[256,1280]{1,0:T(8,128)(2,1)S(1)} %slice.555), channel_id=1, source_target_pairs={{0,2},{1,3},{2,0},{3,1},{4,6},{5,7},{6,4},{7,5},{8,10},{9,11},{10,... | collective-permute-start | bytes 1966088 | tf_op jit(solution)/shard_map/ppermute | solution.py:67
  407.4 40.0 %collective-permute-start.28 = (bf16[256,1280]{1,0:T(8,128)(2,1)S(1)}, bf16[256,1280]{1,0:T(8,128)(2,1)S(1)}, u32[]{:S(2)}, u32[]{:S(2)}) collective-permute-start(bf16[256,1280]{1,0:T(8,128)(2,1)S(1)} %convert_element_type.417), channel_id=1, source_target_pairs={{0,2},{1,3},{2,0},{3,1},{4,6},{5,7},{6,4},{7,5},{8,10},{9,11},{10,... | collective-permute-start | bytes 1966088 | tf_op jit(solution)/shard_map/ppermute | solution.py:48
  419.3 30.1 %slice-start = ((s8[6553600]{0:T(1024)(128)(4,1)}), s8[4194304]{0:T(1024)(128)(4,1)S(1)}, s32[]{:S(2)}) async-start(s8[6553600]{0:T(1024)(128)(4,1)} %bitcast.244), calls=%async_computation.11 | async-start | bytes 8388608
  420.0 29.4 %slice-start.1 = ((s8[6553600]{0:T(1024)(128)(4,1)}), s8[2359296]{0:T(1024)(128)(4,1)S(1)}, s32[]{:S(2)}) async-start(s8[6553600]{0:T(1024)(128)(4,1)} %bitcast.244), calls=%async_computation.12 | async-start | bytes 4718592
  435.1 25.5 %copy-start.14 = (bf16[256,1280]{1,0:T(8,128)(2,1)}, bf16[256,1280]{1,0:T(8,128)(2,1)S(1)}, u32[]{:S(2)}) copy-start(bf16[256,1280]{1,0:T(8,128)(2,1)S(1)} %convert_element_type.419) | copy-start | bytes 1966084
  435.1 25.5 %collective-permute-start.33 = (bf16[256,1280]{1,0:T(8,128)(2,1)S(1)}, bf16[256,1280]{1,0:T(8,128)(2,1)S(1)}, u32[]{:S(2)}, u32[]{:S(2)}) collective-permute-start(bf16[256,1280]{1,0:T(8,128)(2,1)S(1)} %convert_element_type.419), channel_id=1, source_target_pairs={{0,2},{1,3},{2,0},{3,1},{4,6},{5,7},{6,4},{7,5},{8,10},{9,11},{10,... | collective-permute-start | bytes 1966088 | tf_op jit(solution)/shard_map/ppermute | solution.py:48
  449.4 13.2 %collective-permute-start.29 = (bf16[512,1280]{1,0:T(8,128)(2,1)}, bf16[512,1280]{1,0:T(8,128)(2,1)}, u32[]{:S(2)}, u32[]{:S(2)}) collective-permute-start(bf16[512,1280]{1,0:T(8,128)(2,1)} %pad_maximum_fusion.13), channel_id=1, source_target_pairs={{0,1},{1,0},{2,3},{3,2},{4,5},{5,4},{6,7},{7,6},{8,9},{9,8},{10,11... | collective-permute-start | bytes 3932168 | tf_op jit(solution)/shard_map/ppermute | solution.py:48
  454.5 153.4 %reduce-scatter.15.cloned.1.call-start = ((), (), s32[]{:S(2)}) async-start(), calls=%async_computation.9 | async-start | bytes 1105920
  462.6 41.7 %collective-permute-start.34 = (bf16[512,1280]{1,0:T(8,128)(2,1)}, bf16[512,1280]{1,0:T(8,128)(2,1)}, u32[]{:S(2)}, u32[]{:S(2)}) collective-permute-start(bf16[512,1280]{1,0:T(8,128)(2,1)} %pad_maximum_fusion.14), channel_id=1, source_target_pairs={{0,1},{1,0},{2,3},{3,2},{4,5},{5,4},{6,7},{7,6},{8,9},{9,8},{10,11... | collective-permute-start | bytes 3932168 | tf_op jit(solution)/shard_map/ppermute | solution.py:48
  495.9 10.1 %collective-permute-start.31 = (bf16[512,1280]{1,0:T(8,128)(2,1)S(1)}, bf16[512,1280]{1,0:T(8,128)(2,1)S(1)}, u32[]{:S(2)}, u32[]{:S(2)}) collective-permute-start(bf16[512,1280]{1,0:T(8,128)(2,1)S(1)} %convolution_convert_fusion.1), channel_id=1, source_target_pairs={{0,1},{1,0},{2,3},{3,2},{4,5},{5,4},{6,7},{7,6},{8,9},{9,8},{10,11... | collective-permute-start | bytes 3932168 | tf_op jit(solution)/shard_map/ppermute | solution.py:61
  510.0 68.8 %collective-permute-start.32 = (bf16[256,1280]{1,0:T(8,128)(2,1)}, bf16[256,1280]{1,0:T(8,128)(2,1)}, u32[]{:S(2)}, u32[]{:S(2)}) collective-permute-start(bf16[256,1280]{1,0:T(8,128)(2,1)} %slice.554), channel_id=1, source_target_pairs={{0,2},{1,3},{2,0},{3,1},{4,6},{5,7},{6,4},{7,5},{8,10},{9,11},{10,... | collective-permute-start | bytes 1966088 | tf_op jit(solution)/shard_map/ppermute | solution.py:67
  541.0 31.8 %collective-permute-start.35 = (bf16[512,1280]{1,0:T(8,128)(2,1)}, bf16[512,1280]{1,0:T(8,128)(2,1)}, u32[]{:S(2)}, u32[]{:S(2)}) collective-permute-start(bf16[512,1280]{1,0:T(8,128)(2,1)} %convolution_convert_fusion), channel_id=1, source_target_pairs={{0,1},{1,0},{2,3},{3,2},{4,5},{5,4},{6,7},{7,6},{8,9},{9,8},{10,11... | collective-permute-start | bytes 3932168 | tf_op jit(solution)/shard_map/ppermute | solution.py:61
  544.1 137.6 %reduce-scatter.13.cloned.1.call-start = ((), (), s32[]{:S(2)}) async-start(), calls=%async_computation.8 | async-start | bytes 2949120
  578.2 17.3 %collective-permute-start.36 = (bf16[256,1280]{1,0:T(8,128)(2,1)S(1)}, bf16[256,1280]{1,0:T(8,128)(2,1)S(1)}, u32[]{:S(2)}, u32[]{:S(2)}) collective-permute-start(bf16[256,1280]{1,0:T(8,128)(2,1)S(1)} %slice.553), channel_id=1, source_target_pairs={{0,2},{1,3},{2,0},{3,1},{4,6},{5,7},{6,4},{7,5},{8,10},{9,11},{10,... | collective-permute-start | bytes 1966088 | tf_op jit(solution)/shard_map/ppermute | solution.py:67
  597.9 11.8 %collective-permute-start.37 = (f32[16,520]{1,0:T(8,128)}, f32[16,520]{1,0:T(8,128)}, u32[]{:S(2)}, u32[]{:S(2)}) collective-permute-start(f32[16,520]{1,0:T(8,128)} %slice.358), channel_id=1, source_target_pairs={{0,16},{1,17},{2,18},{3,19},{4,20},{5,21},{6,22},{7,23},{8,24},{9,... | collective-permute-start | bytes 99848 | tf_op jit(solution)/shard_map/ppermute | solution.py:104
  610.6 3.8 collective-permute-start.38
  614.4 3.7 collective-permute-start.39
  618.2 3.7 collective-permute-start.40
  621.9 1.3 collective-permute-start.41
  (69 other events, 431.4 us)
Sparse Core Ops, SparseCore 0:
  10.2 63.6 all-gather.3
  76.0 62.0 all-gather.5
  204.0 60.4 all-gather.7
  355.5 76.2 reduce-scatter.16
  454.6 76.8 reduce-scatter.10
  544.2 63.6 reduce-scatter.14
  611.4 70.2 reduce-scatter.12
